TPU v7x, 16 devices: a 4x2x1 block of a 4x4x8 slice. The times are simulated.
16 devices in a mesh: dp: 2 (over y, z), sp: 8 (over x, core).
Axes of the slice: x: 4, y: 2, z: 1, core: 2. Of those that a mesh axis runs over, the one named last changes fastest.
The devices are a block of a 4x4x8 slice.
Arguments:
- resid: float32 [32, 512, 2560], P('dp', 'sp'), parts along dimension 0
- pre_norm: float32 [2, 2560], replicated
- w_in: bfloat16 [2, 2560, 10576], replicated
- conv_w: float32 [2, 5376, 4], replicated
- conv_b: float32 [2, 5376], replicated
- dt_bias: float32 [2, 80], replicated
- a_log: float32 [2, 80], replicated
- d_skip: float32 [2, 80], replicated
- gate_norm: float32 [2, 1, 5120], replicated
- w_out: bfloat16 [2, 5120, 2560], replicated
Outputs:
- output 1: float32 [32, 512, 2560], P('dp', 'sp'), parts along dimension 0
- output 2: float32 [32, 2, 80, 64, 128], P('dp', None, 'sp'), parts along dimension 0
- output 3: bfloat16 [32, 2, 5376, 3], P('dp'), parts along dimension 0
There are 2 independent parts. A program takes and returns all parts, laid end to end along the dimension named above; an argument that names none is the same for every part.
All inputs are finite; a program needn't handle non-finite values.
Results may differ from a plain program's by a relative error of at most 0.017196.
Values are sent between devices in bfloat16 or wider.
A program may use at most 768 MiB of HBM per device.

v0:
```python
import jax
import jax.numpy as jnp
from jax import lax
from jax.sharding import PartitionSpec as P

CONV_WIDTH = 4
CHUNK = 256
EPSILON = 1e-5


def rms_norm(values, gain_vec):
    mean_sq = jnp.mean(values * values, axis=-1, keepdims=True)
    return values * lax.rsqrt(mean_sq + EPSILON) * gain_vec


def ssd_scan(x_in, dt_in, bc_in, a_neg, d_vec):
    batch, seq_len, groups, per_group, head_dim = x_in.shape
    d_state = bc_in.shape[-1]
    causal = jnp.arange(CHUNK)[:, None] >= jnp.arange(CHUNK)[None, :]

    def body(chunk_index, carry):
        state, y_buffer = carry
        start = chunk_index * CHUNK
        x_chunk = lax.dynamic_slice_in_dim(x_in, start, CHUNK, axis=1)
        dt_chunk = lax.dynamic_slice_in_dim(dt_in, start, CHUNK, axis=1).astype(jnp.float32)
        bc_chunk = lax.dynamic_slice_in_dim(bc_in, start, CHUNK, axis=1)
        b_chunk = bc_chunk[:, :, 0]
        c_chunk = bc_chunk[:, :, 1]
        cum_log = jnp.cumsum(dt_chunk * a_neg, axis=1)
        cum_heads = jnp.transpose(cum_log, (0, 2, 3, 1))
        log_diff = cum_heads[..., :, None] - cum_heads[..., None, :]
        decay_mat = jnp.exp(jnp.where(causal, log_diff, -jnp.inf))
        scores = jnp.einsum('btgn,bsgn->bgts', c_chunk, b_chunk, preferred_element_type=jnp.float32)
        mix_mat = decay_mat * scores[:, :, None]
        x_float = x_chunk.astype(jnp.float32)
        x_scaled = x_float * dt_chunk[..., None]
        y_intra = jnp.einsum('bghts,bsghp->btghp', mix_mat, x_scaled, preferred_element_type=jnp.float32)
        y_inter = jnp.einsum('btgn,bghpn->btghp', c_chunk.astype(jnp.float32), state, preferred_element_type=jnp.float32)
        to_end = jnp.exp(cum_log[:, -1:] - cum_log)
        state = state * jnp.exp(cum_log[:, -1])[..., None, None] + jnp.einsum('bsghp,bsgn->bghpn', x_scaled * to_end[..., None], b_chunk.astype(jnp.float32), preferred_element_type=jnp.float32)
        y_chunk = y_intra + y_inter * jnp.exp(cum_log)[..., None] + d_vec[:, :, None] * x_float
        y_buffer = lax.dynamic_update_slice_in_dim(y_buffer, y_chunk.astype(jnp.bfloat16), start, axis=1)
        return state, y_buffer

    state_zero = jnp.zeros((batch, groups, per_group, head_dim, d_state), jnp.float32)
    y_zero = jnp.zeros(x_in.shape, jnp.bfloat16)
    return lax.fori_loop(0, seq_len // CHUNK, body, (state_zero, y_zero))


def solution(mesh):
    seg_count = mesh.shape['sp']

    def layer(resid, pre_w, w_in_l, conv_w_l, conv_b_l, dt_b, a_log_l, d_l, gate_w, w_out_l):
        batch, seg_len, d_model = resid.shape
        n_groups, group_width = gate_w.shape
        d_inner = n_groups * group_width
        n_heads = dt_b.shape[0]
        conv_dim = conv_b_l.shape[0]
        d_state = (conv_dim - d_inner) // (2 * n_groups)
        head_dim = d_inner // n_heads
        seq_len = seg_len * seg_count
        local_heads = n_heads // seg_count
        local_groups = max(n_groups // seg_count, 1)
        local_per_group = local_heads // local_groups
        repeat_count = max(seg_count // n_groups, 1)
        seg_index = lax.axis_index('sp')

        normed = rms_norm(resid, pre_w).astype(jnp.bfloat16)
        projected = jnp.einsum('bld,de->ble', normed, w_in_l, preferred_element_type=jnp.float32).astype(jnp.bfloat16)
        gate_z = projected[..., :d_inner]
        xbc = projected[..., d_inner:d_inner + conv_dim]
        dt_raw = projected[..., d_inner + conv_dim:]
        halo_rows = lax.ppermute(xbc[:, seg_len - (CONV_WIDTH - 1):], 'sp', [(source, source + 1) for source in range(seg_count - 1)])
        padded = jnp.concatenate([halo_rows, xbc], axis=1)
        conv_out = conv_b_l + sum(padded[:, tap_index:tap_index + seg_len].astype(jnp.float32) * conv_w_l[:, tap_index] for tap_index in range(CONV_WIDTH))
        activated = jax.nn.silu(conv_out).astype(jnp.bfloat16)
        delta = jax.nn.softplus(dt_raw.astype(jnp.float32) + dt_b).astype(jnp.bfloat16)
        bc_tokens = jnp.repeat(activated[..., d_inner:].reshape(batch, seg_len, 2, n_groups, d_state), repeat_count, axis=3)

        x_local = lax.all_to_all(activated[..., :d_inner], 'sp', 2, 1, tiled=True)
        dt_local = lax.all_to_all(delta, 'sp', 2, 1, tiled=True)
        bc_local = lax.all_to_all(bc_tokens, 'sp', 3, 1, tiled=True)

        head_start = seg_index * local_heads
        a_neg = -jnp.exp(lax.dynamic_slice_in_dim(a_log_l, head_start, local_heads)).reshape(local_groups, local_per_group)
        d_local = lax.dynamic_slice_in_dim(d_l, head_start, local_heads).reshape(local_groups, local_per_group)
        final, y_local = ssd_scan(x_local.reshape(batch, seq_len, local_groups, local_per_group, head_dim), dt_local.reshape(batch, seq_len, local_groups, local_per_group), bc_local, a_neg, d_local)

        y_tokens = lax.all_to_all(y_local.reshape(batch, seq_len, local_heads * head_dim), 'sp', 1, 2, tiled=True)

        gated = y_tokens.reshape(batch, seg_len, n_groups, group_width).astype(jnp.float32) * jax.nn.silu(gate_z.reshape(batch, seg_len, n_groups, group_width).astype(jnp.float32))
        normed_y = (gated * lax.rsqrt(jnp.mean(gated * gated, axis=-1, keepdims=True) + EPSILON) * gate_w).astype(jnp.bfloat16)
        out_proj = jnp.einsum('blgc,gcd->bld', normed_y, w_out_l.reshape(n_groups, group_width, d_model), preferred_element_type=jnp.float32)
        tail_rows = jnp.where(seg_index == seg_count - 1, xbc[:, seg_len - (CONV_WIDTH - 1):], jnp.zeros((), jnp.bfloat16))
        conv_state = lax.psum(tail_rows, 'sp')
        return resid + out_proj, final.reshape(batch, local_heads, head_dim, d_state), jnp.swapaxes(conv_state, 1, 2)

    def forward(resid, pre_norm, w_in, conv_w, conv_b, dt_bias, a_log, d_skip, gate_norm, w_out):
        finals = []
        tails = []
        for layer_index in range(w_in.shape[0]):
            resid, final, tail_rows = layer(resid, pre_norm[layer_index], w_in[layer_index], conv_w[layer_index], conv_b[layer_index], dt_bias[layer_index], a_log[layer_index], d_skip[layer_index], gate_norm[layer_index], w_out[layer_index])
            finals.append(final)
            tails.append(tail_rows)
        return resid, jnp.stack(finals, axis=1), jnp.stack(tails, axis=1)

    return jax.shard_map(forward, mesh=mesh, in_specs=(P('dp', 'sp', None), P(), P(), P(), P(), P(), P(), P(), P(), P()), out_specs=(P('dp', 'sp', None), P('dp', None, 'sp', None, None), P('dp', None, None, None)), check_vma=False)
```

profile of v0, /device:TPU:112, one launch (start us, length us, event | category | flops | bytes accessed | tf_op | source)
XLA Modules:
  0.0 1418.5 jit_solution(15654714945109230238)
XLA Ops:
  13.4 66.4 %fusion.126 = bf16[16,64,10576]{2,1,0:T(8,128)(2,1)} fusion(bf16[2,2560,10576]{1,2,0:T(8,128)(2,1)} %param.16, f32[16,64,2560]{2,1,0:T(8,128)} %param.14, f32[2560]{0:T(1024)S(1)} %get-tuple-element.452, f32[16,64]{1,0:T(8,128)S(1)} %add_rsqrt_fusion.3), kind=kOutput, calls=%fused_computation.150 | convolution fusion | flops 55467393024 | bytes 86308864 | tf_op jit(solution)/shard_map/bld,de->ble/dot_general | solution.py:69
  87.5 6.5 all-to-all-start
  98.8 16.6 %multiply_convert_fusion.1 = bf16[16,64,5376]{2,1,0:T(8,128)(2,1)S(1)} fusion(bf16[16,64,5376]{2,1,0:T(8,128)(2,1)S(1)} %slice-done, bf16[16,3,5376]{2,1,0:T(4,128)(2,1)S(1)} %copy.245, f32[5376]{0:T(1024)S(1)} %get-tuple-element.446, f32[5376]{0:T(1024)S(1)} %get-tuple-element.447, f32[5376]{0:T(1024)S(1)} %get-tuple-element.448, ...), kind=kLoop, calls=%fused_computation.133 | loop fusion | flops 143130624 | bytes 22643712 | tf_op jit(solution)/shard_map/convert_element_type | solution.py:76
  127.9 9.0 slice.271
  137.0 25.0 %copy.246 = bf16[16,64,5120]{1,0,2:T(8,128)(2,1)} copy(bf16[16,64,5120]{2,1,0:T(8,128)(2,1)} %slice.271) | data formatting | bytes 20971520 | tf_op jit(solution)/shard_map/slice | solution.py:80
  162.0 19.7 %reshape.594 = bf16[8,2,327680]{2,1,0:T(2,128)(2,1)} reshape(bf16[5120,16,64]{2,1,0:T(8,128)(2,1)} %bitcast.398) | data formatting | bytes 20971520
  181.8 5.5 all-to-all-start.1
  189.3 5.6 copy.249
  194.8 109.3 %all-to-all-done.1 = bf16[8,2,327680]{2,1,0:T(2,128)(2,1)} async-done(((bf16[8,2,327680]{2,1,0:T(2,128)(2,1)}), bf16[8,2,327680]{2,1,0:T(2,128)(2,1)}, u32[]{:S(2)}, u32[]{:S(2)}) %all-to-all-start.1) | async-done | bytes 10485792 | tf_op jit(solution)/shard_map/all_to_all | solution.py:80
  304.1 19.5 %reshape.595 = bf16[5120,16,64]{2,1,0:T(8,128)(2,1)} reshape(bf16[8,2,327680]{2,1,0:T(2,128)(2,1)} %all-to-all-done.1) | data formatting | bytes 20971520
  323.7 22.7 %copy.298 = bf16[16,64,8,640]{1,2,3,0:T(8,128)(2,1)} copy(bf16[16,64,8,640]{1,0,3,2:T(8,128)(2,1)} %bitcast.394) | data formatting | bytes 20971520 | tf_op jit(solution)/shard_map/all_to_all | solution.py:80
  346.4 27.8 %reshape.533 = bf16[16,512,1,10,64]{1,4,3,0,2:T(8,128)(2,1)} reshape(bf16[16,8,64,640]{2,1,3,0:T(8,128)(2,1)} %bitcast.395) | data formatting | bytes 20971520 | tf_op jit(solution)/shard_map/reshape | solution.py:87
  374.2 5.4 broadcast.177.clone
  379.6 94.2 %while.32 = (s32[]{:T(128)}, f32[16,1,10,64,128]{4,3,2,0,1:T(8,128)}, bf16[16,512,1,10,64]{1,4,3,0,2:T(8,128)(2,1)}, bf16[16,512,1,10]{1,0,3,2:T(8,128)(2,1)S(1)...) while((s32[]{:T(128)}, ...), condition=%wide.region_4.5_spmd.clone, body=%wide.region_1.4_spmd.clone.sunk | while | flops 3023839744 | bytes 77752232 | solution.py:47
  380.1 9.1 reduce-window.36
  392.9 14.0 fusion.210
  407.3 10.3 fusion.211
  418.2 7.0 bitcast_add_fusion.4
  425.5 9.1 reduce-window.36
  438.4 14.0 fusion.210
  452.7 11.8 fusion.211
  465.2 8.6 bitcast_add_fusion.4
  473.8 17.5 %copy.251 = bf16[16,512,640]{2,0,1:T(8,128)(2,1)} copy(bf16[16,512,640]{1,2,0:T(8,128)(2,1)} %bitcast.401) | data formatting | bytes 20971520 | tf_op jit(solution)/shard_map/reshape | solution.py:89
  491.3 5.9 all-to-all-start.3
  497.8 116.3 %all-to-all-done.3 = bf16[16,512,640]{2,0,1:T(8,128)(2,1)} async-done(((bf16[16,512,640]{2,0,1:T(8,128)(2,1)}), bf16[16,512,640]{2,0,1:T(8,128)(2,1)}, u32[]{:S(2)}, u32[]{:S(2)}) %all-to-all-start.3) | async-done | bytes 10485792 | tf_op jit(solution)/shard_map/all_to_all | solution.py:89
  614.1 10.5 copy.252
  624.5 13.9 convert_bitcast_fusion.3
  638.5 8.7 copy.283
  647.2 9.6 multiply_reduce_fusion.1
  656.8 12.1 multiply_convert_fusion.9.clone.5
  668.9 35.2 %multiply_reduce_fusion.2 = (f32[16,64]{1,0:T(8,128)S(1)}, f32[16,64,2560]{2,1,0:T(8,128)}) fusion(f32[16,64,2560]{2,1,0:T(8,128)S(1)} %bitcast.409, bf16[2,5120,2560]{2,1,0:T(8,128)(2,1)} %param.23, bf16[16,64,5120]{2,1,0:T(8,128)(2,1)} %multiply_convert_fusion.9.clone.5), kind=kOutput, calls=%fused_computation.170 | convolution fusion | flops 26851409920 | bytes 57675776 | tf_op jit(solution)/shard_map/blgc,gcd->bld/dot_general | solution.py:93
  704.1 66.4 %fusion.129 = bf16[16,64,10576]{2,1,0:T(8,128)(2,1)} fusion(bf16[2,2560,10576]{1,2,0:T(8,128)(2,1)} %param.16, f32[16,64,2560]{2,1,0:T(8,128)} %get-tuple-element.506, f32[2560]{0:T(1024)S(1)} %copy-done.8, f32[16,64]{1,0:T(8,128)S(1)} %add_rsqrt_fusion.1), kind=kOutput, calls=%fused_computation.151 | convolution fusion | flops 55467393024 | bytes 86308864 | tf_op jit(solution)/shard_map/bld,de->ble/dot_general | solution.py:69
  775.1 9.7 slice.276
  791.8 24.7 %multiply_convert_fusion = bf16[16,64,5376]{2,1,0:T(8,128)(2,1)S(1)} fusion(bf16[16,64,5376]{2,1,0:T(8,128)(2,1)} %slice.276, bf16[16,3,5376]{2,1,0:T(4,128)(2,1)S(1)} %copy.257, f32[5376]{0:T(1024)S(1)} %get-tuple-element.442, f32[5376]{0:T(1024)S(1)} %get-tuple-element.443, f32[5376]{0:T(1024)S(1)} %get-tuple-element.444, ...), kind=kLoop, calls=%fused_computation.132 | loop fusion | flops 143130624 | bytes 22643712 | tf_op jit(solution)/shard_map/convert_element_type | solution.py:76
  829.0 9.0 slice.285
  838.1 25.0 %copy.258 = bf16[16,64,5120]{1,0,2:T(8,128)(2,1)} copy(bf16[16,64,5120]{2,1,0:T(8,128)(2,1)} %slice.285) | data formatting | bytes 20971520 | tf_op jit(solution)/shard_map/slice | solution.py:80
  863.1 19.7 %reshape.598 = bf16[8,2,327680]{2,1,0:T(2,128)(2,1)} reshape(bf16[5120,16,64]{2,1,0:T(8,128)(2,1)} %bitcast.399) | data formatting | bytes 20971520
  882.8 5.4 all-to-all-start.5
  889.0 5.6 copy.261
  894.6 110.5 %all-to-all-done.5 = bf16[8,2,327680]{2,1,0:T(2,128)(2,1)} async-done(((bf16[8,2,327680]{2,1,0:T(2,128)(2,1)}), bf16[8,2,327680]{2,1,0:T(2,128)(2,1)}, u32[]{:S(2)}, u32[]{:S(2)}) %all-to-all-start.5) | async-done | bytes 10485792 | tf_op jit(solution)/shard_map/all_to_all | solution.py:80
  1005.1 19.5 %reshape.599 = bf16[5120,16,64]{2,1,0:T(8,128)(2,1)} reshape(bf16[8,2,327680]{2,1,0:T(2,128)(2,1)} %all-to-all-done.5) | data formatting | bytes 20971520
  1024.6 22.7 %copy.297 = bf16[16,64,8,640]{1,2,3,0:T(8,128)(2,1)} copy(bf16[16,64,8,640]{1,0,3,2:T(8,128)(2,1)} %bitcast.396) | data formatting | bytes 20971520 | tf_op jit(solution)/shard_map/all_to_all | solution.py:80
  1047.3 27.8 %reshape.539 = bf16[16,512,1,10,64]{1,4,3,0,2:T(8,128)(2,1)} reshape(bf16[16,8,64,640]{2,1,3,0:T(8,128)(2,1)} %bitcast.397) | data formatting | bytes 20971520 | tf_op jit(solution)/shard_map/reshape | solution.py:87
  1075.1 5.4 broadcast.177
  1080.5 94.4 %while.33 = (s32[]{:T(128)}, f32[16,1,10,64,128]{4,3,2,0,1:T(8,128)}, bf16[16,512,1,10,64]{1,4,3,0,2:T(8,128)(2,1)}, bf16[16,512,1,10]{1,0,3,2:T(8,128)(2,1)S(1)...) while((s32[]{:T(128)}, ...), condition=%wide.region_10.11_spmd.clone, body=%wide.region_7.10_spmd.clone.sunk | while | flops 3023839744 | bytes 77752232 | solution.py:47
  1081.2 9.1 reduce-window.38
  1094.1 14.0 fusion.222
  1108.5 10.3 fusion.223
  1119.4 7.0 bitcast_add_fusion.5
  1126.7 9.1 reduce-window.38
  1139.5 14.0 fusion.222
  1154.0 11.8 fusion.223
  1166.4 8.5 bitcast_add_fusion.5
  1175.0 17.5 %copy.263 = bf16[16,512,640]{2,0,1:T(8,128)(2,1)} copy(bf16[16,512,640]{1,2,0:T(8,128)(2,1)} %bitcast.400) | data formatting | bytes 20971520 | tf_op jit(solution)/shard_map/reshape | solution.py:89
  1192.5 5.4 all-to-all-start.7
  1198.7 76.3 %all-reduce.3.cloned.1.call-done = (bf16[16,1,5376,3]{2,3,0,1:T(4,128)(2,1)}, bf16[16,1,5376,3]{2,3,0,1:T(4,128)(2,1)}) async-done(((bf16[16,1,5376,3]{2,3,0,1:T(4,128)(2,1)}, bf16[16,1,5376,3]{2,3,0,1:T(4,128)(2,1)}), (bf16[16,1,5376,3]{2,3,0,1:T(4,128)(2,1)}, bf16[16,1,5376,3]{2,3,0,1:T(4,128)(2,1)})) %all-reduce.3.cloned.1.call-update) | async-done | bytes 1032208 | tf_op jit(solution)/shard_map/psum | solution.py:95
  1279.5 10.3 pad_maximum_fusion.2
  1289.8 37.8 %all-to-all-done.7 = bf16[16,512,640]{2,0,1:T(8,128)(2,1)} async-done(((bf16[16,512,640]{2,0,1:T(8,128)(2,1)}), bf16[16,512,640]{2,0,1:T(8,128)(2,1)}, u32[]{:S(2)}, u32[]{:S(2)}) %all-to-all-start.7) | async-done | bytes 10485792 | tf_op jit(solution)/shard_map/all_to_all | solution.py:89
  1327.6 10.3 copy.264
  1338.0 13.9 convert_bitcast_fusion.2
  1351.9 8.9 copy.284
  1360.8 8.8 multiply_reduce_fusion
  1369.7 9.1 multiply_convert_fusion.23
  1378.8 32.6 %fusion.143 = f32[16,64,2560]{2,1,0:T(8,128)} fusion(f32[16,64,2560]{2,1,0:T(8,128)} %get-tuple-element.506, bf16[2,5120,2560]{2,1,0:T(8,128)(2,1)} %param.23, bf16[16,64,5120]{2,1,0:T(8,128)(2,1)S(1)} %multiply_convert_fusion.23), kind=kOutput, calls=%fused_computation.176 | convolution fusion | flops 26846167040 | bytes 57671680 | tf_op jit(solution)/shard_map/blgc,gcd->bld/dot_general | solution.py:93
  (208 shorter events, 83.5 us)
Async XLA Ops:
  13.4 71.0 %copy-start.10 = (f32[2,80]{1,0:T(2,128)S(1)}, f32[2,80]{1,0:T(2,128)}, u32[]{:S(2)}) copy-start(f32[2,80]{1,0:T(2,128)} %param.19) | copy-start | bytes 1924
  13.4 80.6 %copy-start.3 = (f32[2,5376,4]{1,2,0:T(4,128)S(1)}, f32[2,5376,4]{1,2,0:T(4,128)}, u32[]{:S(2)}) copy-start(f32[2,5376,4]{1,2,0:T(4,128)} %param.17) | copy-start | bytes 516100
  82.6 13.7 collective-permute-start
  87.5 32.2 %all-to-all-start = ((bf16[8,2,5120]{2,1,0:T(2,128)(2,1)}), bf16[8,2,5120]{2,1,0:T(2,128)(2,1)S(1)}, u32[]{:S(2)}, u32[]{:S(2)}) async-start(bf16[8,2,5120]{2,1,0:T(2,128)(2,1)} %reshape.592), calls=%async_computation | async-start | bytes 327680 | tf_op jit(solution)/shard_map/all_to_all | solution.py:81
  94.7 0.8 copy-start.6
  94.7 4.2 slice-start
  115.5 4.1 copy-start
  122.8 59.0 %all-to-all-start.2 = ((bf16[16,64,2,8,128]{4,1,0,2,3:T(8,128)(2,1)}), bf16[16,64,2,8,128]{4,1,0,2,3:T(8,128)(2,1)}, u32[]{:S(2)}, u32[]{:S(2)}) async-start(bf16[16,64,2,8,128]{4,1,0,2,3:T(8,128)(2,1)} %reshape.535), calls=%async_computation.2 | async-start | bytes 8388608 | tf_op jit(solution)/shard_map/all_to_all | solution.py:82
  181.8 5.6 copy-start.11
  181.8 6.2 copy-start.12
  181.8 122.4 %all-to-all-start.1 = ((bf16[8,2,327680]{2,1,0:T(2,128)(2,1)}), bf16[8,2,327680]{2,1,0:T(2,128)(2,1)}, u32[]{:S(2)}, u32[]{:S(2)}) async-start(bf16[8,2,327680]{2,1,0:T(2,128)(2,1)} %reshape.594), calls=%async_computation.1 | async-start | bytes 20971520 | tf_op jit(solution)/shard_map/all_to_all | solution.py:80
  491.3 5.9 copy-start.7
  491.3 122.8 %all-to-all-start.3 = ((bf16[16,512,640]{2,0,1:T(8,128)(2,1)}), bf16[16,512,640]{2,0,1:T(8,128)(2,1)}, u32[]{:S(2)}, u32[]{:S(2)}) async-start(bf16[16,512,640]{2,0,1:T(8,128)(2,1)} %copy.251), calls=%async_computation.3 | async-start | bytes 20971520 | tf_op jit(solution)/shard_map/all_to_all | solution.py:89
  647.2 21.7 %slice-start.1 = ((s8[10485760]{0:T(1024)(128)(4,1)}), s8[4194304]{0:T(1024)(128)(4,1)S(1)}, s32[]{:S(2)}) async-start(s8[10485760]{0:T(1024)(128)(4,1)} %bitcast.408), calls=%async_computation.10 | async-start | bytes 8388608
  647.2 21.7 %slice-start.2 = ((s8[10485760]{0:T(1024)(128)(4,1)}), s8[4194304]{0:T(1024)(128)(4,1)S(1)}, s32[]{:S(2)}) async-start(s8[10485760]{0:T(1024)(128)(4,1)} %bitcast.408), calls=%async_computation.11 | async-start | bytes 8388608
  656.8 12.1 slice-start.3
  668.9 35.2 %copy-start.8 = (f32[2560]{0:T(1024)S(1)}, f32[2560]{0:T(1024)}, u32[]{:S(2)}) copy-start(f32[2560]{0:T(1024)} %get-tuple-element.451) | copy-start | bytes 30724
  704.1 70.7 %copy-start.2 = (f32[5376,4]{0,1:T(4,128)S(1)}, f32[5376,4]{0,1:T(4,128)}, u32[]{:S(2)}) copy-start(f32[5376,4]{0,1:T(4,128)} %get-tuple-element.495) | copy-start | bytes 258052
  773.5 18.0 %collective-permute-start.1 = (bf16[16,3,5376]{2,0,1:T(8,128)(2,1)S(1)}, bf16[16,3,5376]{2,0,1:T(8,128)(2,1)S(1)}, u32[]{:S(2)}, u32[]{:S(2)}) collective-permute-start(bf16[16,3,5376]{2,0,1:T(8,128)(2,1)S(1)} %copy.256), channel_id=1, source_target_pairs={{0,1},{1,2},{2,3},{3,4},{4,5},{5,6},{6,7},{8,9},{9,10},{10,11},{11... | collective-permute-start | bytes 1548296 | tf_op jit(solution)/shard_map/ppermute | solution.py:73
  775.1 9.7 copy-start.9
  775.1 16.7 %copy-start.4 = (f32[5376]{0:T(1024)S(1)}, f32[5376]{0:T(1024)}, u32[]{:S(2)}) copy-start(f32[5376]{0:T(1024)} %get-tuple-element.449) | copy-start | bytes 64516
  787.3 33.4 %all-to-all-start.4 = ((bf16[8,2,5120]{2,1,0:T(2,128)(2,1)}), bf16[8,2,5120]{2,1,0:T(2,128)(2,1)S(1)}, u32[]{:S(2)}, u32[]{:S(2)}) async-start(bf16[8,2,5120]{2,1,0:T(2,128)(2,1)} %reshape.596), calls=%async_computation.4 | async-start | bytes 327680 | tf_op jit(solution)/shard_map/all_to_all | solution.py:81
  816.5 4.1 copy-start.1
  823.8 59.0 %all-to-all-start.6 = ((bf16[16,64,2,8,128]{4,1,0,2,3:T(8,128)(2,1)}), bf16[16,64,2,8,128]{4,1,0,2,3:T(8,128)(2,1)}, u32[]{:S(2)}, u32[]{:S(2)}) async-start(bf16[16,64,2,8,128]{4,1,0,2,3:T(8,128)(2,1)} %reshape.541), calls=%async_computation.6 | async-start | bytes 8388608 | tf_op jit(solution)/shard_map/all_to_all | solution.py:82
  882.8 5.4 copy-start.13
  882.8 5.5 copy-start.14
  882.8 122.2 %all-to-all-start.5 = ((bf16[8,2,327680]{2,1,0:T(2,128)(2,1)}), bf16[8,2,327680]{2,1,0:T(2,128)(2,1)}, u32[]{:S(2)}, u32[]{:S(2)}) async-start(bf16[8,2,327680]{2,1,0:T(2,128)(2,1)} %reshape.598), calls=%async_computation.5 | async-start | bytes 20971520 | tf_op jit(solution)/shard_map/all_to_all | solution.py:80
  1192.5 135.1 %all-to-all-start.7 = ((bf16[16,512,640]{2,0,1:T(8,128)(2,1)}), bf16[16,512,640]{2,0,1:T(8,128)(2,1)}, u32[]{:S(2)}, u32[]{:S(2)}) async-start(bf16[16,512,640]{2,0,1:T(8,128)(2,1)} %copy.263), calls=%async_computation.7 | async-start | bytes 20971520 | tf_op jit(solution)/shard_map/all_to_all | solution.py:89
  1197.9 77.1 %all-reduce.3.cloned.1.call-start = ((), (), s32[]{:S(2)}) async-start(), calls=%async_computation.8 | async-start | bytes 2752512 | tf_op jit(solution)/shard_map/psum | solution.py:95
  1360.8 8.8 copy-start.5
Sparse Core Ops, SparseCore 0:
  1201.8 73.1 all-reduce.2
where the time goes:
time: 1430 us; the launch traced here: 1420 us
  waiting for transfers between devices  451 us (32%)
  local copies, waits for them, and re-layouts  392 us (27%)
  matrix products  341 us (24%)
  other arithmetic  172 us (12%)
  starting transfers between devices  46.5 us (3%)
  between operations  14.7 us (1%)
    all_to_all x2, waiting for transfers between devices, layer(): x_local = lax.all_to_all(activated[..., :d_inner], 'sp', 2, 1, tiled=True)  220 us
    all_to_all x2, waiting for transfers between devices, layer(): lax.all_to_all(y_local.reshape(batch, seq_len, local_heads * head_dim), '...  154 us
    dot_general x2, matrix products, layer(): jnp.einsum('bld,de->ble', normed, w_in_l, preferred_element_type=jnp.floa...  133 us
    unnamed x45, local copies, waits for them, and re-layouts  92.1 us
    psum x1, waiting for transfers between devices, layer(): conv_state = lax.psum(tail_rows, 'sp')  76.3 us
    slice x4, local copies, waits for them, and re-layouts, layer(): x_local = lax.all_to_all(activated[..., :d_inner], 'sp', 2, 1, tiled=True)  68.2 us
    dot_general x2, matrix products, layer(): jnp.einsum('blgc,gcd->bld', normed_y, w_out_l.reshape(n_groups, group_wid...  67.8 us
    dot_general x4, matrix products, body(): jnp.einsum('bghts,bsghp->btghp', mix_mat, x_scaled, preferred_element_typ...  56 us
  transfers between devices with their start and end apart: 11, of which 5 were waited for; matrix products, arithmetic and copies ran while one was open for 14% of the time, Pallas kernels for 0%

commit v1 on v0

v1 whole, which is shorter than its diff:
```python
import functools

import jax
import jax.numpy as jnp
from jax import lax
from jax.experimental import pallas as pl
from jax.experimental.pallas import tpu as pltpu
from jax.sharding import PartitionSpec as P

CONV_WIDTH = 4
EPSILON = 1e-5
LANES = 128
CHUNKS = 4


def conv_kernel(n_prompts, seg_len, width, n_heads, x_ref, bc_ref, dtr_ref, xh_ref, bch_ref, wx_ref, wbc_ref, bx_ref, bbc_ref, dtb_ref, sel_ref, out_ref, bc_keep, dt_keep):
    dest = pl.program_id(0)
    taps = CONV_WIDTH - 1
    blocks = width // LANES

    def conv(cur, halo, w, bias):
        cur = cur.astype(jnp.float32)
        halo = halo.astype(jnp.float32)
        acc = bias + cur * w[taps:taps + 1]
        for back in range(1, CONV_WIDTH):
            shifted = jnp.concatenate([halo[taps - back:], cur[:seg_len - back]], axis=0)
            acc = acc + shifted * w[taps - back:taps - back + 1]
        return (acc * jax.nn.sigmoid(acc)).astype(jnp.bfloat16)

    @pl.when(dest == 0)
    def _():
        raw = dtr_ref[...].astype(jnp.float32)
        column = lax.broadcasted_iota(jnp.int32, raw.shape, 1)
        delta = jax.nn.softplus(raw + dtb_ref[...])
        delta = jnp.where(column < n_heads, delta, 0.0).astype(jnp.bfloat16)
        rows = lax.dot_general(sel_ref[...], delta, (((1,), (1,)), ((), ())), preferred_element_type=jnp.float32)
        rows = rows.astype(jnp.bfloat16)
        for d in range(dt_keep.shape[0]):
            for part in range(dt_keep.shape[1] // 16):
                dt_keep[d, part * 16:(part + 1) * 16] = rows[d * 16:(d + 1) * 16, part * LANES:(part + 1) * LANES]

    @pl.when(dest < 2)
    def _():
        for p in range(n_prompts):
            bc_keep[dest, p] = conv(bc_ref[p * seg_len:(p + 1) * seg_len], bch_ref[p], wbc_ref[...], bbc_ref[...])

    parity = lax.rem(dest, 2)
    per_prompt = (blocks + 1) * seg_len
    for p in range(n_prompts):
        for j in range(blocks):
            cols = slice(j * LANES, (j + 1) * LANES)
            out_ref[0, p * per_prompt + j * seg_len:p * per_prompt + (j + 1) * seg_len] = conv(
                x_ref[p * seg_len:(p + 1) * seg_len, cols], xh_ref[p, :, cols], wx_ref[:, cols], bx_ref[:, cols])
        out_ref[0, p * per_prompt + blocks * seg_len:(p + 1) * per_prompt] = bc_keep[parity, p]
    out_ref[0, n_prompts * per_prompt:] = dt_keep[dest]


def conv_call(u, halo, conv_w, conv_b, dt_b, select, sizes):
    n_prompts, seg_len, d_inner, conv_dim, n_heads, n_dest = sizes
    width = d_inner // n_dest
    blocks = width // LANES
    dt_rows = n_prompts * seg_len // LANES * 16
    rows = n_prompts * (blocks + 1) * seg_len + dt_rows
    tokens = n_prompts * seg_len
    x0 = d_inner // width
    bc0 = 2 * d_inner // LANES
    dt0 = (d_inner + conv_dim) // LANES
    taps = CONV_WIDTH - 1
    body = functools.partial(conv_kernel, n_prompts, seg_len, width, n_heads)
    parity = lambda d: lax.rem(d, 2)
    return pl.pallas_call(
        body,
        grid=(n_dest,),
        in_specs=[
            pl.BlockSpec((tokens, width), lambda d: (0, x0 + d)),
            pl.BlockSpec((tokens, LANES), lambda d: (0, bc0 + parity(d))),
            pl.BlockSpec((tokens, LANES), lambda d: (0, dt0)),
            pl.BlockSpec((n_prompts, taps, width), lambda d: (0, 0, d)),
            pl.BlockSpec((n_prompts, taps, LANES), lambda d: (0, 0, d_inner // LANES + parity(d))),
            pl.BlockSpec((CONV_WIDTH, width), lambda d: (0, d)),
            pl.BlockSpec((CONV_WIDTH, LANES), lambda d: (0, d_inner // LANES + parity(d))),
            pl.BlockSpec((1, width), lambda d: (0, d)),
            pl.BlockSpec((1, LANES), lambda d: (0, d_inner // LANES + parity(d))),
            pl.BlockSpec((1, LANES), lambda d: (0, 0)),
            pl.BlockSpec((n_dest * 16, LANES), lambda d: (0, 0)),
        ],
        out_specs=pl.BlockSpec((1, rows, LANES), lambda d: (d, 0, 0)),
        out_shape=jax.ShapeDtypeStruct((n_dest, rows, LANES), jnp.bfloat16),
        scratch_shapes=[
            pltpu.VMEM((2, n_prompts, seg_len, LANES), jnp.bfloat16),
            pltpu.VMEM((n_dest, dt_rows, LANES), jnp.bfloat16),
        ],
        compiler_params=pltpu.CompilerParams(vmem_limit_bytes=16 * 1024 * 1024),
        cost_estimate=pl.CostEstimate(flops=tokens * d_inner * 60, bytes_accessed=4 * tokens * d_inner, transcendentals=tokens * d_inner),
        name='conv_pack',
    )(u, u, u, halo, halo, conv_w, conv_w, conv_b, conv_b, dt_b, select)


def scan_kernel(seg_count, seg_len, blocks, n_local, head_dim, par_ref, x_ref, other_ref, dt_ref, a_ref, d_ref, *rest):
    y_ref, fin_ref, state = rest[-3:]
    per_chunk = LANES // seg_len
    pairs = LANES // head_dim
    tokens = LANES
    even = par_ref[0] == 0
    row = lax.broadcasted_iota(jnp.int32, (tokens, tokens), 0)
    col = lax.broadcasted_iota(jnp.int32, (tokens, tokens), 1)
    causal = row >= col
    first = col < head_dim
    lane = lax.broadcasted_iota(jnp.int32, (16, tokens), 1)
    a_neg = a_ref[...]
    for half in range(LANES // seg_len):
        per_prompt = (blocks + 1) * seg_len
        base = half * per_prompt
        state[...] = jnp.zeros_like(state)
        for chunk in range(seg_count // per_chunk):
            segs = range(chunk * per_chunk, (chunk + 1) * per_chunk)
            tok = lambda ref, lo: jnp.concatenate([ref[s, lo:lo + seg_len] for s in segs], axis=0)
            mine = tok(x_ref, base + blocks * seg_len)
            other = tok(other_ref, half * seg_len)
            b_mat = jnp.where(even, mine, other)
            c_mat = jnp.where(even, other, mine)
            dt = jnp.concatenate([dt_ref[s, :16, half * seg_len:(half + 1) * seg_len] for s in segs], axis=1).astype(jnp.float32)
            cum = dt * a_neg
            step = 1
            while step < tokens:
                cum = cum + jnp.where(lane >= step, pltpu.roll(cum, step, 1), 0.0)
                step *= 2
            last = cum[:, tokens - 1:]
            weight = jnp.exp(last - cum) * dt
            cum_c = cum.T
            dt_c = dt.T
            exp_c = jnp.exp(cum_c)
            weight_c = weight.T
            last_e = jnp.exp(last)
            scores = lax.dot_general(c_mat, b_mat, (((1,), (1,)), ((), ())), preferred_element_type=jnp.float32)
            scores = jnp.where(causal, scores, 0.0)
            for j in range(blocks):
                heads = [j * pairs + k for k in range(pairs)]
                pick = lambda arr: jnp.where(first, arr[:, heads[0]:heads[0] + 1], arr[:, heads[1]:heads[1] + 1])
                mixes = []
                for h in heads:
                    diff = jnp.where(causal, cum_c[:, h:h + 1] - cum[h:h + 1, :], -jnp.inf)
                    mixes.append((jnp.exp(diff) * scores).astype(jnp.bfloat16))
                x2 = tok(x_ref, base + j * seg_len).astype(jnp.float32)
                xs = (x2 * pick(dt_c)).astype(jnp.bfloat16)
                zero = jnp.zeros_like(xs)
                stacked = jnp.concatenate([jnp.where(first, xs, zero), jnp.where(first, zero, xs)], axis=0)
                y_intra = jnp.dot(jnp.concatenate(mixes, axis=1), stacked, preferred_element_type=jnp.float32)
                s_old = state[j * LANES:(j + 1) * LANES]
                y_inter = lax.dot_general(c_mat, s_old.astype(jnp.bfloat16), (((1,), (1,)), ((), ())), preferred_element_type=jnp.float32)
                y = y_intra + y_inter * pick(exp_c) + d_ref[:, j * LANES:(j + 1) * LANES] * x2
                y = y.astype(jnp.bfloat16)
                for k, s in enumerate(segs):
                    y_ref[s, (half * blocks + j) * seg_len:(half * blocks + j + 1) * seg_len] = y[k * seg_len:(k + 1) * seg_len]
                xw = (x2 * pick(weight_c)).astype(jnp.bfloat16)
                gain = lax.dot_general(xw, b_mat, (((0,), (0,)), ((), ())), preferred_element_type=jnp.float32)
                decay = jnp.concatenate([jnp.broadcast_to(last_e[h:h + 1], (head_dim, 1)) for h in heads], axis=0)
                state[j * LANES:(j + 1) * LANES] = s_old * decay + gain
        for h in range(n_local):
            fin_ref[half, 0, h] = state[h * head_dim:(h + 1) * head_dim]


def scan_call(parity, packed, other, a_neg, d_wide, finals, place, sizes):
    n_prompts, seg_len, seg_count, n_local, head_dim, d_state, batch, layers = sizes
    blocks = n_local * head_dim // LANES
    group = LANES // seg_len
    per_prompt = (blocks + 1) * seg_len
    dt_first = n_prompts * per_prompt // 16
    layer_index, first_prompt = place
    steps = n_prompts // group
    body = functools.partial(scan_kernel, seg_count, seg_len, blocks, n_local, head_dim)
    in_specs = [
        pl.BlockSpec(memory_space=pltpu.SMEM),
        pl.BlockSpec((seg_count, group * per_prompt, LANES), lambda g: (0, g, 0)),
        pl.BlockSpec((seg_count, group * seg_len, LANES), lambda g: (0, g, 0)),
        pl.BlockSpec((seg_count, 16, LANES), lambda g: (0, dt_first + g, 0)),
        pl.BlockSpec((16, LANES), lambda g: (0, 0)),
        pl.BlockSpec((1, n_local * head_dim), lambda g: (0, 0)),
    ]
    operands = [parity, packed, other, packed, a_neg, d_wide]
    aliases = {}
    if finals is not None:
        in_specs.append(pl.BlockSpec(memory_space=pl.ANY))
        operands.append(finals)
        aliases = {6: 1}
    tokens = n_prompts * seg_len * seg_count
    return pl.pallas_call(
        body,
        grid=(steps,),
        in_specs=in_specs,
        out_specs=[
            pl.BlockSpec((seg_count, group * blocks * seg_len, LANES), lambda g: (0, g, 0)),
            pl.BlockSpec((group, 1, n_local, head_dim, d_state), lambda g: (first_prompt // group + g, layer_index, 0, 0, 0)),
        ],
        out_shape=[
            jax.ShapeDtypeStruct((seg_count, n_prompts * blocks * seg_len, LANES), jnp.bfloat16),
            jax.ShapeDtypeStruct((batch, layers, n_local, head_dim, d_state), jnp.float32),
        ],
        scratch_shapes=[pltpu.VMEM((n_local * head_dim, d_state), jnp.float32)],
        input_output_aliases=aliases,
        compiler_params=pltpu.CompilerParams(vmem_limit_bytes=24 * 1024 * 1024),
        cost_estimate=pl.CostEstimate(flops=tokens * n_local * 16000, bytes_accessed=tokens * n_local * head_dim * 6, transcendentals=tokens * n_local * LANES),
        name='scan',
    )(*operands)


def gate_kernel(n_src, blocks, seg_len, y_ref, z_ref, w_ref, out_ref, keep):
    total = jnp.zeros((seg_len, LANES), jnp.float32)
    for d in range(n_src):
        for j in range(blocks):
            cols = slice((d * blocks + j) * LANES, (d * blocks + j + 1) * LANES)
            z = z_ref[:, cols].astype(jnp.float32)
            g = y_ref[d, j * seg_len:(j + 1) * seg_len].astype(jnp.float32) * (z * jax.nn.sigmoid(z))
            keep[:, cols] = g
            total = total + g * g
    width = n_src * blocks * LANES
    scale = lax.rsqrt(jnp.sum(total, axis=1, keepdims=True) / width + EPSILON)
    for i in range(n_src * blocks):
        cols = slice(i * LANES, (i + 1) * LANES)
        out_ref[:, cols] = (keep[:, cols] * scale * w_ref[:, cols]).astype(jnp.bfloat16)


def gate_call(y, u, gate_w, n_prompts, seg_len, d_inner):
    n_src = y.shape[0]
    blocks = d_inner // n_src // LANES
    tokens = n_prompts * seg_len
    return pl.pallas_call(
        functools.partial(gate_kernel, n_src, blocks, seg_len),
        grid=(n_prompts,),
        in_specs=[
            pl.BlockSpec((n_src, blocks * seg_len, LANES), lambda p: (0, p, 0)),
            pl.BlockSpec((seg_len, d_inner), lambda p: (p, 0)),
            pl.BlockSpec((1, d_inner), lambda p: (0, 0)),
        ],
        out_specs=pl.BlockSpec((seg_len, d_inner), lambda p: (p, 0)),
        out_shape=jax.ShapeDtypeStruct((tokens, d_inner), jnp.bfloat16),
        scratch_shapes=[pltpu.VMEM((seg_len, d_inner), jnp.float32)],
        compiler_params=pltpu.CompilerParams(vmem_limit_bytes=16 * 1024 * 1024),
        cost_estimate=pl.CostEstimate(flops=tokens * d_inner * 40, bytes_accessed=6 * tokens * d_inner, transcendentals=tokens * d_inner),
        name='gate',
    )(y, u, gate_w)


def solution(mesh):
    seg_count = mesh.shape['sp']

    def forward(resid, pre_norm, w_in, conv_w, conv_b, dt_bias, a_log, d_skip, gate_norm, w_out):
        batch, seg_len, d_model = resid.shape
        layers, n_heads = dt_bias.shape
        conv_dim = conv_b.shape[1]
        d_inner = gate_norm.shape[1] * gate_norm.shape[2]
        d_state = (conv_dim - d_inner) // 2
        head_dim = d_inner // n_heads
        n_local = n_heads // seg_count
        n_prompts = batch // CHUNKS
        blocks = n_local * head_dim // LANES
        per_prompt = (blocks + 1) * seg_len
        taps = CONV_WIDTH - 1
        seg_index = lax.axis_index('sp')
        parity = lax.rem(seg_index, 2).astype(jnp.int32).reshape(1)
        forward_pairs = [(source, source + 1) for source in range(seg_count - 1)]
        core_pairs = [(source, source ^ 1) for source in range(seg_count)]

        slot = jnp.arange(seg_count * 16)
        wanted = jnp.where(slot % 16 < n_local, slot // 16 * n_local + slot % 16, -1)
        select = (wanted[:, None] == jnp.arange(LANES)[None, :]).astype(jnp.bfloat16)
        pad_heads = lambda values: jnp.pad(values, ((0, 0), (0, LANES - n_heads)))
        dt_bias_wide = pad_heads(dt_bias)
        conv_wt = jnp.swapaxes(conv_w, 1, 2)

        finals = None
        tails = []
        streams = [resid[c * n_prompts:(c + 1) * n_prompts].reshape(n_prompts * seg_len, d_model) for c in range(CHUNKS)]
        for l in range(layers):
            mine = lax.dynamic_slice_in_dim(a_log[l], seg_index * n_local, n_local)
            a_neg = jnp.broadcast_to(jnp.pad(-jnp.exp(mine), (0, 16 - n_local))[:, None], (16, LANES))
            d_wide = jnp.repeat(lax.dynamic_slice_in_dim(d_skip[l], seg_index * n_local, n_local), head_dim)[None]
            layer_tails = []
            for c in range(CHUNKS):
                r = streams[c]
                with jax.named_scope(f'in{l}_{c}'):
                    h = (r * lax.rsqrt(jnp.mean(r * r, axis=-1, keepdims=True) + EPSILON) * pre_norm[l]).astype(jnp.bfloat16)
                    u = jnp.dot(h, w_in[l], preferred_element_type=jnp.float32).astype(jnp.bfloat16)
                    tail = u.reshape(n_prompts, seg_len, -1)[:, seg_len - taps:, d_inner:d_inner + conv_dim]
                    halo = lax.ppermute(tail, 'sp', forward_pairs)
                    layer_tails.append(tail)
                    packed = conv_call(u, halo, conv_wt[l], conv_b[l:l + 1], dt_bias_wide[l:l + 1], select, (n_prompts, seg_len, d_inner, conv_dim, n_heads, seg_count))
                with jax.named_scope(f'go{l}_{c}'):
                    packed = lax.all_to_all(packed, 'sp', 0, 0, tiled=True)
                with jax.named_scope(f'scan{l}_{c}'):
                    bc = packed[:, :n_prompts * per_prompt].reshape(seg_count, n_prompts, blocks + 1, seg_len, LANES)[:, :, blocks]
                    other = lax.ppermute(bc.reshape(seg_count, n_prompts * seg_len, LANES), 'sp', core_pairs)
                    y, finals = scan_call(parity, packed, other, a_neg, d_wide, finals, (l, c * n_prompts), (n_prompts, seg_len, seg_count, n_local, head_dim, d_state, batch, layers))
                with jax.named_scope(f'back{l}_{c}'):
                    y = lax.all_to_all(y, 'sp', 0, 0, tiled=True)
                with jax.named_scope(f'out{l}_{c}'):
                    g = gate_call(y, u, gate_norm[l], n_prompts, seg_len, d_inner)
                    streams[c] = r + jnp.dot(g, w_out[l], preferred_element_type=jnp.float32)
            tails.append(jnp.concatenate(layer_tails, axis=0))
        tail_rows = jnp.stack(tails, axis=2)
        tail_rows = jnp.where(seg_index == seg_count - 1, tail_rows, jnp.zeros((), jnp.bfloat16))
        conv_state = lax.psum(tail_rows, 'sp')
        out = jnp.concatenate(streams, axis=0).reshape(batch, seg_len, d_model)
        return out, finals, jnp.transpose(conv_state, (0, 2, 3, 1))

    return jax.shard_map(forward, mesh=mesh, in_specs=(P('dp', 'sp', None), P(), P(), P(), P(), P(), P(), P(), P(), P()), out_specs=(P('dp', 'sp', None), P('dp', None, 'sp', None, None), P('dp', None, None, None)), check_vma=False)
```

time: 1430 us -> 1010 us (0.71)
  waiting for transfers between devices: 451 us -> 141 us
  local copies, waits for them, and re-layouts: 392 us -> 106 us
  Pallas kernels: 0 us -> 274 us
  other arithmetic: 172 us -> 24.5 us
  starting transfers between devices: 46.5 us -> 133 us
  matrix products: 341 us -> 307 us
    all_to_all x8 -> x16, waiting for transfers between devices: 374 us -> 75.2 us  [the longest x8 39.5 us: forward(): y = lax.all_to_all(y, 'sp', 0, 0, tiled=True)]
    pallas_call x0 -> x24, Pallas kernels: none -> 274 us  [the longest x8 205 us: scan_call(): pl.pallas_call(body, grid=(steps,), in_specs=in_specs, out_specs=[pl.Bloc...]
    reshape x10 -> x0, local copies, waits for them, and re-layouts: 97.6 us -> none  [the longest x2 55.6 us: layer(): x_local.reshape(batch, seq_len, local_groups, local_per_group, head_dim)]
    all_to_all x8 -> x0, local copies, waits for them, and re-layouts: 77.6 us -> none  [the longest x2 45.4 us: layer(): x_local = lax.all_to_all(activated[..., :d_inner], 'sp', 2, 1, tiled=True)]
    all_to_all x8 -> x16, starting transfers between devices: 43.1 us -> 109 us  [the longest x8 72.9 us: forward(): packed = lax.all_to_all(packed, 'sp', 0, 0, tiled=True)]
    slice x24 -> x29, local copies, waits for them, and re-layouts: 85.6 us -> 28.7 us  [the longest x16 17.5 us: forward(): packed[:, :n_prompts * per_prompt]]
    another operation x20 -> x2, other arithmetic: 55.2 us -> 4.1 us  [forward(): tail_rows = jnp.stack(tails, axis=2)]
    convert_element_type x4 -> x2, other arithmetic: 43.8 us -> 6 us  [the longest x1 5.92 us: forward(): (r * lax.rsqrt(jnp.mean(r * r, axis=-1, keepdims=True) + EPSILON) * pre_n...]
  transfers between devices with their start and end apart: 11 -> 33, of which waited for: 5 -> 19; matrix products, arithmetic and copies ran while one was open for 14% -> 31% of each run, Pallas kernels for 0% -> 27%
where the time goes in v1:
time: 1010 us; the launch traced here: 1000 us
  matrix products  307 us (30%)
  Pallas kernels  274 us (27%)
  waiting for transfers between devices  141 us (14%)
  starting transfers between devices  133 us (13%)
  local copies, waits for them, and re-layouts  106 us (10%)
  other arithmetic  24.5 us (2%)
  between operations  15.4 us (2%)
    pallas_call x8, Pallas kernels, scan_call(): pl.pallas_call(body, grid=(steps,), in_specs=in_specs, out_specs=[pl.Bloc...  205 us
    dot_general x8, matrix products, forward(): jnp.dot(h, w_in[l], preferred_element_type=jnp.float32).astype(jnp.bfloat16)  196 us
    dot_general x8, matrix products, forward(): streams[c] = r + jnp.dot(g, w_out[l], preferred_element_type=jnp.float32)  112 us
    unnamed x127, local copies, waits for them, and re-layouts  76.1 us
    all_to_all x8, starting transfers between devices, forward(): packed = lax.all_to_all(packed, 'sp', 0, 0, tiled=True)  72.9 us
    psum x1, waiting for transfers between devices, forward(): conv_state = lax.psum(tail_rows, 'sp')  59.4 us
    pallas_call x8, Pallas kernels, conv_call(): pl.pallas_call(body, grid=(n_dest,), in_specs=[pl.BlockSpec((tokens, widt...  43.7 us
    all_to_all x8, waiting for transfers between devices, forward(): y = lax.all_to_all(y, 'sp', 0, 0, tiled=True)  39.5 us
  transfers between devices with their start and end apart: 33, of which 19 were waited for; matrix products, arithmetic and copies ran while one was open for 31% of the time, Pallas kernels for 27%

profile of v1, /device:TPU:112, one launch (start us, length us, event | category | flops | bytes accessed | tf_op | source)
XLA Modules:
  0.0 1000.3 jit_solution(15457899835710885050)
XLA Ops:
  7.2 5.0 multiply_reduce_fusion.7
  14.2 5.9 multiply_convert_fusion.7
  20.2 23.7 %fusion.48.x_ref.bc_ref.dtr_ref.z_ref = bf16[256,10576]{1,0:T(8,128)(2,1)} fusion(bf16[256,2560]{1,0:T(8,128)(2,1)S(1)} %bitcast.173, bf16[2,2560,10576]{1,2,0:T(8,128)(2,1)} %param.12), kind=kOutput, calls=%fused_computation.48 | convolution fusion | flops 13864882176 | bytes 60874752 | tf_op jit(solution)/shard_map/in0_0/dot_general | solution.py:283
  50.3 5.1 conv_pack.8
  57.1 9.3 all-to-all-start
  66.4 24.1 %fusion.57.x_ref.bc_ref.dtr_ref.z_ref = bf16[256,10576]{1,0:T(8,128)(2,1)} fusion(bf16[256,2560]{1,0:T(8,128)(2,1)} %bitcast.172, bf16[2,2560,10576]{1,2,0:T(8,128)(2,1)} %param.12), kind=kOutput, calls=%fused_computation.51 | convolution fusion | flops 13864882176 | bytes 60874752 | tf_op jit(solution)/shard_map/in0_1/dot_general | solution.py:283
  97.5 5.1 conv_pack.12
  105.9 12.8 %all-to-all-start.5 = ((bf16[8,1568,128]{2,1,0:T(8,128)(2,1)}), bf16[8,1568,128]{2,1,0:T(8,128)(2,1)}, u32[]{:S(2)}, u32[]{:S(2)}) async-start(bf16[8,1568,128]{2,1,0:T(8,128)(2,1)} %copy-done.22), calls=%async_computation.5 | async-start | bytes 6422528 | tf_op jit(solution)/shard_map/go0_1/all_to_all | solution.py:289
  118.7 24.0 %fusion.54.x_ref.bc_ref.dtr_ref.z_ref = bf16[256,10576]{1,0:T(8,128)(2,1)} fusion(bf16[256,2560]{1,0:T(8,128)(2,1)} %bitcast.171, bf16[2,2560,10576]{1,2,0:T(8,128)(2,1)} %param.12), kind=kOutput, calls=%fused_computation.50 | convolution fusion | flops 13864882176 | bytes 60874752 | tf_op jit(solution)/shard_map/in0_2/dot_general | solution.py:283
  149.8 5.1 conv_pack.11
  158.0 12.5 %all-to-all-start.4 = ((bf16[8,1568,128]{2,1,0:T(8,128)(2,1)}), bf16[8,1568,128]{2,1,0:T(8,128)(2,1)}, u32[]{:S(2)}, u32[]{:S(2)}) async-start(bf16[8,1568,128]{2,1,0:T(8,128)(2,1)} %copy-done.20), calls=%async_computation.4 | async-start | bytes 6422528 | tf_op jit(solution)/shard_map/go0_2/all_to_all | solution.py:289
  170.5 24.0 %fusion.51.x_ref.bc_ref.dtr_ref.z_ref = bf16[256,10576]{1,0:T(8,128)(2,1)} fusion(bf16[256,2560]{1,0:T(8,128)(2,1)} %bitcast.170, bf16[2,2560,10576]{1,2,0:T(8,128)(2,1)} %param.12), kind=kOutput, calls=%fused_computation.49 | convolution fusion | flops 13864882176 | bytes 60874752 | tf_op jit(solution)/shard_map/in0_3/dot_general | solution.py:283
  201.6 5.1 conv_pack.10
  210.0 13.0 %all-to-all-start.3 = ((bf16[8,1568,128]{2,1,0:T(8,128)(2,1)}), bf16[8,1568,128]{2,1,0:T(8,128)(2,1)}, u32[]{:S(2)}, u32[]{:S(2)}) async-start(bf16[8,1568,128]{2,1,0:T(8,128)(2,1)} %copy-done.16), calls=%async_computation.3 | async-start | bytes 6422528 | tf_op jit(solution)/shard_map/go0_3/all_to_all | solution.py:289
  226.1 25.4 %scan.8 = (bf16[8,1280,128]{2,1,0:T(8,128)(2,1)S(1)}, f32[16,2,10,64,128]{4,3,2,1,0:T(8,128)}) custom-call(s32[1]{0:T(128)} %bitcast.1.par_ref, bf16[8,1568,128]{2,1,0:T(8,128)(2,1)S(1)} %all-to-all-done.x_ref.dt_ref, bf16[8,256,128]{2,1,0:T(8,128)(2,1)} %collective-permute-done.1.other_ref, bf16[8,1568,128]{2,1,0:T(8,128)(2,1)S(1)} %all-to-all-done.x_ref.dt_ref, ...), custom_call_target="tpu_custom_call" | custom-call | flops 327680000 | bytes 7864320 | tf_op jit(solution)/shard_map/scan0_0/scan/pallas_call | solution.py:187
  252.9 9.0 all-to-all-done.3.x_ref.dt_ref
  261.9 4.3 all-to-all-start.1
  273.8 25.5 %scan.9 = (bf16[8,1280,128]{2,1,0:T(8,128)(2,1)S(1)}, f32[16,2,10,64,128]{4,3,2,1,0:T(8,128)}) custom-call(s32[1]{0:T(128)} %bitcast.1.par_ref, bf16[8,1568,128]{2,1,0:T(8,128)(2,1)} %all-to-all-done.5.x_ref.dt_ref, bf16[8,256,128]{2,1,0:T(8,128)(2,1)S(1)} %collective-permute-done.9.other_ref, ...), custom_call_target="tpu_custom_call", output_to_operand_aliasing={{1}: (6, {})} | custom-call | flops 327680000 | bytes 7864320 | tf_op jit(solution)/shard_map/scan0_1/scan/pallas_call | solution.py:187
  300.8 25.7 %scan.10 = (bf16[8,1280,128]{2,1,0:T(8,128)(2,1)S(1)}, f32[16,2,10,64,128]{4,3,2,1,0:T(8,128)}) custom-call(s32[1]{0:T(128)} %bitcast.1.par_ref, bf16[8,1568,128]{2,1,0:T(8,128)(2,1)} %all-to-all-done.4.x_ref.dt_ref, bf16[8,256,128]{2,1,0:T(8,128)(2,1)S(1)} %collective-permute-done.7.other_ref, ...), custom_call_target="tpu_custom_call", output_to_operand_aliasing={{1}: (6, {})} | custom-call | flops 327680000 | bytes 7864320 | tf_op jit(solution)/shard_map/scan0_2/scan/pallas_call | solution.py:187
  328.0 25.7 %scan.11 = (bf16[8,1280,128]{2,1,0:T(8,128)(2,1)S(1)}, f32[16,2,10,64,128]{4,3,2,1,0:T(8,128)}) custom-call(s32[1]{0:T(128)} %bitcast.1.par_ref, bf16[8,1568,128]{2,1,0:T(8,128)(2,1)} %all-to-all-done.3.x_ref.dt_ref, bf16[8,256,128]{2,1,0:T(8,128)(2,1)S(1)} %collective-permute-done.5.other_ref, ...), custom_call_target="tpu_custom_call", output_to_operand_aliasing={{1}: (6, {})} | custom-call | flops 327680000 | bytes 7864320 | tf_op jit(solution)/shard_map/scan0_3/scan/pallas_call | solution.py:187
  355.2 4.9 all-to-all-start.7
  365.3 12.9 %multiply_reduce_fusion.6 = (f32[256]{0:T(256)S(1)}, f32[256,2560]{1,0:T(8,128)S(1)}) fusion(f32[256,2560]{1,0:T(8,128)} %bitcast.169, bf16[256,5120]{1,0:T(8,128)(2,1)S(1)} %gate.8, bf16[2,5120,2560]{2,1,0:T(8,128)(2,1)} %param.19), kind=kOutput, calls=%fused_computation.78 | convolution fusion | flops 6712852480 | bytes 34079744 | tf_op jit(solution)/shard_map/out0_0/dot_general | solution.py:298
  378.2 25.2 %fusion.60.x_ref.bc_ref.dtr_ref.z_ref = bf16[256,10576]{1,0:T(8,128)(2,1)} fusion(bf16[2,2560,10576]{1,2,0:T(8,128)(2,1)} %param.12, f32[256,2560]{1,0:T(8,128)S(1)} %get-tuple-element.71, f32[2560]{0:T(1024)S(1)} %copy-done.52, f32[256]{0:T(256)S(1)} %add_rsqrt_fusion.7), kind=kOutput, calls=%fused_computation.52 | convolution fusion | flops 13866848256 | bytes 62196736 | tf_op jit(solution)/shard_map/in1_0/dot_general | solution.py:283
  405.1 5.4 all-to-all-start.10
  413.1 4.0 gate.10
  417.1 13.8 %multiply_reduce_fusion.2 = (f32[256]{0:T(256)S(1)}, f32[256,2560]{1,0:T(8,128)}) fusion(f32[256,2560]{1,0:T(8,128)} %bitcast.168, bf16[256,5120]{1,0:T(8,128)(2,1)S(1)} %gate.10, bf16[2,5120,2560]{2,1,0:T(8,128)(2,1)} %param.19), kind=kOutput, calls=%fused_computation.70 | convolution fusion | flops 6712852480 | bytes 34079744 | tf_op jit(solution)/shard_map/out0_1/dot_general | solution.py:298
  430.9 24.8 %fusion.63.x_ref.bc_ref.dtr_ref.z_ref = bf16[256,10576]{1,0:T(8,128)(2,1)} fusion(bf16[2,2560,10576]{1,2,0:T(8,128)(2,1)} %param.12, f32[256,2560]{1,0:T(8,128)} %get-tuple-element.69, f32[256]{0:T(256)S(1)} %add_rsqrt_fusion.6, f32[2560]{0:T(1024)S(1)} %copy-done.52), kind=kOutput, calls=%fused_computation.53 | convolution fusion | flops 13866848256 | bytes 62196736 | tf_op jit(solution)/shard_map/in1_1/dot_general | solution.py:283
  457.5 3.1 collective-permute-start.2
  460.6 3.6 collective-permute-start.10
  465.7 3.8 all-to-all-start.13
  478.1 14.7 %multiply_reduce_fusion.1 = (f32[256]{0:T(256)S(1)}, f32[256,2560]{1,0:T(8,128)}) fusion(f32[256,2560]{1,0:T(8,128)} %bitcast.167, bf16[256,5120]{1,0:T(8,128)(2,1)} %copy-done.37, bf16[2,5120,2560]{2,1,0:T(8,128)(2,1)} %param.19), kind=kOutput, calls=%fused_computation.68 | convolution fusion | flops 6712852480 | bytes 34079744 | tf_op jit(solution)/shard_map/out0_2/dot_general | solution.py:298
  492.8 6.0 conv_pack.9
  503.7 4.0 all-to-all-start.2
  507.7 24.8 %fusion.66.x_ref.bc_ref.dtr_ref.z_ref = bf16[256,10576]{1,0:T(8,128)(2,1)} fusion(bf16[2,2560,10576]{1,2,0:T(8,128)(2,1)} %param.12, f32[256,2560]{1,0:T(8,128)} %get-tuple-element.67, f32[256]{0:T(256)S(1)} %add_rsqrt_fusion.5, f32[2560]{0:T(1024)S(1)} %copy-done.52), kind=kOutput, calls=%fused_computation.54 | convolution fusion | flops 13866848256 | bytes 62196736 | tf_op jit(solution)/shard_map/in1_2/dot_general | solution.py:283
  548.3 6.0 conv_pack.13
  556.0 4.7 all-to-all-start.8
  560.7 14.7 %multiply_reduce_fusion = (f32[256]{0:T(256)S(1)}, f32[256,2560]{1,0:T(8,128)}) fusion(f32[256,2560]{1,0:T(8,128)} %bitcast.166, bf16[256,5120]{1,0:T(8,128)(2,1)} %copy-done.36, bf16[2,5120,2560]{2,1,0:T(8,128)(2,1)} %param.19), kind=kOutput, calls=%fused_computation.66 | convolution fusion | flops 6712852480 | bytes 34079744 | tf_op jit(solution)/shard_map/out0_3/dot_general | solution.py:298
  575.4 6.0 conv_pack.14
  583.2 16.6 %all-to-all-done.8.x_ref.dt_ref = bf16[8,1568,128]{2,1,0:T(8,128)(2,1)} async-done(((bf16[8,1568,128]{2,1,0:T(8,128)(2,1)}), bf16[8,1568,128]{2,1,0:T(8,128)(2,1)}, u32[]{:S(2)}, u32[]{:S(2)}) %all-to-all-start.8) | async-done | bytes 3211296 | tf_op jit(solution)/shard_map/go1_1/all_to_all | solution.py:289
  599.7 3.9 all-to-all-start.11
  603.6 24.8 %fusion.69.x_ref.bc_ref.dtr_ref.z_ref = bf16[256,10576]{1,0:T(8,128)(2,1)} fusion(bf16[2,2560,10576]{1,2,0:T(8,128)(2,1)} %param.12, f32[256,2560]{1,0:T(8,128)} %get-tuple-element.65, f32[256]{0:T(256)S(1)} %add_rsqrt_fusion.4, f32[2560]{0:T(1024)S(1)} %copy-done.52), kind=kOutput, calls=%fused_computation.55 | convolution fusion | flops 13866848256 | bytes 62196736 | tf_op jit(solution)/shard_map/in1_3/dot_general | solution.py:283
  635.2 5.3 conv_pack.15
  642.8 12.8 %all-to-all-start.14 = ((bf16[8,1568,128]{2,1,0:T(8,128)(2,1)}), bf16[8,1568,128]{2,1,0:T(8,128)(2,1)}, u32[]{:S(2)}, u32[]{:S(2)}) async-start(bf16[8,1568,128]{2,1,0:T(8,128)(2,1)} %copy-done.17), calls=%async_computation.14 | async-start | bytes 6422528 | tf_op jit(solution)/shard_map/go1_3/all_to_all | solution.py:289
  662.6 25.4 %scan.12 = (bf16[8,1280,128]{2,1,0:T(8,128)(2,1)S(1)}, f32[16,2,10,64,128]{4,3,2,1,0:T(8,128)}) custom-call(s32[1]{0:T(128)} %bitcast.1.par_ref, bf16[8,1568,128]{2,1,0:T(8,128)(2,1)S(1)} %copy-done.15, bf16[8,256,128]{2,1,0:T(8,128)(2,1)} %collective-permute-done.3.other_ref, bf16[8,1568,128]{2,1,0:T(8,128)(2,1)S(1)} %copy-done.15, ...), custom_call_target="tpu_custom_call", output_to_operand_aliasing={{1}: (6, {})} | custom-call | flops 327680000 | bytes 7864320 | tf_op jit(solution)/shard_map/scan1_0/scan/pallas_call | solution.py:187
  689.5 5.2 all-to-all-done.14.x_ref.dt_ref
  694.8 4.7 all-to-all-start.6
  714.0 59.4 %all-reduce.5.cloned.1.call-done = bf16[16,2,5376,3]{2,3,0,1:T(4,128)(2,1)} async-done(((bf16[16,2,5376,3]{2,3,0,1:T(4,128)(2,1)}), bf16[16,2,5376,3]{2,3,0,1:T(4,128)(2,1)}) %all-reduce.5.cloned.1.call-update) | async-done | bytes 1032208 | tf_op jit(solution)/shard_map/psum | solution.py:302
  773.4 3.5 copy.28
  777.0 25.5 %scan.13 = (bf16[8,1280,128]{2,1,0:T(8,128)(2,1)S(1)}, f32[16,2,10,64,128]{4,3,2,1,0:T(8,128)}) custom-call(s32[1]{0:T(128)} %bitcast.1.par_ref, bf16[8,1568,128]{2,1,0:T(8,128)(2,1)} %all-to-all-done.8.x_ref.dt_ref, bf16[8,256,128]{2,1,0:T(8,128)(2,1)} %collective-permute-done.11.other_ref, ...), custom_call_target="tpu_custom_call", output_to_operand_aliasing={{1}: (6, {})} | custom-call | flops 327680000 | bytes 7864320 | tf_op jit(solution)/shard_map/scan1_1/scan/pallas_call | solution.py:187
  802.5 25.8 %scan.14 = (bf16[8,1280,128]{2,1,0:T(8,128)(2,1)S(1)}, f32[16,2,10,64,128]{4,3,2,1,0:T(8,128)}) custom-call(s32[1]{0:T(128)} %bitcast.1.par_ref, bf16[8,1568,128]{2,1,0:T(8,128)(2,1)S(1)} %all-to-all-done.11.x_ref.dt_ref, bf16[8,256,128]{2,1,0:T(8,128)(2,1)} %collective-permute-done.13.other_ref, ...), custom_call_target="tpu_custom_call", output_to_operand_aliasing={{1}: (6, {})} | custom-call | flops 327680000 | bytes 7864320 | tf_op jit(solution)/shard_map/scan1_2/scan/pallas_call | solution.py:187
  829.8 25.7 %scan.15 = (bf16[8,1280,128]{2,1,0:T(8,128)(2,1)S(1)}, f32[16,2,10,64,128]{4,3,2,1,0:T(8,128)}) custom-call(s32[1]{0:T(128)} %bitcast.1.par_ref, bf16[8,1568,128]{2,1,0:T(8,128)(2,1)} %all-to-all-done.14.x_ref.dt_ref, bf16[8,256,128]{2,1,0:T(8,128)(2,1)} %collective-permute-done.15.other_ref, ...), custom_call_target="tpu_custom_call", output_to_operand_aliasing={{1}: (6, {})} | custom-call | flops 327680000 | bytes 7864320 | tf_op jit(solution)/shard_map/scan1_3/scan/pallas_call | solution.py:187
  857.0 3.8 all-to-all-start.9
  863.4 4.0 gate.9
  867.4 13.9 %fusion.84 = f32[256,2560]{1,0:T(8,128)} fusion(f32[256,2560]{1,0:T(8,128)} %copy-done.58, bf16[256,5120]{1,0:T(8,128)(2,1)S(1)} %gate.9, bf16[2,5120,2560]{2,1,0:T(8,128)(2,1)} %param.19), kind=kOutput, calls=%fused_computation.61 | convolution fusion | flops 6711541760 | bytes 34078720 | tf_op jit(solution)/shard_map/out1_0/dot_general | solution.py:298
  881.2 12.2 %all-to-all-done.9.y_ref = bf16[8,1280,128]{2,1,0:T(8,128)(2,1)S(1)} async-done(((bf16[8,1280,128]{2,1,0:T(8,128)(2,1)}), bf16[8,1280,128]{2,1,0:T(8,128)(2,1)S(1)}, u32[]{:S(2)}, u32[]{:S(2)}) %all-to-all-start.9) | async-done | bytes 2621472 | tf_op jit(solution)/shard_map/back1_1/all_to_all | solution.py:295
  893.4 4.8 all-to-all-start.12
  903.5 13.9 %fusion.87 = f32[256,2560]{1,0:T(8,128)} fusion(f32[256,2560]{1,0:T(8,128)} %get-tuple-element.69, bf16[256,5120]{1,0:T(8,128)(2,1)S(1)} %gate.11, bf16[2,5120,2560]{2,1,0:T(8,128)(2,1)} %param.19), kind=kOutput, calls=%fused_computation.62 | convolution fusion | flops 6711541760 | bytes 34078720 | tf_op jit(solution)/shard_map/out1_1/dot_general | solution.py:298
  917.3 13.5 %all-to-all-done.12.y_ref = bf16[8,1280,128]{2,1,0:T(8,128)(2,1)} async-done(((bf16[8,1280,128]{2,1,0:T(8,128)(2,1)}), bf16[8,1280,128]{2,1,0:T(8,128)(2,1)}, u32[]{:S(2)}, u32[]{:S(2)}) %all-to-all-start.12) | async-done | bytes 2621472 | tf_op jit(solution)/shard_map/back1_2/all_to_all | solution.py:295
  930.9 3.8 all-to-all-start.15
  937.2 4.0 gate.13
  941.2 13.9 %fusion.90 = f32[256,2560]{1,0:T(8,128)} fusion(f32[256,2560]{1,0:T(8,128)} %get-tuple-element.67, bf16[256,5120]{1,0:T(8,128)(2,1)S(1)} %gate.13, bf16[2,5120,2560]{2,1,0:T(8,128)(2,1)} %param.19), kind=kOutput, calls=%fused_computation.63 | convolution fusion | flops 6711541760 | bytes 34078720 | tf_op jit(solution)/shard_map/out1_2/dot_general | solution.py:298
  955.2 12.1 %all-to-all-done.15.y_ref = bf16[8,1280,128]{2,1,0:T(8,128)(2,1)S(1)} async-done(((bf16[8,1280,128]{2,1,0:T(8,128)(2,1)}), bf16[8,1280,128]{2,1,0:T(8,128)(2,1)S(1)}, u32[]{:S(2)}, u32[]{:S(2)}) %all-to-all-start.15) | async-done | bytes 2621472 | tf_op jit(solution)/shard_map/back1_3/all_to_all | solution.py:295
  972.5 14.0 %fusion.93 = f32[256,2560]{1,0:T(8,128)} fusion(f32[256,2560]{1,0:T(8,128)} %get-tuple-element.65, bf16[256,5120]{1,0:T(8,128)(2,1)S(1)} %gate.15, bf16[2,5120,2560]{2,1,0:T(8,128)(2,1)} %param.19), kind=kOutput, calls=%fused_computation.64 | convolution fusion | flops 6711541760 | bytes 34078720 | tf_op jit(solution)/shard_map/out1_3/dot_general | solution.py:298
  986.5 6.5 pad_maximum_fusion
  (227 shorter events, 153.1 us)
Async XLA Ops:
  7.2 5.0 copy-start.51
  7.2 7.0 copy-start.38
  20.2 26.6 %copy-start.48 = (f32[2,5376,4]{1,2,0:T(4,128)S(1)}, f32[2,5376,4]{1,2,0:T(4,128)}, u32[]{:S(2)}) copy-start(f32[2,5376,4]{1,2,0:T(4,128)} %param.13) | copy-start | bytes 516100
  20.2 26.6 %copy-start.49 = (f32[2,5376]{1,0:T(2,128)S(1)}, f32[2,5376]{1,0:T(2,128)}, u32[]{:S(2)}) copy-start(f32[2,5376]{1,0:T(2,128)} %param.14) | copy-start | bytes 129028
  20.2 26.8 %copy-start.54 = (f32[2,80]{1,0:T(2,128)S(1)}, f32[2,80]{1,0:T(2,128)}, u32[]{:S(2)}) copy-start(f32[2,80]{1,0:T(2,128)} %param.15) | copy-start | bytes 1924
  45.0 2.8 copy-start.42
  45.0 2.8 collective-permute-start
  47.8 2.5 copy-start.8
  57.1 48.8 %all-to-all-start = ((bf16[8,1568,128]{2,1,0:T(8,128)(2,1)}), bf16[8,1568,128]{2,1,0:T(8,128)(2,1)S(1)}, u32[]{:S(2)}, u32[]{:S(2)}) async-start(bf16[8,1568,128]{2,1,0:T(8,128)(2,1)} %copy-done.23), calls=%async_computation | async-start | bytes 6422528 | tf_op jit(solution)/shard_map/go0_0/all_to_all | solution.py:289
  91.5 3.5 collective-permute-start.8
  95.0 2.5 copy-start.10
  105.9 52.2 %all-to-all-start.5 = ((bf16[8,1568,128]{2,1,0:T(8,128)(2,1)}), bf16[8,1568,128]{2,1,0:T(8,128)(2,1)}, u32[]{:S(2)}, u32[]{:S(2)}) async-start(bf16[8,1568,128]{2,1,0:T(8,128)(2,1)} %copy-done.22), calls=%async_computation.5 | async-start | bytes 6422528 | tf_op jit(solution)/shard_map/go0_1/all_to_all | solution.py:289
  143.8 3.5 collective-permute-start.6
  158.0 51.9 %all-to-all-start.4 = ((bf16[8,1568,128]{2,1,0:T(8,128)(2,1)}), bf16[8,1568,128]{2,1,0:T(8,128)(2,1)}, u32[]{:S(2)}, u32[]{:S(2)}) async-start(bf16[8,1568,128]{2,1,0:T(8,128)(2,1)} %copy-done.20), calls=%async_computation.4 | async-start | bytes 6422528 | tf_op jit(solution)/shard_map/go0_2/all_to_all | solution.py:289
  195.6 3.5 collective-permute-start.4
  210.0 51.9 %all-to-all-start.3 = ((bf16[8,1568,128]{2,1,0:T(8,128)(2,1)}), bf16[8,1568,128]{2,1,0:T(8,128)(2,1)}, u32[]{:S(2)}, u32[]{:S(2)}) async-start(bf16[8,1568,128]{2,1,0:T(8,128)(2,1)} %copy-done.16), calls=%async_computation.3 | async-start | bytes 6422528 | tf_op jit(solution)/shard_map/go0_3/all_to_all | solution.py:289
  224.0 2.0 collective-permute-start.1
  261.9 93.3 %all-to-all-start.1 = ((bf16[8,1280,128]{2,1,0:T(8,128)(2,1)}), bf16[8,1280,128]{2,1,0:T(8,128)(2,1)S(1)}, u32[]{:S(2)}, u32[]{:S(2)}) async-start(bf16[8,1280,128]{2,1,0:T(8,128)(2,1)} %copy-done.31), calls=%async_computation.1 | async-start | bytes 5242880 | tf_op jit(solution)/shard_map/back0_0/all_to_all | solution.py:295
  268.4 5.4 collective-permute-start.9
  271.0 2.8 copy-start.50
  271.0 29.8 %collective-permute-start.7 = (bf16[8,256,128]{2,1,0:T(8,128)(2,1)S(1)}, bf16[8,256,128]{2,1,0:T(8,128)(2,1)S(1)}, u32[]{:S(2)}, u32[]{:S(2)}) collective-permute-start(bf16[8,256,128]{2,1,0:T(8,128)(2,1)S(1)} %bitcast.175), channel_id=1, source_target_pairs={{0,1},{1,0},{2,3},{3,2},{4,5},{5,4},{6,7},{7,6},{8,9},{9,8},{10,11... | collective-permute-start | bytes 1572872 | tf_op jit(solution)/shard_map/scan0_2/ppermute | solution.py:292
  273.4 54.6 %collective-permute-start.5 = (bf16[8,256,128]{2,1,0:T(8,128)(2,1)S(1)}, bf16[8,256,128]{2,1,0:T(8,128)(2,1)S(1)}, u32[]{:S(2)}, u32[]{:S(2)}) collective-permute-start(bf16[8,256,128]{2,1,0:T(8,128)(2,1)S(1)} %bitcast.174), channel_id=1, source_target_pairs={{0,1},{1,0},{2,3},{3,2},{4,5},{5,4},{6,7},{7,6},{8,9},{9,8},{10,11... | collective-permute-start | bytes 1572872 | tf_op jit(solution)/shard_map/scan0_3/ppermute | solution.py:292
  355.2 49.9 %all-to-all-start.7 = ((bf16[8,1280,128]{2,1,0:T(8,128)(2,1)}), bf16[8,1280,128]{2,1,0:T(8,128)(2,1)}, u32[]{:S(2)}, u32[]{:S(2)}) async-start(bf16[8,1280,128]{2,1,0:T(8,128)(2,1)} %copy-done.33), calls=%async_computation.7 | async-start | bytes 5242880 | tf_op jit(solution)/shard_map/back0_1/all_to_all | solution.py:295
  360.1 2.5 copy-start.9
  365.3 12.9 %copy-start.52 = (f32[2560]{0:T(1024)S(1)}, f32[2560]{0:T(1024)}, u32[]{:S(2)}) copy-start(f32[2560]{0:T(1024)} %get-tuple-element.42) | copy-start | bytes 30724
  378.2 25.2 %copy-start.58 = (f32[256,2560]{1,0:T(8,128)}, f32[256,2560]{1,0:T(8,128)S(1)}, u32[]{:S(2)}) copy-start(f32[256,2560]{1,0:T(8,128)S(1)} %get-tuple-element.71) | copy-start | bytes 7864324
  405.1 59.1 %all-to-all-start.10 = ((bf16[8,1280,128]{2,1,0:T(8,128)(2,1)}), bf16[8,1280,128]{2,1,0:T(8,128)(2,1)S(1)}, u32[]{:S(2)}, u32[]{:S(2)}) async-start(bf16[8,1280,128]{2,1,0:T(8,128)(2,1)} %copy-done.30), calls=%async_computation.10 | async-start | bytes 5242880 | tf_op jit(solution)/shard_map/back0_2/all_to_all | solution.py:295
  410.5 2.5 copy-start.11
  457.5 35.3 %collective-permute-start.2 = (bf16[4,3,5376]{2,1,0:T(4,128)(2,1)}, bf16[4,3,5376]{2,1,0:T(4,128)(2,1)}, u32[]{:S(2)}, u32[]{:S(2)}) collective-permute-start(bf16[4,3,5376]{2,1,0:T(4,128)(2,1)} %slice.230), channel_id=1, source_target_pairs={{0,1},{1,2},{2,3},{3,4},{4,5},{5,6},{6,7},{8,9},{9,10},{10,11},{11... | collective-permute-start | bytes 387080 | tf_op jit(solution)/shard_map/in1_0/ppermute | solution.py:285
  460.6 85.1 %collective-permute-start.10 = (bf16[4,3,5376]{2,1,0:T(4,128)(2,1)}, bf16[4,3,5376]{2,1,0:T(4,128)(2,1)}, u32[]{:S(2)}, u32[]{:S(2)}) collective-permute-start(bf16[4,3,5376]{2,1,0:T(4,128)(2,1)} %slice.243), channel_id=1, source_target_pairs={{0,1},{1,2},{2,3},{3,4},{4,5},{5,6},{6,7},{8,9},{9,10},{10,11},{11... | collective-permute-start | bytes 387080 | tf_op jit(solution)/shard_map/in1_1/ppermute | solution.py:285
  465.7 36.4 %all-to-all-start.13 = ((bf16[8,1280,128]{2,1,0:T(8,128)(2,1)}), bf16[8,1280,128]{2,1,0:T(8,128)(2,1)S(1)}, u32[]{:S(2)}, u32[]{:S(2)}) async-start(bf16[8,1280,128]{2,1,0:T(8,128)(2,1)} %copy-done.29), calls=%async_computation.13 | async-start | bytes 5242880 | tf_op jit(solution)/shard_map/back0_3/all_to_all | solution.py:295
  469.6 2.5 copy-start.6
  478.1 14.7 %slice-start = ((s8[5439488]{0:T(1024)(128)(4,1)}), s8[4194304]{0:T(1024)(128)(4,1)S(1)}, s32[]{:S(2)}) async-start(s8[5439488]{0:T(1024)(128)(4,1)} %bitcast.146), calls=%async_computation.17 | async-start | bytes 8388608
  478.1 14.7 %slice-start.1 = ((s8[5439488]{0:T(1024)(128)(4,1)}), s8[1245184]{0:T(1024)(128)(4,1)S(1)}, s32[]{:S(2)}) async-start(s8[5439488]{0:T(1024)(128)(4,1)} %bitcast.146), calls=%async_computation.18 | async-start | bytes 2490368
  503.7 52.3 %all-to-all-start.2 = ((bf16[8,1568,128]{2,1,0:T(8,128)(2,1)}), bf16[8,1568,128]{2,1,0:T(8,128)(2,1)S(1)}, u32[]{:S(2)}, u32[]{:S(2)}) async-start(bf16[8,1568,128]{2,1,0:T(8,128)(2,1)} %copy-done.19), calls=%async_computation.2 | async-start | bytes 6422528 | tf_op jit(solution)/shard_map/go1_0/all_to_all | solution.py:289
  534.3 41.1 %collective-permute-start.12 = (bf16[4,3,5376]{2,1,0:T(4,128)(2,1)}, bf16[4,3,5376]{2,1,0:T(4,128)(2,1)}, u32[]{:S(2)}, u32[]{:S(2)}) collective-permute-start(bf16[4,3,5376]{2,1,0:T(4,128)(2,1)} %slice.246), channel_id=1, source_target_pairs={{0,1},{1,2},{2,3},{3,4},{4,5},{5,6},{6,7},{8,9},{9,10},{10,11},{11... | collective-permute-start | bytes 387080 | tf_op jit(solution)/shard_map/in1_2/ppermute | solution.py:285
  545.7 2.5 copy-start.1
  556.0 4.7 copy-start.14
  556.0 43.7 %all-to-all-start.8 = ((bf16[8,1568,128]{2,1,0:T(8,128)(2,1)}), bf16[8,1568,128]{2,1,0:T(8,128)(2,1)}, u32[]{:S(2)}, u32[]{:S(2)}) async-start(bf16[8,1568,128]{2,1,0:T(8,128)(2,1)} %copy-done.21), calls=%async_computation.8 | async-start | bytes 6422528 | tf_op jit(solution)/shard_map/go1_1/all_to_all | solution.py:289
  560.7 14.7 %slice-start.2 = ((s8[5439488]{0:T(1024)(128)(4,1)}), s8[4194304]{0:T(1024)(128)(4,1)S(1)}, s32[]{:S(2)}) async-start(s8[5439488]{0:T(1024)(128)(4,1)} %bitcast.152), calls=%async_computation.19 | async-start | bytes 8388608
  560.7 14.7 %slice-start.3 = ((s8[5439488]{0:T(1024)(128)(4,1)}), s8[1245184]{0:T(1024)(128)(4,1)S(1)}, s32[]{:S(2)}) async-start(s8[5439488]{0:T(1024)(128)(4,1)} %bitcast.152), calls=%async_computation.20 | async-start | bytes 2490368
  599.7 43.1 %all-to-all-start.11 = ((bf16[8,1568,128]{2,1,0:T(8,128)(2,1)}), bf16[8,1568,128]{2,1,0:T(8,128)(2,1)S(1)}, u32[]{:S(2)}, u32[]{:S(2)}) async-start(bf16[8,1568,128]{2,1,0:T(8,128)(2,1)} %copy-done.18), calls=%async_computation.11 | async-start | bytes 6422528 | tf_op jit(solution)/shard_map/go1_2/all_to_all | solution.py:289
  629.5 3.1 collective-permute-start.14
  642.8 51.9 %all-to-all-start.14 = ((bf16[8,1568,128]{2,1,0:T(8,128)(2,1)}), bf16[8,1568,128]{2,1,0:T(8,128)(2,1)}, u32[]{:S(2)}, u32[]{:S(2)}) async-start(bf16[8,1568,128]{2,1,0:T(8,128)(2,1)} %copy-done.17), calls=%async_computation.14 | async-start | bytes 6422528 | tf_op jit(solution)/shard_map/go1_3/all_to_all | solution.py:289
  655.6 3.5 copy-start.53
  655.6 3.6 copy-start.57
  658.6 2.0 collective-permute-start.3
  694.8 5.2 copy-start.43
  694.8 162.2 %all-to-all-start.6 = ((bf16[8,1280,128]{2,1,0:T(8,128)(2,1)}), bf16[8,1280,128]{2,1,0:T(8,128)(2,1)}, u32[]{:S(2)}, u32[]{:S(2)}) async-start(bf16[8,1280,128]{2,1,0:T(8,128)(2,1)} %copy-done.28), calls=%async_computation.6 | async-start | bytes 5242880 | tf_op jit(solution)/shard_map/back1_0/all_to_all | solution.py:295
  699.5 74.0 %all-reduce.5.cloned.1.call-start = ((), (), s32[]{:S(2)}) async-start(), calls=%async_computation.16 | async-start | bytes 2752512 | tf_op jit(solution)/shard_map/psum | solution.py:302
  704.1 3.2 copy-start.39
  707.1 69.9 %collective-permute-start.11 = (bf16[8,256,128]{2,1,0:T(8,128)(2,1)}, bf16[8,256,128]{2,1,0:T(8,128)(2,1)}, u32[]{:S(2)}, u32[]{:S(2)}) collective-permute-start(bf16[8,256,128]{2,1,0:T(8,128)(2,1)} %bitcast.37), channel_id=1, source_target_pairs={{0,1},{1,0},{2,3},{3,2},{4,5},{5,4},{6,7},{7,6},{8,9},{9,8},{10,11... | collective-permute-start | bytes 1572872 | tf_op jit(solution)/shard_map/scan1_1/ppermute | solution.py:292
  710.6 91.9 %collective-permute-start.13 = (bf16[8,256,128]{2,1,0:T(8,128)(2,1)}, bf16[8,256,128]{2,1,0:T(8,128)(2,1)}, u32[]{:S(2)}, u32[]{:S(2)}) collective-permute-start(bf16[8,256,128]{2,1,0:T(8,128)(2,1)} %bitcast.41), channel_id=1, source_target_pairs={{0,1},{1,0},{2,3},{3,2},{4,5},{5,4},{6,7},{7,6},{8,9},{9,8},{10,11... | collective-permute-start | bytes 1572872 | tf_op jit(solution)/shard_map/scan1_2/ppermute | solution.py:292
  713.9 115.9 %collective-permute-start.15 = (bf16[8,256,128]{2,1,0:T(8,128)(2,1)}, bf16[8,256,128]{2,1,0:T(8,128)(2,1)}, u32[]{:S(2)}, u32[]{:S(2)}) collective-permute-start(bf16[8,256,128]{2,1,0:T(8,128)(2,1)} %bitcast.45), channel_id=1, source_target_pairs={{0,1},{1,0},{2,3},{3,2},{4,5},{5,4},{6,7},{7,6},{8,9},{9,8},{10,11... | collective-permute-start | bytes 1572872 | tf_op jit(solution)/shard_map/scan1_3/ppermute | solution.py:292
  802.5 25.8 %copy-start.35 = (bf16[8,1280,128]{2,1,0:T(8,128)(2,1)}, bf16[8,1280,128]{2,1,0:T(8,128)(2,1)S(1)}, u32[]{:S(2)}) copy-start(bf16[8,1280,128]{2,1,0:T(8,128)(2,1)S(1)} %get-tuple-element.27) | copy-start | bytes 7864324
  857.0 36.4 %all-to-all-start.9 = ((bf16[8,1280,128]{2,1,0:T(8,128)(2,1)}), bf16[8,1280,128]{2,1,0:T(8,128)(2,1)S(1)}, u32[]{:S(2)}, u32[]{:S(2)}) async-start(bf16[8,1280,128]{2,1,0:T(8,128)(2,1)} %copy-done.35), calls=%async_computation.9 | async-start | bytes 5242880 | tf_op jit(solution)/shard_map/back1_1/all_to_all | solution.py:295
  860.8 2.5 copy-start
  893.4 37.4 %all-to-all-start.12 = ((bf16[8,1280,128]{2,1,0:T(8,128)(2,1)}), bf16[8,1280,128]{2,1,0:T(8,128)(2,1)}, u32[]{:S(2)}, u32[]{:S(2)}) async-start(bf16[8,1280,128]{2,1,0:T(8,128)(2,1)} %copy-done.34), calls=%async_computation.12 | async-start | bytes 5242880 | tf_op jit(solution)/shard_map/back1_2/all_to_all | solution.py:295
  898.3 2.5 copy-start.2
  930.9 36.4 %all-to-all-start.15 = ((bf16[8,1280,128]{2,1,0:T(8,128)(2,1)}), bf16[8,1280,128]{2,1,0:T(8,128)(2,1)S(1)}, u32[]{:S(2)}, u32[]{:S(2)}) async-start(bf16[8,1280,128]{2,1,0:T(8,128)(2,1)} %copy-done.32), calls=%async_computation.15 | async-start | bytes 5242880 | tf_op jit(solution)/shard_map/back1_3/all_to_all | solution.py:295
  934.7 2.5 copy-start.7
  967.3 2.5 copy-start.13
  972.5 14.0 %copy-start.40 = (f32[256,2560]{1,0:T(8,128)S(1)}, f32[256,2560]{1,0:T(8,128)}, u32[]{:S(2)}) copy-start(f32[256,2560]{1,0:T(8,128)} %fusion.84) | copy-start | bytes 7864324
  972.5 14.0 %copy-start.41 = (f32[256,2560]{1,0:T(8,128)S(1)}, f32[256,2560]{1,0:T(8,128)}, u32[]{:S(2)}) copy-start(f32[256,2560]{1,0:T(8,128)} %fusion.87) | copy-start | bytes 7864324
  (32 other events, 59.1 us)
Sparse Core Ops, SparseCore 0:
  709.7 63.7 all-reduce.4

commit v2 on v1

v2 whole, which is shorter than its diff:
```python
import functools

import jax
import jax.numpy as jnp
from jax import lax
from jax.experimental import pallas as pl
from jax.experimental.pallas import tpu as pltpu
from jax.sharding import PartitionSpec as P


CONV_WIDTH = 4
EPSILON = 1e-5
LANES = 128
SIZES = (8, 8)


def conv_kernel(n_prompts, seg_len, width, n_heads, x_ref, bc_ref, dtr_ref, xh_ref, bch_ref, wx_ref, wbc_ref, bx_ref, bbc_ref, dtb_ref, sel_ref, out_ref, bc_keep, dt_keep):
    dest = pl.program_id(0)
    taps = CONV_WIDTH - 1
    blocks = width // LANES

    def conv(cur, halo, w, bias):
        cur = cur.astype(jnp.float32)
        halo = halo.astype(jnp.float32)
        acc = bias + cur * w[taps:taps + 1]
        for back in range(1, CONV_WIDTH):
            shifted = jnp.concatenate([halo[taps - back:], cur[:seg_len - back]], axis=0)
            acc = acc + shifted * w[taps - back:taps - back + 1]
        return (acc * jax.nn.sigmoid(acc)).astype(jnp.bfloat16)

    @pl.when(dest == 0)
    def _():
        raw = dtr_ref[...].astype(jnp.float32)
        column = lax.broadcasted_iota(jnp.int32, raw.shape, 1)
        delta = jax.nn.softplus(raw + dtb_ref[...])
        delta = jnp.where(column < n_heads, delta, 0.0).astype(jnp.bfloat16)
        rows = lax.dot_general(sel_ref[...], delta, (((1,), (1,)), ((), ())), preferred_element_type=jnp.float32)
        rows = rows.astype(jnp.bfloat16)
        for d in range(dt_keep.shape[0]):
            for part in range(dt_keep.shape[1] // 16):
                dt_keep[d, part * 16:(part + 1) * 16] = rows[d * 16:(d + 1) * 16, part * LANES:(part + 1) * LANES]

    @pl.when(dest < 2)
    def _():
        for p in range(n_prompts):
            bc_keep[dest, p] = conv(bc_ref[p * seg_len:(p + 1) * seg_len], bch_ref[:, p], wbc_ref[...], bbc_ref[...])

    parity = lax.rem(dest, 2)
    per_prompt = blocks * seg_len
    bc_start = n_prompts * per_prompt
    for p in range(n_prompts):
        for j in range(blocks):
            cols = slice(j * LANES, (j + 1) * LANES)
            out_ref[0, p * per_prompt + j * seg_len:p * per_prompt + (j + 1) * seg_len] = conv(
                x_ref[p * seg_len:(p + 1) * seg_len, cols], xh_ref[:, p, cols], wx_ref[:, cols], bx_ref[:, cols])
        out_ref[0, bc_start + p * seg_len:bc_start + (p + 1) * seg_len] = bc_keep[parity, p]
    out_ref[0, bc_start + n_prompts * seg_len:] = dt_keep[dest]


def tail_kernel(n_prompts, seg_len, u_ref, out_ref):
    taps = CONV_WIDTH - 1
    for k in range(taps):
        rows = [u_ref[(p + 1) * seg_len - 16:(p + 1) * seg_len].astype(jnp.float32)[16 - taps + k:17 - taps + k] for p in range(n_prompts)]
        out_ref[k] = jnp.concatenate(rows, axis=0).astype(jnp.bfloat16)


def tail_call(u, n_prompts, seg_len, conv_dim):
    taps = CONV_WIDTH - 1
    width = 6 * LANES
    return pl.pallas_call(
        functools.partial(tail_kernel, n_prompts, seg_len),
        grid=(conv_dim // width,),
        in_specs=[pl.BlockSpec((n_prompts * seg_len, width), lambda i: (0, i))],
        out_specs=pl.BlockSpec((taps, n_prompts, width), lambda i: (0, 0, i)),
        out_shape=jax.ShapeDtypeStruct((taps, n_prompts, conv_dim), jnp.bfloat16),
        cost_estimate=pl.CostEstimate(flops=n_prompts * conv_dim * 100, bytes_accessed=2 * n_prompts * seg_len * conv_dim, transcendentals=0),
        name='tail',
    )(u)


def conv_call(u, halo, conv_w, conv_b, dt_b, select, sizes):
    n_prompts, seg_len, d_inner, conv_dim, n_heads, n_dest = sizes
    width = d_inner // n_dest
    blocks = width // LANES
    dt_rows = n_prompts * seg_len // LANES * 16
    rows = n_prompts * (blocks + 1) * seg_len + dt_rows
    tokens = n_prompts * seg_len
    bc0 = d_inner // LANES
    dt0 = conv_dim // LANES
    taps = CONV_WIDTH - 1
    body = functools.partial(conv_kernel, n_prompts, seg_len, width, n_heads)
    parity = lambda d: lax.rem(d, 2)
    return pl.pallas_call(
        body,
        grid=(n_dest,),
        in_specs=[
            pl.BlockSpec((tokens, width), lambda d: (0, d)),
            pl.BlockSpec((tokens, LANES), lambda d: (0, bc0 + parity(d))),
            pl.BlockSpec((tokens, LANES), lambda d: (0, dt0)),
            pl.BlockSpec((taps, n_prompts, width), lambda d: (0, 0, d)),
            pl.BlockSpec((taps, n_prompts, LANES), lambda d: (0, 0, d_inner // LANES + parity(d))),
            pl.BlockSpec((CONV_WIDTH, width), lambda d: (0, d)),
            pl.BlockSpec((CONV_WIDTH, LANES), lambda d: (0, d_inner // LANES + parity(d))),
            pl.BlockSpec((1, width), lambda d: (0, d)),
            pl.BlockSpec((1, LANES), lambda d: (0, d_inner // LANES + parity(d))),
            pl.BlockSpec((1, LANES), lambda d: (0, 0)),
            pl.BlockSpec((n_dest * 16, LANES), lambda d: (0, 0)),
        ],
        out_specs=pl.BlockSpec((1, rows, LANES), lambda d: (d, 0, 0)),
        out_shape=jax.ShapeDtypeStruct((n_dest, rows, LANES), jnp.bfloat16),
        scratch_shapes=[
            pltpu.VMEM((2, n_prompts, seg_len, LANES), jnp.bfloat16),
            pltpu.VMEM((n_dest, dt_rows, LANES), jnp.bfloat16),
        ],
        cost_estimate=pl.CostEstimate(flops=tokens * d_inner * 60, bytes_accessed=4 * tokens * d_inner, transcendentals=tokens * d_inner),
        name='conv_pack',
    )(u, u, u, halo, halo, conv_w, conv_w, conv_b, conv_b, dt_b, select)


def scan_kernel(seg_count, seg_len, blocks, n_local, head_dim, par_ref, x_ref, mine_ref, other_ref, dt_ref, a_ref, d_ref, *rest):
    y_ref, fin_ref, state = rest[-3:]
    tokens = LANES
    per_chunk = tokens // seg_len
    n_chunks = seg_count // per_chunk
    pairs = LANES // head_dim
    even = par_ref[0] == 0
    half = lax.rem(pl.program_id(0), 2)
    row = lax.broadcasted_iota(jnp.int32, (tokens, tokens), 0)
    col = lax.broadcasted_iota(jnp.int32, (tokens, tokens), 1)
    causal = row >= col
    first = col < head_dim

    left = lax.broadcasted_iota(jnp.int32, (16, tokens), 1) < seg_len
    dts = []
    for chunk in range(n_chunks):
        lo = dt_ref[per_chunk * chunk].astype(jnp.float32)
        hi = dt_ref[per_chunk * chunk + 1].astype(jnp.float32)
        lo = jnp.where(half == 0, lo, pltpu.roll(lo, seg_len, 1))
        hi = jnp.where(half == 0, pltpu.roll(hi, seg_len, 1), hi)
        dts.append(jnp.where(left, lo, hi))
    dt = jnp.concatenate(dts, axis=0)
    lane = lax.broadcasted_iota(jnp.int32, dt.shape, 1)
    cum = dt * jnp.concatenate([a_ref[...]] * n_chunks, axis=0)
    step = 1
    while step < tokens:
        cum = cum + jnp.where(lane >= step, pltpu.roll(cum, step, 1), 0.0)
        step *= 2
    last = cum[:, tokens - 1:]
    weight = jnp.exp(last - cum) * dt
    last_e = jnp.exp(last)
    cum_c = jnp.transpose(cum)

    state[...] = jnp.zeros_like(state)
    for chunk in range(n_chunks):
        segs = range(chunk * per_chunk, (chunk + 1) * per_chunk)
        tok = lambda ref, lo: jnp.concatenate([ref[s, lo:lo + seg_len] for s in segs], axis=0)
        mine = tok(mine_ref, 0)
        other = tok(other_ref, 0)
        b_mat = jnp.where(even, mine, other)
        c_mat = jnp.where(even, other, mine)
        scores = lax.dot_general(c_mat, b_mat, (((1,), (1,)), ((), ())), preferred_element_type=jnp.float32)
        if chunk:
            carried = lax.dot_general(c_mat, state[...].astype(jnp.bfloat16), (((1,), (1,)), ((), ())), preferred_element_type=jnp.float32)
        scaled = []
        for j in range(blocks):
            rows = [chunk * 16 + j * pairs + k for k in range(pairs)]
            mixes = []
            starts = []
            for h in rows:
                start = jnp.broadcast_to(cum_c[:, h:h + 1], (tokens, tokens))
                diff = jnp.where(causal, start - cum[h:h + 1, :], -jnp.inf)
                mixes.append((jnp.exp(diff) * (scores * dt[h:h + 1, :])).astype(jnp.bfloat16))
                starts.append(start)
            x2 = tok(x_ref, j * seg_len)
            zero = jnp.zeros_like(x2)
            stacked = jnp.concatenate([jnp.where(first, x2, zero), jnp.where(first, zero, x2)], axis=0)
            y = jnp.dot(jnp.concatenate(mixes, axis=1), stacked, preferred_element_type=jnp.float32)
            x_float = x2.astype(jnp.float32)
            y = y + d_ref[:, j * LANES:(j + 1) * LANES] * x_float
            if chunk:
                y = y + carried[:, j * LANES:(j + 1) * LANES] * jnp.exp(jnp.where(first, starts[0], starts[1]))
            y = y.astype(jnp.bfloat16)
            for k, s in enumerate(segs):
                y_ref[s, j * seg_len:(j + 1) * seg_len] = y[k * seg_len:(k + 1) * seg_len]
            x_t = jnp.transpose(x_float)
            for k, h in enumerate(rows):
                scaled.append((x_t[k * head_dim:(k + 1) * head_dim] * weight[h:h + 1, :]).astype(jnp.bfloat16))
        gain = jnp.dot(jnp.concatenate(scaled, axis=0), b_mat, preferred_element_type=jnp.float32)
        for h in range(n_local):
            part = slice(h * head_dim, (h + 1) * head_dim)
            new = gain[part]
            if chunk:
                new = new + state[part] * last_e[chunk * 16 + h:chunk * 16 + h + 1]
            if chunk == n_chunks - 1:
                fin_ref[0, 0, h] = new
            else:
                state[part] = new


def scan_call(parity, packed, other, a_neg, d_wide, finals, place, sizes):
    n_prompts, seg_len, seg_count, n_local, head_dim, d_state, batch, layers = sizes
    blocks = n_local * head_dim // LANES
    group = LANES // seg_len
    per_prompt = (blocks + 1) * seg_len
    dt_first = n_prompts * per_prompt // 16
    layer_index, first_prompt = place
    body = functools.partial(scan_kernel, seg_count, seg_len, blocks, n_local, head_dim)
    in_specs = [
        pl.BlockSpec(memory_space=pltpu.SMEM),
        pl.BlockSpec((seg_count, blocks * seg_len, LANES), lambda g: (0, g, 0)),
        pl.BlockSpec((seg_count, seg_len, LANES), lambda g: (0, n_prompts * blocks + g, 0)),
        pl.BlockSpec((seg_count, seg_len, LANES), lambda g: (0, g, 0)),
        pl.BlockSpec((seg_count, 16, LANES), lambda g: (0, dt_first + g // group, 0)),
        pl.BlockSpec((16, LANES), lambda g: (0, 0)),
        pl.BlockSpec((1, n_local * head_dim), lambda g: (0, 0)),
    ]
    operands = [parity, packed, packed, other, packed, a_neg, d_wide]
    aliases = {}
    if finals is not None:
        in_specs.append(pl.BlockSpec(memory_space=pl.ANY))
        operands.append(finals)
        aliases = {7: 1}
    tokens = n_prompts * seg_len * seg_count
    return pl.pallas_call(
        body,
        grid=(n_prompts,),
        in_specs=in_specs,
        out_specs=[
            pl.BlockSpec((seg_count, blocks * seg_len, LANES), lambda g: (0, g, 0)),
            pl.BlockSpec((1, 1, n_local, head_dim, d_state), lambda g: (first_prompt + g, layer_index, 0, 0, 0)),
        ],
        out_shape=[
            jax.ShapeDtypeStruct((seg_count, n_prompts * blocks * seg_len, LANES), jnp.bfloat16),
            jax.ShapeDtypeStruct((batch, layers, n_local, head_dim, d_state), jnp.float32),
        ],
        scratch_shapes=[pltpu.VMEM((n_local * head_dim, d_state), jnp.float32)],
        input_output_aliases=aliases,
        cost_estimate=pl.CostEstimate(flops=tokens * n_local * 16000, bytes_accessed=tokens * n_local * head_dim * 6, transcendentals=tokens * n_local * LANES),
        name='scan',
    )(*operands)


def gate_kernel(n_src, blocks, seg_len, y_ref, z_ref, w_ref, out_ref, keep):
    total = jnp.zeros((seg_len, LANES), jnp.float32)
    for d in range(n_src):
        for j in range(blocks):
            cols = slice((d * blocks + j) * LANES, (d * blocks + j + 1) * LANES)
            z = z_ref[:, cols].astype(jnp.float32)
            g = y_ref[d, j * seg_len:(j + 1) * seg_len].astype(jnp.float32) * (z * jax.nn.sigmoid(z))
            keep[:, cols] = g
            total = total + g * g
    width = n_src * blocks * LANES
    scale = lax.rsqrt(jnp.sum(total, axis=1, keepdims=True) / width + EPSILON)
    for i in range(n_src * blocks):
        cols = slice(i * LANES, (i + 1) * LANES)
        out_ref[:, cols] = (keep[:, cols] * scale * w_ref[:, cols]).astype(jnp.bfloat16)


def gate_call(y, u, gate_w, n_prompts, seg_len, d_inner):
    n_src = y.shape[0]
    blocks = d_inner // n_src // LANES
    tokens = n_prompts * seg_len
    return pl.pallas_call(
        functools.partial(gate_kernel, n_src, blocks, seg_len),
        grid=(n_prompts,),
        in_specs=[
            pl.BlockSpec((n_src, blocks * seg_len, LANES), lambda p: (0, p, 0)),
            pl.BlockSpec((seg_len, d_inner), lambda p: (p, 0)),
            pl.BlockSpec((1, d_inner), lambda p: (0, 0)),
        ],
        out_specs=pl.BlockSpec((seg_len, d_inner), lambda p: (p, 0)),
        out_shape=jax.ShapeDtypeStruct((tokens, d_inner), jnp.bfloat16),
        scratch_shapes=[pltpu.VMEM((seg_len, d_inner), jnp.float32)],
        cost_estimate=pl.CostEstimate(flops=tokens * d_inner * 40, bytes_accessed=6 * tokens * d_inner, transcendentals=tokens * d_inner),
        name='gate',
    )(y, u, gate_w)


def solution(mesh):
    seg_count = mesh.shape['sp']

    def forward(resid, pre_norm, w_in, conv_w, conv_b, dt_bias, a_log, d_skip, gate_norm, w_out):
        batch, seg_len, d_model = resid.shape
        layers, n_heads = dt_bias.shape
        conv_dim = conv_b.shape[1]
        d_inner = gate_norm.shape[1] * gate_norm.shape[2]
        d_state = (conv_dim - d_inner) // 2
        head_dim = d_inner // n_heads
        n_local = n_heads // seg_count
        blocks = n_local * head_dim // LANES
        taps = CONV_WIDTH - 1
        seg_index = lax.axis_index('sp')
        parity = lax.rem(seg_index, 2).astype(jnp.int32).reshape(1)
        forward_pairs = [(source, source + 1) for source in range(seg_count - 1)]
        core_pairs = [(source, source ^ 1) for source in range(seg_count)]

        slot = jnp.arange(seg_count * 16)
        wanted = jnp.where(slot % 16 < n_local, slot // 16 * n_local + slot % 16, -1)
        select = (wanted[:, None] == jnp.arange(LANES)[None, :]).astype(jnp.bfloat16)
        pad_heads = lambda values: jnp.pad(values, ((0, 0), (0, LANES - n_heads)))
        dt_bias_wide = pad_heads(dt_bias)
        conv_wt = jnp.swapaxes(conv_w, 1, 2)

        finals = None
        starts = [sum(SIZES[:c]) for c in range(len(SIZES))]
        streams = [resid[starts[c]:starts[c] + SIZES[c]].reshape(SIZES[c] * seg_len, d_model) for c in range(len(SIZES))]
        tails = [[] for _ in range(layers)]
        last_seg = seg_count - 1
        hops = [[(last_seg, 1)], [(last_seg, last_seg - 2), (1, 3)], [(source, source - 1) for source in range(1, seg_count, 2)]]

        def spread(rows, hop):
            got = lax.ppermute(rows, 'sp', hop)
            takes = functools.reduce(jnp.logical_or, [seg_index == dest for _, dest in hop])
            return jnp.where(takes, got, rows)

        for l in range(layers):
            final_layer = l == layers - 1
            mine = lax.dynamic_slice_in_dim(a_log[l], seg_index * n_local, n_local)
            a_neg = jnp.broadcast_to(jnp.pad(-jnp.exp(mine), (0, 16 - n_local))[:, None], (16, LANES))
            d_wide = jnp.repeat(lax.dynamic_slice_in_dim(d_skip[l], seg_index * n_local, n_local), head_dim)[None]
            packs, gates = [], []
            for c, n_prompts in enumerate(SIZES):
                if c > 0:
                    streams[c], tails[l][c - 1] = lax.optimization_barrier((streams[c], tails[l][c - 1]))
                r = streams[c]
                h = (r * lax.rsqrt(jnp.mean(r * r, axis=-1, keepdims=True) + EPSILON) * pre_norm[l]).astype(jnp.bfloat16)
                u = jnp.dot(h, w_in[l, :, d_inner:], preferred_element_type=jnp.float32).astype(jnp.bfloat16)
                tail = tail_call(u, n_prompts, seg_len, conv_dim)
                tails[l].append(tail)
                halo = lax.ppermute(tail, 'sp', forward_pairs)
                packed = conv_call(u, halo, conv_wt[l], conv_b[l:l + 1], dt_bias_wide[l:l + 1], select, (n_prompts, seg_len, d_inner, conv_dim, n_heads, seg_count))
                packed, h = lax.optimization_barrier((packed, h))
                packs.append(packed)
                gates.append(jnp.dot(h, w_in[l, :, :d_inner], preferred_element_type=jnp.float32).astype(jnp.bfloat16))
            if final_layer:
                tail_rows = jnp.concatenate([rows for layer_rows in tails for rows in layer_rows], axis=1)
            outs, arrived = [], []
            for c in range(len(SIZES)):
                arrived.append(lax.all_to_all(packs[c], 'sp', 0, 0, tiled=True))
            if final_layer:
                arrived[-1], tail_rows = lax.optimization_barrier((arrived[-1], spread(tail_rows, hops[0])))
            for c, n_prompts in enumerate(SIZES):
                packed = arrived[c]
                bc_start = n_prompts * blocks * seg_len
                bc = packed[:, bc_start:bc_start + n_prompts * seg_len]
                other = lax.ppermute(bc, 'sp', core_pairs)
                y, finals = scan_call(parity, packed, other, a_neg, d_wide, finals, (l, starts[c]), (n_prompts, seg_len, seg_count, n_local, head_dim, d_state, batch, layers))
                y = lax.all_to_all(y, 'sp', 0, 0, tiled=True)
                if final_layer and c >= len(SIZES) - 2:
                    y, tail_rows = lax.optimization_barrier((y, spread(tail_rows, hops[c - len(SIZES) + 3])))
                outs.append(y)
            for c, n_prompts in enumerate(SIZES):
                g = gate_call(outs[c], gates[c], gate_norm[l], n_prompts, seg_len, d_inner)
                streams[c] = streams[c] + jnp.dot(g, w_out[l], preferred_element_type=jnp.float32)
        out = jnp.concatenate(streams, axis=0).reshape(batch, seg_len, d_model)
        conv_state = tail_rows.reshape(taps, layers, batch, conv_dim)
        return out, finals, jnp.transpose(conv_state, (2, 1, 3, 0))

    return jax.shard_map(forward, mesh=mesh, in_specs=(P('dp', 'sp', None), P(), P(), P(), P(), P(), P(), P(), P(), P()), out_specs=(P('dp', 'sp', None), P('dp', None, 'sp', None, None), P('dp', None, None, None)), check_vma=False)
```

time: 1010 us -> 803 us (0.80)
  local copies, waits for them, and re-layouts: 106 us -> 22.8 us
  Pallas kernels: 274 us -> 192 us
  matrix products: 307 us -> 257 us
  waiting for transfers between devices: 141 us -> 157 us
  other arithmetic: 24.5 us -> 39.6 us
  between operations: 15.4 us -> 1.39 us
  starting transfers between devices: 133 us -> 120 us
    pallas_call x8, Pallas kernels: 205 us -> 106 us  [the longest x4 83.6 us: scan_call(): pl.pallas_call(body, grid=(n_prompts,), in_specs=in_specs, out_specs=[pl....]
    all_to_all x8 -> x4, waiting for transfers between devices: 35.7 us -> 104 us  [forward(): arrived.append(lax.all_to_all(packs[c], 'sp', 0, 0, tiled=True))]
    unnamed x127 -> x46, local copies, waits for them, and re-layouts: 76.1 us -> 8.35 us
    psum x1 -> x0, waiting for transfers between devices: 59.4 us -> none  [forward(): conv_state = lax.psum(tail_rows, 'sp')]
    dot_general x16 -> x12, matrix products: 307 us -> 257 us  [the longest x4 89.9 us: forward(): jnp.dot(g, w_out[l], preferred_element_type=jnp.float32)]
    all_to_all x8 -> x4, starting transfers between devices: 72.9 us -> 45.6 us  [forward(): arrived.append(lax.all_to_all(packs[c], 'sp', 0, 0, tiled=True))]
    slice x24 -> x4, local copies, waits for them, and re-layouts: 28 us -> 6.16 us  [forward(): bc = packed[:, bc_start:bc_start + n_prompts * seg_len]]
    pallas_call x8 -> x4, Pallas kernels: 25.3 us -> 39.7 us  [gate_call(): pl.pallas_call(functools.partial(gate_kernel, n_src, blocks, seg_len), gr...]
  transfers between devices with their start and end apart: 33 -> 19, of which waited for: 19 -> 11; matrix products, arithmetic and copies ran while one was open for 31% -> 31% of each run, Pallas kernels for 27% -> 19%
where the time goes in v2:
time: 803 us; the launch traced here: 791 us
  matrix products  257 us (32%)
  Pallas kernels  192 us (24%)
  waiting for transfers between devices  157 us (20%)
  starting transfers between devices  120 us (15%)
  other arithmetic  39.6 us (5%)
  local copies, waits for them, and re-layouts  22.8 us (3%)
    all_to_all x4, waiting for transfers between devices, forward(): arrived.append(lax.all_to_all(packs[c], 'sp', 0, 0, tiled=True))  104 us
    dot_general x4, matrix products, forward(): jnp.dot(g, w_out[l], preferred_element_type=jnp.float32)  89.9 us
    dot_general x4, matrix products, forward(): jnp.dot(h, w_in[l, :, d_inner:], preferred_element_type=jnp.float32)  87.6 us
    pallas_call x4, Pallas kernels, scan_call(): pl.pallas_call(body, grid=(n_prompts,), in_specs=in_specs, out_specs=[pl....  83.6 us
    dot_general x4, matrix products, forward(): jnp.dot(h, w_in[l, :, :d_inner], preferred_element_type=jnp.float32)  79.9 us
    all_to_all x4, starting transfers between devices, forward(): y = lax.all_to_all(y, 'sp', 0, 0, tiled=True)  48.9 us
    all_to_all x4, waiting for transfers between devices, forward(): y = lax.all_to_all(y, 'sp', 0, 0, tiled=True)  47.3 us
    pallas_call x4, Pallas kernels, conv_call(): pl.pallas_call(body, grid=(n_dest,), in_specs=[pl.BlockSpec((tokens, widt...  46.6 us
  transfers between devices with their start and end apart: 19, of which 11 were waited for; matrix products, arithmetic and copies ran while one was open for 31% of the time, Pallas kernels for 19%

profile of v2, /device:TPU:112, one launch (start us, length us, event | category | flops | bytes accessed | tf_op | source)
XLA Modules:
  0.0 790.9 jit_solution(16430880538271003976)
XLA Ops:
  0.6 9.6 %fusion.84 = (f32[8,64,2560]{2,1,0:T(8,128)}, f32[8,64]{1,0:T(8,128)S(1)}, f32[8,64,2560]{2,1,0:T(8,128)}) fusion(f32[16,64,2560]{2,1,0:T(8,128)} %param.10), kind=kLoop, calls=%fused_computation.99 | loop fusion | flops 2620928 | bytes 20973568 | tf_op jit(solution)/shard_map/slice | solution.py:306
  11.4 21.8 %fusion.36.u_ref.x_ref.bc_ref.dtr_ref = bf16[512,5456]{1,0:T(8,128)(2,1)} fusion(bf16[512,2560]{1,0:T(8,128)(2,1)S(1)} %bitcast.105, bf16[2,2560,10576]{1,2,0:T(8,128)(2,1)} %param.12), kind=kOutput, calls=%fused_computation.37 | convolution fusion | flops 14305370112 | bytes 36143104 | tf_op jit(solution)/shard_map/dot_general | solution.py:327
  33.2 5.6 tail.4
  38.9 1.7 collective-permute-start
  40.7 2.9 multiply_reduce_fusion.1
  45.5 6.4 fusion.61
  53.3 11.6 %conv_pack.4 = bf16[8,3136,128]{2,1,0:T(8,128)(2,1)} custom-call(bf16[512,5456]{1,0:T(8,128)(2,1)} %fusion.36.u_ref.x_ref.bc_ref.dtr_ref, bf16[512,5456]{1,0:T(8,128)(2,1)} %fusion.36.u_ref.x_ref.bc_ref.dtr_ref, bf16[512,5456]{1,0:T(8,128)(2,1)} %fusion.36.u_ref.x_ref.bc_ref.dtr_ref, bf16[3,8,5376]{2,1,0:T(8,128)(2,1)} %copy-done.9, ...), custom_call_target="tpu_custom_call" | custom-call | flops 157286400 | bytes 10485760 | tf_op jit(solution)/shard_map/conv_pack/pallas_call | solution.py:93
  64.9 6.5 all-to-all-start
  71.4 21.9 %fusion.39.u_ref.x_ref.bc_ref.dtr_ref = bf16[512,5456]{1,0:T(8,128)(2,1)} fusion(bf16[512,2560]{1,0:T(8,128)(2,1)S(1)} %get-tuple-element.39, bf16[2,2560,10576]{1,2,0:T(8,128)(2,1)} %param.12), kind=kOutput, calls=%fused_computation.38 | convolution fusion | flops 14305370112 | bytes 36143104 | tf_op jit(solution)/shard_map/dot_general | solution.py:327
  93.3 5.6 tail.6
  98.9 3.1 collective-permute-start.4
  103.9 11.6 %conv_pack.6 = bf16[8,3136,128]{2,1,0:T(8,128)(2,1)} custom-call(bf16[512,5456]{1,0:T(8,128)(2,1)} %fusion.39.u_ref.x_ref.bc_ref.dtr_ref, bf16[512,5456]{1,0:T(8,128)(2,1)} %fusion.39.u_ref.x_ref.bc_ref.dtr_ref, bf16[512,5456]{1,0:T(8,128)(2,1)} %fusion.39.u_ref.x_ref.bc_ref.dtr_ref, bf16[3,8,5376]{2,1,0:T(8,128)(2,1)} %copy-done.12, ...), custom_call_target="tpu_custom_call" | custom-call | flops 157286400 | bytes 10485760 | tf_op jit(solution)/shard_map/conv_pack/pallas_call | solution.py:93
  115.5 30.1 %all-to-all-done.x_ref.mine_ref.dt_ref = bf16[8,3136,128]{2,1,0:T(8,128)(2,1)} async-done(((bf16[8,3136,128]{2,1,0:T(8,128)(2,1)}), bf16[8,3136,128]{2,1,0:T(8,128)(2,1)}, u32[]{:S(2)}, u32[]{:S(2)}) %all-to-all-start) | async-done | bytes 6422560 | tf_op jit(solution)/shard_map/all_to_all | solution.py:339
  145.6 16.6 %all-to-all-start.3 = ((bf16[8,3136,128]{2,1,0:T(8,128)(2,1)}), bf16[8,3136,128]{2,1,0:T(8,128)(2,1)}, u32[]{:S(2)}, u32[]{:S(2)}) async-start(bf16[8,3136,128]{2,1,0:T(8,128)(2,1)} %conv_pack.6), calls=%async_computation.3 | async-start | bytes 12845056 | tf_op jit(solution)/shard_map/all_to_all | solution.py:339
  162.2 2.3 slice.121
  168.3 20.8 %scan.4 = (bf16[8,2560,128]{2,1,0:T(8,128)(2,1)}, f32[16,2,10,64,128]{4,3,2,1,0:T(8,128)}) custom-call(s32[1]{0:T(128)} %bitcast.1.par_ref, bf16[8,3136,128]{2,1,0:T(8,128)(2,1)} %all-to-all-done.x_ref.mine_ref.dt_ref, bf16[8,3136,128]{2,1,0:T(8,128)(2,1)} %all-to-all-done.x_ref.mine_ref.dt_ref, bf16[8,512,128]{2,1,0:T(8,128)(2,1)} %collective-permute-done.1.other_ref, ...), custom_call_target="tpu_custom_call" | custom-call | flops 655360000 | bytes 15728640 | tf_op jit(solution)/shard_map/scan/pallas_call | solution.py:224
  189.1 46.7 %all-to-all-done.3.x_ref.mine_ref.dt_ref = bf16[8,3136,128]{2,1,0:T(8,128)(2,1)} async-done(((bf16[8,3136,128]{2,1,0:T(8,128)(2,1)}), bf16[8,3136,128]{2,1,0:T(8,128)(2,1)}, u32[]{:S(2)}, u32[]{:S(2)}) %all-to-all-start.3) | async-done | bytes 6422560 | tf_op jit(solution)/shard_map/all_to_all | solution.py:339
  235.8 5.0 all-to-all-start.1
  243.0 20.3 %fusion.48.z_ref = bf16[512,5120]{1,0:T(8,128)(2,1)} fusion(bf16[512,2560]{1,0:T(8,128)(2,1)} %get-tuple-element.31, bf16[2,2560,10576]{1,2,0:T(8,128)(2,1)} %param.12), kind=kOutput, calls=%fused_computation.41 | convolution fusion | flops 13424394240 | bytes 34078720 | tf_op jit(solution)/shard_map/dot_general | solution.py:334
  264.3 21.0 %scan.5 = (bf16[8,2560,128]{2,1,0:T(8,128)(2,1)}, f32[16,2,10,64,128]{4,3,2,1,0:T(8,128)}) custom-call(s32[1]{0:T(128)} %bitcast.1.par_ref, bf16[8,3136,128]{2,1,0:T(8,128)(2,1)} %all-to-all-done.3.x_ref.mine_ref.dt_ref, bf16[8,3136,128]{2,1,0:T(8,128)(2,1)} %all-to-all-done.3.x_ref.mine_ref.dt_ref, ...), custom_call_target="tpu_custom_call", output_to_operand_aliasing={{1}: (7, {})} | custom-call | flops 655360000 | bytes 15728640 | tf_op jit(solution)/shard_map/scan/pallas_call | solution.py:224
  285.3 16.3 %all-to-all-done.1.y_ref = bf16[8,2560,128]{2,1,0:T(8,128)(2,1)} async-done(((bf16[8,2560,128]{2,1,0:T(8,128)(2,1)}), bf16[8,2560,128]{2,1,0:T(8,128)(2,1)}, u32[]{:S(2)}, u32[]{:S(2)}) %all-to-all-start.1) | async-done | bytes 5242912 | tf_op jit(solution)/shard_map/all_to_all | solution.py:348
  301.6 5.2 all-to-all-start.5
  306.8 9.9 %gate.4 = bf16[512,5120]{1,0:T(8,128)(2,1)} custom-call(bf16[8,2560,128]{2,1,0:T(8,128)(2,1)} %all-to-all-done.1.y_ref, bf16[512,5120]{1,0:T(8,128)(2,1)} %fusion.48.z_ref, f32[1,5120]{1,0:T(1,128)} %get-tuple-element.65.w_ref), custom_call_target="tpu_custom_call" | custom-call | flops 104857600 | bytes 15728640 | tf_op jit(solution)/shard_map/gate/pallas_call | solution.py:263
  316.8 22.6 %multiply_reduce_fusion.2 = (f32[512]{0:T(512)S(1)}, f32[512,2560]{1,0:T(8,128)}) fusion(bf16[512,5120]{1,0:T(8,128)(2,1)} %gate.4, bf16[2,5120,2560]{2,1,0:T(8,128)(2,1)} %param.19, f32[8,64,2560]{2,1,0:T(8,128)} %get-tuple-element.57), kind=kOutput, calls=%fused_computation.54 | convolution fusion | flops 13425704960 | bytes 41945088 | tf_op jit(solution)/shard_map/dot_general | solution.py:354
  339.4 3.0 multiply_convert_fusion.2
  342.4 1.5 copy-done.2
  344.0 21.8 %fusion.42.u_ref.x_ref.bc_ref.dtr_ref = bf16[512,5456]{1,0:T(8,128)(2,1)} fusion(bf16[512,2560]{1,0:T(8,128)(2,1)S(1)} %multiply_convert_fusion.2, bf16[2,2560,10576]{1,2,0:T(8,128)(2,1)} %param.12), kind=kOutput, calls=%fused_computation.39 | convolution fusion | flops 14305370112 | bytes 36143104 | tf_op jit(solution)/shard_map/dot_general | solution.py:327
  365.8 5.6 tail.5
  371.4 2.3 collective-permute-start.2
  373.7 19.6 %fusion.51.z_ref = bf16[512,5120]{1,0:T(8,128)(2,1)} fusion(bf16[512,2560]{1,0:T(8,128)(2,1)S(1)} %get-tuple-element.39, bf16[2,2560,10576]{1,2,0:T(8,128)(2,1)} %param.12), kind=kOutput, calls=%fused_computation.42 | convolution fusion | flops 13424394240 | bytes 34078720 | tf_op jit(solution)/shard_map/dot_general | solution.py:334
  393.3 9.9 %gate.5 = bf16[512,5120]{1,0:T(8,128)(2,1)} custom-call(bf16[8,2560,128]{2,1,0:T(8,128)(2,1)} %all-to-all-done.5.y_ref, bf16[512,5120]{1,0:T(8,128)(2,1)} %fusion.51.z_ref, f32[1,5120]{1,0:T(1,128)} %get-tuple-element.65.w_ref), custom_call_target="tpu_custom_call" | custom-call | flops 104857600 | bytes 15728640 | tf_op jit(solution)/shard_map/gate/pallas_call | solution.py:263
  404.0 11.7 %conv_pack.5 = bf16[8,3136,128]{2,1,0:T(8,128)(2,1)} custom-call(bf16[512,5456]{1,0:T(8,128)(2,1)} %fusion.42.u_ref.x_ref.bc_ref.dtr_ref, bf16[512,5456]{1,0:T(8,128)(2,1)} %fusion.42.u_ref.x_ref.bc_ref.dtr_ref, bf16[512,5456]{1,0:T(8,128)(2,1)} %fusion.42.u_ref.x_ref.bc_ref.dtr_ref, bf16[3,8,5376]{2,1,0:T(8,128)(2,1)} %copy-done.10, ...), custom_call_target="tpu_custom_call" | custom-call | flops 157286400 | bytes 10485760 | tf_op jit(solution)/shard_map/conv_pack/pallas_call | solution.py:93
  415.7 5.6 all-to-all-start.2
  421.3 22.5 %fusion.64 = f32[512,2560]{1,0:T(8,128)} fusion(f32[512,2560]{1,0:T(8,128)} %bitcast.102, bf16[512,5120]{1,0:T(8,128)(2,1)} %gate.5, bf16[2,5120,2560]{2,1,0:T(8,128)(2,1)} %param.19), kind=kOutput, calls=%fused_computation.57 | convolution fusion | flops 13423083520 | bytes 41943040 | tf_op jit(solution)/shard_map/dot_general | solution.py:354
  443.7 3.1 multiply_reduce_fusion
  448.3 22.0 %fusion.45.u_ref.x_ref.bc_ref.dtr_ref = bf16[512,5456]{1,0:T(8,128)(2,1)} fusion(bf16[512,2560]{1,0:T(8,128)(2,1)S(1)} %multiply_convert_fusion, bf16[2,2560,10576]{1,2,0:T(8,128)(2,1)} %param.12), kind=kOutput, calls=%fused_computation.40 | convolution fusion | flops 14305370112 | bytes 36143104 | tf_op jit(solution)/shard_map/dot_general | solution.py:327
  470.3 5.6 tail.7
  475.8 3.0 collective-permute-start.6
  478.8 1.3 collective-permute-done.6.xh_ref.bch_ref
  480.8 11.6 %conv_pack.7 = bf16[8,3136,128]{2,1,0:T(8,128)(2,1)} custom-call(bf16[512,5456]{1,0:T(8,128)(2,1)} %fusion.45.u_ref.x_ref.bc_ref.dtr_ref, bf16[512,5456]{1,0:T(8,128)(2,1)} %fusion.45.u_ref.x_ref.bc_ref.dtr_ref, bf16[512,5456]{1,0:T(8,128)(2,1)} %fusion.45.u_ref.x_ref.bc_ref.dtr_ref, bf16[3,8,5376]{2,1,0:T(8,128)(2,1)} %copy-done.11, ...), custom_call_target="tpu_custom_call" | custom-call | flops 157286400 | bytes 10485760 | tf_op jit(solution)/shard_map/conv_pack/pallas_call | solution.py:93
  492.5 2.8 all-to-all-done.2.x_ref.mine_ref.dt_ref
  495.3 16.9 %all-to-all-start.6 = ((bf16[8,3136,128]{2,1,0:T(8,128)(2,1)}), bf16[8,3136,128]{2,1,0:T(8,128)(2,1)}, u32[]{:S(2)}, u32[]{:S(2)}) async-start(bf16[8,3136,128]{2,1,0:T(8,128)(2,1)} %conv_pack.7), calls=%async_computation.6 | async-start | bytes 12845056 | tf_op jit(solution)/shard_map/all_to_all | solution.py:339
  513.0 2.0 pad_maximum_fusion.1
  515.0 1.8 collective-permute-start.7
  516.8 1.3 slice.123
  518.4 20.3 %fusion.54.z_ref = bf16[512,5120]{1,0:T(8,128)(2,1)} fusion(bf16[512,2560]{1,0:T(8,128)(2,1)} %copy-done.2, bf16[2,2560,10576]{1,2,0:T(8,128)(2,1)} %param.12), kind=kOutput, calls=%fused_computation.43 | convolution fusion | flops 13424394240 | bytes 34078720 | tf_op jit(solution)/shard_map/dot_general | solution.py:334
  540.4 20.8 %scan.6 = (bf16[8,2560,128]{2,1,0:T(8,128)(2,1)}, f32[16,2,10,64,128]{4,3,2,1,0:T(8,128)}) custom-call(s32[1]{0:T(128)} %bitcast.1.par_ref, bf16[8,3136,128]{2,1,0:T(8,128)(2,1)} %all-to-all-done.2.x_ref.mine_ref.dt_ref, bf16[8,3136,128]{2,1,0:T(8,128)(2,1)} %all-to-all-done.2.x_ref.mine_ref.dt_ref, ...), custom_call_target="tpu_custom_call", output_to_operand_aliasing={{1}: (7, {})} | custom-call | flops 655360000 | bytes 15728640 | tf_op jit(solution)/shard_map/scan/pallas_call | solution.py:224
  561.2 24.7 %all-to-all-done.6.x_ref.mine_ref.dt_ref = bf16[8,3136,128]{2,1,0:T(8,128)(2,1)} async-done(((bf16[8,3136,128]{2,1,0:T(8,128)(2,1)}), bf16[8,3136,128]{2,1,0:T(8,128)(2,1)}, u32[]{:S(2)}, u32[]{:S(2)}) %all-to-all-start.6) | async-done | bytes 6422560 | tf_op jit(solution)/shard_map/all_to_all | solution.py:339
  585.9 4.9 all-to-all-start.4
  592.8 19.6 %fusion.57.z_ref = bf16[512,5120]{1,0:T(8,128)(2,1)} fusion(bf16[512,2560]{1,0:T(8,128)(2,1)S(1)} %multiply_convert_fusion, bf16[2,2560,10576]{1,2,0:T(8,128)(2,1)} %param.12), kind=kOutput, calls=%fused_computation.44 | convolution fusion | flops 13424394240 | bytes 34078720 | tf_op jit(solution)/shard_map/dot_general | solution.py:334
  612.4 1.3 slice.119
  613.7 10.8 %collective-permute-start.9 = (bf16[8,512,128]{2,1,0:T(8,128)(2,1)S(1)}, bf16[8,512,128]{2,1,0:T(8,128)(2,1)S(1)}, u32[]{:S(2)}, u32[]{:S(2)}) collective-permute-start(bf16[8,512,128]{2,1,0:T(8,128)(2,1)S(1)} %slice.119), channel_id=1, source_target_pairs={{0,1},{1,0},{2,3},{3,2},{4,5},{5,4},{6,7},{7,6},{8,9},{9,8},{10,11... | collective-permute-start | bytes 3145736 | tf_op jit(solution)/shard_map/ppermute | solution.py:346
  624.6 2.2 collective-permute-done.9.other_ref
  627.7 21.0 %scan.7 = (bf16[8,2560,128]{2,1,0:T(8,128)(2,1)}, f32[16,2,10,64,128]{4,3,2,1,0:T(8,128)}) custom-call(s32[1]{0:T(128)} %bitcast.1.par_ref, bf16[8,3136,128]{2,1,0:T(8,128)(2,1)} %all-to-all-done.6.x_ref.mine_ref.dt_ref, bf16[8,3136,128]{2,1,0:T(8,128)(2,1)} %all-to-all-done.6.x_ref.mine_ref.dt_ref, ...), custom_call_target="tpu_custom_call", output_to_operand_aliasing={{1}: (7, {})} | custom-call | flops 655360000 | bytes 15728640 | tf_op jit(solution)/shard_map/scan/pallas_call | solution.py:224
  648.7 4.0 all-to-all-done.4.y_ref
  652.8 33.8 %all-to-all-start.7 = ((bf16[8,2560,128]{2,1,0:T(8,128)(2,1)}), bf16[8,2560,128]{2,1,0:T(8,128)(2,1)}, u32[]{:S(2)}, u32[]{:S(2)}) async-start(bf16[8,2560,128]{2,1,0:T(8,128)(2,1)} %get-tuple-element.49), calls=%async_computation.7 | async-start | bytes 10485760 | tf_op jit(solution)/shard_map/all_to_all | solution.py:348
  686.6 1.5 collective-permute-start.10
  688.1 9.9 %gate.6 = bf16[512,5120]{1,0:T(8,128)(2,1)} custom-call(bf16[8,2560,128]{2,1,0:T(8,128)(2,1)} %all-to-all-done.4.y_ref, bf16[512,5120]{1,0:T(8,128)(2,1)} %fusion.54.z_ref, f32[1,5120]{1,0:T(1,128)} %get-tuple-element.64.w_ref), custom_call_target="tpu_custom_call" | custom-call | flops 104857600 | bytes 15728640 | tf_op jit(solution)/shard_map/gate/pallas_call | solution.py:263
  698.0 22.5 %fusion.67 = f32[512,2560]{1,0:T(8,128)} fusion(f32[512,2560]{1,0:T(8,128)} %get-tuple-element.75, bf16[512,5120]{1,0:T(8,128)(2,1)} %gate.6, bf16[2,5120,2560]{2,1,0:T(8,128)(2,1)} %param.19), kind=kOutput, calls=%fused_computation.58 | convolution fusion | flops 13423083520 | bytes 41943040 | tf_op jit(solution)/shard_map/dot_general | solution.py:354
  720.6 27.0 %all-to-all-done.7.y_ref = bf16[8,2560,128]{2,1,0:T(8,128)(2,1)} async-done(((bf16[8,2560,128]{2,1,0:T(8,128)(2,1)}), bf16[8,2560,128]{2,1,0:T(8,128)(2,1)}, u32[]{:S(2)}, u32[]{:S(2)}) %all-to-all-start.7) | async-done | bytes 5242912 | tf_op jit(solution)/shard_map/all_to_all | solution.py:348
  747.6 9.9 %gate.7 = bf16[512,5120]{1,0:T(8,128)(2,1)} custom-call(bf16[8,2560,128]{2,1,0:T(8,128)(2,1)} %all-to-all-done.7.y_ref, bf16[512,5120]{1,0:T(8,128)(2,1)} %fusion.57.z_ref, f32[1,5120]{1,0:T(1,128)} %get-tuple-element.64.w_ref), custom_call_target="tpu_custom_call" | custom-call | flops 104857600 | bytes 15728640 | tf_op jit(solution)/shard_map/gate/pallas_call | solution.py:263
  757.5 22.3 %fusion.70 = f32[512,2560]{1,0:T(8,128)} fusion(f32[512,2560]{1,0:T(8,128)} %fusion.64, bf16[512,5120]{1,0:T(8,128)(2,1)} %gate.7, bf16[2,5120,2560]{2,1,0:T(8,128)(2,1)} %param.19), kind=kOutput, calls=%fused_computation.59 | convolution fusion | flops 13423083520 | bytes 41943040 | tf_op jit(solution)/shard_map/dot_general | solution.py:354
  779.8 1.8 copy.26
  781.6 8.9 %pad_maximum_fusion = f32[1024,2560]{1,0:T(8,128)} fusion(f32[512,2560]{1,0:T(8,128)} %fusion.70, f32[512,2560]{1,0:T(8,128)} %fusion.67), kind=kLoop, calls=%fused_computation.36 | loop fusion | flops 2621440 | bytes 20971520 | tf_op jit(solution)/shard_map/concatenate | solution.py:355
  (89 shorter events, 22.0 us)
Async XLA Ops:
  0.6 10.2 %copy-start = (f32[16,64,2560]{2,1,0:T(8,128)S(1)}, f32[16,64,2560]{2,1,0:T(8,128)}, u32[]{:S(2)}) copy-start(f32[16,64,2560]{2,1,0:T(8,128)} %param.10) | copy-start | bytes 31457284
  0.6 9.6 %copy-start.17 = (f32[2,2560]{1,0:T(2,128)S(1)}, f32[2,2560]{1,0:T(2,128)}, u32[]{:S(2)}) copy-start(f32[2,2560]{1,0:T(2,128)} %param.11) | copy-start | bytes 61444
  33.2 10.4 %copy-start.13 = (f32[2,5376,4]{1,2,0:T(4,128)S(1)}, f32[2,5376,4]{1,2,0:T(4,128)}, u32[]{:S(2)}) copy-start(f32[2,5376,4]{1,2,0:T(4,128)} %param.13) | copy-start | bytes 516100
  33.2 11.1 %copy-start.15 = (f32[2,5376]{1,0:T(2,128)S(1)}, f32[2,5376]{1,0:T(2,128)}, u32[]{:S(2)}) copy-start(f32[2,5376]{1,0:T(2,128)} %param.14) | copy-start | bytes 129028
  33.2 11.7 %copy-start.19 = (f32[2,80]{1,0:T(2,128)S(1)}, f32[2,80]{1,0:T(2,128)}, u32[]{:S(2)}) copy-start(f32[2,80]{1,0:T(2,128)} %param.15) | copy-start | bytes 1924
  38.9 13.7 %collective-permute-start = (bf16[3,8,5376]{2,1,0:T(8,128)(2,1)}, bf16[3,8,5376]{2,1,0:T(8,128)(2,1)S(1)}, u32[]{:S(2)}, u32[]{:S(2)}) collective-permute-start(bf16[3,8,5376]{2,1,0:T(8,128)(2,1)} %tail.4), channel_id=1, source_target_pairs={{0,1},{1,2},{2,3},{3,4},{4,5},{5,6},{6,7},{8,9},{9,10},{10,11},{11... | collective-permute-start | bytes 774152 | tf_op jit(solution)/shard_map/ppermute | solution.py:330
  52.6 0.7 copy-start.9
  64.9 80.7 %all-to-all-start = ((bf16[8,3136,128]{2,1,0:T(8,128)(2,1)}), bf16[8,3136,128]{2,1,0:T(8,128)(2,1)}, u32[]{:S(2)}, u32[]{:S(2)}) async-start(bf16[8,3136,128]{2,1,0:T(8,128)(2,1)} %conv_pack.4), calls=%async_computation | async-start | bytes 12845056 | tf_op jit(solution)/shard_map/all_to_all | solution.py:339
  98.9 4.2 collective-permute-start.4
  103.1 0.7 copy-start.12
  115.5 49.5 %copy-start.20 = (f32[2,80]{1,0:T(2,128)S(1)}, f32[2,80]{1,0:T(2,128)}, u32[]{:S(2)}) copy-start(f32[2,80]{1,0:T(2,128)} %param.17) | copy-start | bytes 1924
  115.5 50.8 %copy-start.21 = (f32[2,80]{1,0:T(2,128)S(1)}, f32[2,80]{1,0:T(2,128)}, u32[]{:S(2)}) copy-start(f32[2,80]{1,0:T(2,128)} %param.16) | copy-start | bytes 1924
  145.6 90.2 %all-to-all-start.3 = ((bf16[8,3136,128]{2,1,0:T(8,128)(2,1)}), bf16[8,3136,128]{2,1,0:T(8,128)(2,1)}, u32[]{:S(2)}, u32[]{:S(2)}) async-start(bf16[8,3136,128]{2,1,0:T(8,128)(2,1)} %conv_pack.6), calls=%async_computation.3 | async-start | bytes 12845056 | tf_op jit(solution)/shard_map/all_to_all | solution.py:339
  164.5 3.1 collective-permute-start.1
  235.8 5.0 copy-start.16
  235.8 65.7 %all-to-all-start.1 = ((bf16[8,2560,128]{2,1,0:T(8,128)(2,1)}), bf16[8,2560,128]{2,1,0:T(8,128)(2,1)}, u32[]{:S(2)}, u32[]{:S(2)}) async-start(bf16[8,2560,128]{2,1,0:T(8,128)(2,1)} %get-tuple-element.30), calls=%async_computation.1 | async-start | bytes 10485760 | tf_op jit(solution)/shard_map/all_to_all | solution.py:348
  242.7 20.6 %collective-permute-start.5 = (bf16[8,512,128]{2,1,0:T(8,128)(2,1)S(1)}, bf16[8,512,128]{2,1,0:T(8,128)(2,1)S(1)}, u32[]{:S(2)}, u32[]{:S(2)}) collective-permute-start(bf16[8,512,128]{2,1,0:T(8,128)(2,1)S(1)} %slice.124), channel_id=1, source_target_pairs={{0,1},{1,0},{2,3},{3,2},{4,5},{5,4},{6,7},{7,6},{8,9},{9,8},{10,11... | collective-permute-start | bytes 3145736 | tf_op jit(solution)/shard_map/ppermute | solution.py:346
  263.3 1.0 copy-start.7
  301.6 91.8 %all-to-all-start.5 = ((bf16[8,2560,128]{2,1,0:T(8,128)(2,1)}), bf16[8,2560,128]{2,1,0:T(8,128)(2,1)}, u32[]{:S(2)}, u32[]{:S(2)}) async-start(bf16[8,2560,128]{2,1,0:T(8,128)(2,1)} %get-tuple-element.38), calls=%async_computation.5 | async-start | bytes 10485760 | tf_op jit(solution)/shard_map/all_to_all | solution.py:348
  316.8 22.7 %copy-start.14 = (f32[2560]{0:T(1024)S(1)}, f32[2560]{0:T(1024)}, u32[]{:S(2)}) copy-start(f32[2560]{0:T(1024)} %get-tuple-element.55) | copy-start | bytes 30724
  342.4 1.5 copy-start.2
  371.4 31.9 %collective-permute-start.2 = (bf16[3,8,5376]{2,1,0:T(8,128)(2,1)}, bf16[3,8,5376]{2,1,0:T(8,128)(2,1)S(1)}, u32[]{:S(2)}, u32[]{:S(2)}) collective-permute-start(bf16[3,8,5376]{2,1,0:T(8,128)(2,1)} %tail.5), channel_id=1, source_target_pairs={{0,1},{1,2},{2,3},{3,4},{4,5},{5,6},{6,7},{8,9},{9,10},{10,11},{11... | collective-permute-start | bytes 774152 | tf_op jit(solution)/shard_map/ppermute | solution.py:330
  403.3 0.7 copy-start.10
  415.7 79.7 %all-to-all-start.2 = ((bf16[8,3136,128]{2,1,0:T(8,128)(2,1)}), bf16[8,3136,128]{2,1,0:T(8,128)(2,1)}, u32[]{:S(2)}, u32[]{:S(2)}) async-start(bf16[8,3136,128]{2,1,0:T(8,128)(2,1)} %conv_pack.5), calls=%async_computation.2 | async-start | bytes 12845056 | tf_op jit(solution)/shard_map/all_to_all | solution.py:339
  443.7 4.0 copy-start.1
  475.8 4.3 collective-permute-start.6
  480.1 0.7 copy-start.11
  492.5 19.7 %copy-start.18 = (f32[10]{0:T(128)S(1)}, f32[10]{0:T(128)}, u32[]{:S(2)}) copy-start(f32[10]{0:T(128)} %get-tuple-element.79) | copy-start | bytes 124
  492.5 20.5 %copy-start.22 = (f32[10]{0:T(128)S(1)}, f32[10]{0:T(128)}, u32[]{:S(2)}) copy-start(f32[10]{0:T(128)} %get-tuple-element.76) | copy-start | bytes 124
  492.5 20.5 %copy-start.3 = (bf16[3,8,5376]{2,1,0:T(8,128)(2,1)S(1)}, bf16[3,8,5376]{2,1,0:T(8,128)(2,1)}, u32[]{:S(2)}) copy-start(bf16[3,8,5376]{2,1,0:T(8,128)(2,1)} %tail.4) | copy-start | bytes 774148
  492.5 20.5 %copy-start.4 = (bf16[3,8,5376]{2,1,0:T(8,128)(2,1)S(1)}, bf16[3,8,5376]{2,1,0:T(8,128)(2,1)}, u32[]{:S(2)}) copy-start(bf16[3,8,5376]{2,1,0:T(8,128)(2,1)} %tail.6) | copy-start | bytes 774148
  492.5 20.5 %copy-start.5 = (bf16[3,8,5376]{2,1,0:T(8,128)(2,1)S(1)}, bf16[3,8,5376]{2,1,0:T(8,128)(2,1)}, u32[]{:S(2)}) copy-start(bf16[3,8,5376]{2,1,0:T(8,128)(2,1)} %tail.5) | copy-start | bytes 774148
  495.3 90.6 %all-to-all-start.6 = ((bf16[8,3136,128]{2,1,0:T(8,128)(2,1)}), bf16[8,3136,128]{2,1,0:T(8,128)(2,1)}, u32[]{:S(2)}, u32[]{:S(2)}) async-start(bf16[8,3136,128]{2,1,0:T(8,128)(2,1)} %conv_pack.7), calls=%async_computation.6 | async-start | bytes 12845056 | tf_op jit(solution)/shard_map/all_to_all | solution.py:339
  515.0 75.9 %collective-permute-start.7 = (bf16[3,32,5376]{2,1,0:T(8,128)(2,1)}, bf16[3,32,5376]{2,1,0:T(8,128)(2,1)}, u32[]{:S(2)}, u32[]{:S(2)}) collective-permute-start(bf16[3,32,5376]{2,1,0:T(8,128)(2,1)} %pad_maximum_fusion.1), channel_id=1, source_target_pairs={{7,1},{15,9}} | collective-permute-start | bytes 3096584 | tf_op jit(solution)/shard_map/ppermute | solution.py:312
  518.1 20.6 %collective-permute-start.3 = (bf16[8,512,128]{2,1,0:T(8,128)(2,1)S(1)}, bf16[8,512,128]{2,1,0:T(8,128)(2,1)S(1)}, u32[]{:S(2)}, u32[]{:S(2)}) collective-permute-start(bf16[8,512,128]{2,1,0:T(8,128)(2,1)S(1)} %slice.123), channel_id=1, source_target_pairs={{0,1},{1,0},{2,3},{3,2},{4,5},{5,4},{6,7},{7,6},{8,9},{9,8},{10,11... | collective-permute-start | bytes 3145736 | tf_op jit(solution)/shard_map/ppermute | solution.py:346
  538.7 1.0 copy-start.8
  585.9 66.8 %all-to-all-start.4 = ((bf16[8,2560,128]{2,1,0:T(8,128)(2,1)}), bf16[8,2560,128]{2,1,0:T(8,128)(2,1)}, u32[]{:S(2)}, u32[]{:S(2)}) async-start(bf16[8,2560,128]{2,1,0:T(8,128)(2,1)} %get-tuple-element.37), calls=%async_computation.4 | async-start | bytes 10485760 | tf_op jit(solution)/shard_map/all_to_all | solution.py:348
  592.0 32.4 %collective-permute-start.8 = (bf16[3,32,5376]{2,1,0:T(8,128)(2,1)S(1)}, bf16[3,32,5376]{2,1,0:T(8,128)(2,1)S(1)}, u32[]{:S(2)}, u32[]{:S(2)}) collective-permute-start(bf16[3,32,5376]{2,1,0:T(8,128)(2,1)S(1)} %broadcast_select_fusion.1), channel_id=1, source_target_pairs={{7,5},{1,3},{15,13},{9,11}} | collective-permute-start | bytes 3096584 | tf_op jit(solution)/shard_map/ppermute | solution.py:312
  613.7 13.1 %collective-permute-start.9 = (bf16[8,512,128]{2,1,0:T(8,128)(2,1)S(1)}, bf16[8,512,128]{2,1,0:T(8,128)(2,1)S(1)}, u32[]{:S(2)}, u32[]{:S(2)}) collective-permute-start(bf16[8,512,128]{2,1,0:T(8,128)(2,1)S(1)} %slice.119), channel_id=1, source_target_pairs={{0,1},{1,0},{2,3},{3,2},{4,5},{5,4},{6,7},{7,6},{8,9},{9,8},{10,11... | collective-permute-start | bytes 3145736 | tf_op jit(solution)/shard_map/ppermute | solution.py:346
  626.7 1.0 copy-start.6
  652.8 94.8 %all-to-all-start.7 = ((bf16[8,2560,128]{2,1,0:T(8,128)(2,1)}), bf16[8,2560,128]{2,1,0:T(8,128)(2,1)}, u32[]{:S(2)}, u32[]{:S(2)}) async-start(bf16[8,2560,128]{2,1,0:T(8,128)(2,1)} %get-tuple-element.49), calls=%async_computation.7 | async-start | bytes 10485760 | tf_op jit(solution)/shard_map/all_to_all | solution.py:348
  686.6 34.0 %collective-permute-start.10 = (bf16[3,32,5376]{2,1,0:T(8,128)(2,1)S(1)}, bf16[3,32,5376]{2,1,0:T(8,128)(2,1)S(1)}, u32[]{:S(2)}, u32[]{:S(2)}) collective-permute-start(bf16[3,32,5376]{2,1,0:T(8,128)(2,1)S(1)} %broadcast_select_fusion.2), channel_id=1, source_target_pairs={{1,0},{3,2},{5,4},{7,6},{9,8},{11,10},{13,12},{15,14}} | collective-permute-start | bytes 3096584 | tf_op jit(solution)/shard_map/ppermute | solution.py:312

commit v3 on v2

--- a/solution.py
+++ b/solution.py
@@ -12,6 +12,11 @@
 EPSILON = 1e-5
 LANES = 128
 SIZES = (8, 8)
+
+
+def silu(values):
+    half = 0.5 * values
+    return half + half * jnp.tanh(half)
 
 
 def conv_kernel(n_prompts, seg_len, width, n_heads, x_ref, bc_ref, dtr_ref, xh_ref, bch_ref, wx_ref, wbc_ref, bx_ref, bbc_ref, dtb_ref, sel_ref, out_ref, bc_keep, dt_keep):
@@ -26,7 +31,7 @@
         for back in range(1, CONV_WIDTH):
             shifted = jnp.concatenate([halo[taps - back:], cur[:seg_len - back]], axis=0)
             acc = acc + shifted * w[taps - back:taps - back + 1]
-        return (acc * jax.nn.sigmoid(acc)).astype(jnp.bfloat16)
+        return silu(acc).astype(jnp.bfloat16)
 
     @pl.when(dest == 0)
     def _():
@@ -57,25 +62,27 @@
     out_ref[0, bc_start + n_prompts * seg_len:] = dt_keep[dest]
 
 
-def tail_kernel(n_prompts, seg_len, u_ref, out_ref):
+def tail_kernel(*refs):
     taps = CONV_WIDTH - 1
+    out_ref = refs[-1]
+    rows = [ref[...].astype(jnp.float32)[16 - taps:] for ref in refs[:-1]]
     for k in range(taps):
-        rows = [u_ref[(p + 1) * seg_len - 16:(p + 1) * seg_len].astype(jnp.float32)[16 - taps + k:17 - taps + k] for p in range(n_prompts)]
-        out_ref[k] = jnp.concatenate(rows, axis=0).astype(jnp.bfloat16)
+        out_ref[k] = jnp.concatenate([row[k:k + 1] for row in rows], axis=0).astype(jnp.bfloat16)
 
 
 def tail_call(u, n_prompts, seg_len, conv_dim):
     taps = CONV_WIDTH - 1
-    width = 6 * LANES
+    width = conv_dim // 2
+    step = seg_len // 16
     return pl.pallas_call(
-        functools.partial(tail_kernel, n_prompts, seg_len),
-        grid=(conv_dim // width,),
-        in_specs=[pl.BlockSpec((n_prompts * seg_len, width), lambda i: (0, i))],
+        tail_kernel,
+        grid=(2,),
+        in_specs=[pl.BlockSpec((16, width), lambda i, p=p: ((p + 1) * step - 1, i)) for p in range(n_prompts)],
         out_specs=pl.BlockSpec((taps, n_prompts, width), lambda i: (0, 0, i)),
         out_shape=jax.ShapeDtypeStruct((taps, n_prompts, conv_dim), jnp.bfloat16),
-        cost_estimate=pl.CostEstimate(flops=n_prompts * conv_dim * 100, bytes_accessed=2 * n_prompts * seg_len * conv_dim, transcendentals=0),
+        cost_estimate=pl.CostEstimate(flops=n_prompts * conv_dim * 100, bytes_accessed=40 * n_prompts * conv_dim, transcendentals=0),
         name='tail',
-    )(u)
+    )(*[u] * n_prompts)
 
 
 def conv_call(u, halo, conv_w, conv_b, dt_b, select, sizes):
@@ -240,37 +247,41 @@
     )(*operands)
 
 
-def gate_kernel(n_src, blocks, seg_len, y_ref, z_ref, w_ref, out_ref, keep):
-    total = jnp.zeros((seg_len, LANES), jnp.float32)
-    for d in range(n_src):
-        for j in range(blocks):
-            cols = slice((d * blocks + j) * LANES, (d * blocks + j + 1) * LANES)
-            z = z_ref[:, cols].astype(jnp.float32)
-            g = y_ref[d, j * seg_len:(j + 1) * seg_len].astype(jnp.float32) * (z * jax.nn.sigmoid(z))
-            keep[:, cols] = g
-            total = total + g * g
+def gate_kernel(n_src, blocks, seg_len, group, y_ref, z_ref, w_ref, out_ref, keep):
     width = n_src * blocks * LANES
-    scale = lax.rsqrt(jnp.sum(total, axis=1, keepdims=True) / width + EPSILON)
-    for i in range(n_src * blocks):
-        cols = slice(i * LANES, (i + 1) * LANES)
-        out_ref[:, cols] = (keep[:, cols] * scale * w_ref[:, cols]).astype(jnp.bfloat16)
+    for p in range(group):
+        rows = slice(p * seg_len, (p + 1) * seg_len)
+        total = jnp.zeros((seg_len, LANES), jnp.float32)
+        for d in range(n_src):
+            for j in range(blocks):
+                cols = slice((d * blocks + j) * LANES, (d * blocks + j + 1) * LANES)
+                z = z_ref[rows, cols].astype(jnp.float32)
+                y = y_ref[d, (p * blocks + j) * seg_len:(p * blocks + j + 1) * seg_len].astype(jnp.float32)
+                g = y * silu(z)
+                keep[p, :, cols] = g
+                total = total + g * g
+        scale = lax.rsqrt(jnp.sum(total, axis=1, keepdims=True) / width + EPSILON)
+        for i in range(n_src * blocks):
+            cols = slice(i * LANES, (i + 1) * LANES)
+            out_ref[rows, cols] = (keep[p, :, cols] * scale * w_ref[:, cols]).astype(jnp.bfloat16)
 
 
 def gate_call(y, u, gate_w, n_prompts, seg_len, d_inner):
     n_src = y.shape[0]
     blocks = d_inner // n_src // LANES
     tokens = n_prompts * seg_len
+    group = 2
     return pl.pallas_call(
-        functools.partial(gate_kernel, n_src, blocks, seg_len),
-        grid=(n_prompts,),
+        functools.partial(gate_kernel, n_src, blocks, seg_len, group),
+        grid=(n_prompts // group,),
         in_specs=[
-            pl.BlockSpec((n_src, blocks * seg_len, LANES), lambda p: (0, p, 0)),
-            pl.BlockSpec((seg_len, d_inner), lambda p: (p, 0)),
+            pl.BlockSpec((n_src, group * blocks * seg_len, LANES), lambda p: (0, p, 0)),
+            pl.BlockSpec((group * seg_len, d_inner), lambda p: (p, 0)),
             pl.BlockSpec((1, d_inner), lambda p: (0, 0)),
         ],
-        out_specs=pl.BlockSpec((seg_len, d_inner), lambda p: (p, 0)),
+        out_specs=pl.BlockSpec((group * seg_len, d_inner), lambda p: (p, 0)),
         out_shape=jax.ShapeDtypeStruct((tokens, d_inner), jnp.bfloat16),
-        scratch_shapes=[pltpu.VMEM((seg_len, d_inner), jnp.float32)],
+        scratch_shapes=[pltpu.VMEM((group, seg_len, d_inner), jnp.float32)],
         cost_estimate=pl.CostEstimate(flops=tokens * d_inner * 40, bytes_accessed=6 * tokens * d_inner, transcendentals=tokens * d_inner),
         name='gate',
     )(y, u, gate_w)
@@ -304,7 +315,8 @@
         finals = None
         starts = [sum(SIZES[:c]) for c in range(len(SIZES))]
         streams = [resid[starts[c]:starts[c] + SIZES[c]].reshape(SIZES[c] * seg_len, d_model) for c in range(len(SIZES))]
-        tails = [[] for _ in range(layers)]
+        tails = []
+        resid_halo = lax.ppermute(jnp.swapaxes(resid[:, seg_len - taps:], 0, 1), 'sp', forward_pairs)
         last_seg = seg_count - 1
         hops = [[(last_seg, 1)], [(last_seg, last_seg - 2), (1, 3)], [(source, source - 1) for source in range(1, seg_count, 2)]]
 
@@ -320,20 +332,30 @@
             d_wide = jnp.repeat(lax.dynamic_slice_in_dim(d_skip[l], seg_index * n_local, n_local), head_dim)[None]
             packs, gates = [], []
             for c, n_prompts in enumerate(SIZES):
-                if c > 0:
-                    streams[c], tails[l][c - 1] = lax.optimization_barrier((streams[c], tails[l][c - 1]))
                 r = streams[c]
-                h = (r * lax.rsqrt(jnp.mean(r * r, axis=-1, keepdims=True) + EPSILON) * pre_norm[l]).astype(jnp.bfloat16)
-                u = jnp.dot(h, w_in[l, :, d_inner:], preferred_element_type=jnp.float32).astype(jnp.bfloat16)
+                tokens = n_prompts * seg_len
+                mean_sq = jnp.mean(r * r, axis=-1, keepdims=True)
+                if tails:
+                    mean_sq, tails[-1] = lax.optimization_barrier((mean_sq, tails[-1]))
+                h = (r * lax.rsqrt(mean_sq + EPSILON) * pre_norm[l]).astype(jnp.bfloat16)
+                rows = h
+                if l == 0:
+                    early = resid_halo[:, starts[c]:starts[c] + n_prompts].reshape(taps * n_prompts, d_model)
+                    early = early * lax.rsqrt(jnp.mean(early * early, axis=-1, keepdims=True) + EPSILON) * pre_norm[l]
+                    rows = jnp.concatenate([h, early.astype(jnp.bfloat16)], axis=0)
+                u = jnp.dot(rows, w_in[l, :, d_inner:], preferred_element_type=jnp.float32).astype(jnp.bfloat16)
                 tail = tail_call(u, n_prompts, seg_len, conv_dim)
-                tails[l].append(tail)
-                halo = lax.ppermute(tail, 'sp', forward_pairs)
+                tails.append(tail)
+                if l == 0:
+                    halo = u[tokens:, :conv_dim].reshape(taps, n_prompts, conv_dim)
+                else:
+                    halo = lax.ppermute(tail, 'sp', forward_pairs)
                 packed = conv_call(u, halo, conv_wt[l], conv_b[l:l + 1], dt_bias_wide[l:l + 1], select, (n_prompts, seg_len, d_inner, conv_dim, n_heads, seg_count))
                 packed, h = lax.optimization_barrier((packed, h))
                 packs.append(packed)
                 gates.append(jnp.dot(h, w_in[l, :, :d_inner], preferred_element_type=jnp.float32).astype(jnp.bfloat16))
             if final_layer:
-                tail_rows = jnp.concatenate([rows for layer_rows in tails for rows in layer_rows], axis=1)
+                tail_rows = jnp.concatenate(tails, axis=1)
             outs, arrived = [], []
             for c in range(len(SIZES)):
                 arrived.append(lax.all_to_all(packs[c], 'sp', 0, 0, tiled=True))
@@ -347,13 +369,18 @@
                 y, finals = scan_call(parity, packed, other, a_neg, d_wide, finals, (l, starts[c]), (n_prompts, seg_len, seg_count, n_local, head_dim, d_state, batch, layers))
                 y = lax.all_to_all(y, 'sp', 0, 0, tiled=True)
                 if final_layer and c >= len(SIZES) - 2:
-                    y, tail_rows = lax.optimization_barrier((y, spread(tail_rows, hops[c - len(SIZES) + 3])))
+                    if c == len(SIZES) - 1:
+                        tail_rows = spread(tail_rows, hops[1])
+                    y, tail_rows = lax.optimization_barrier((y, tail_rows))
                 outs.append(y)
             for c, n_prompts in enumerate(SIZES):
                 g = gate_call(outs[c], gates[c], gate_norm[l], n_prompts, seg_len, d_inner)
                 streams[c] = streams[c] + jnp.dot(g, w_out[l], preferred_element_type=jnp.float32)
-        out = jnp.concatenate(streams, axis=0).reshape(batch, seg_len, d_model)
-        conv_state = tail_rows.reshape(taps, layers, batch, conv_dim)
+        out = jnp.zeros((batch * seg_len, d_model), jnp.float32)
+        for c in range(len(SIZES)):
+            out = lax.optimization_barrier(lax.dynamic_update_slice(out, streams[c], (starts[c] * seg_len, 0)))
+        out = out.reshape(batch, seg_len, d_model)
+        conv_state = spread(tail_rows, hops[2]).reshape(taps, layers, batch, conv_dim)
         return out, finals, jnp.transpose(conv_state, (2, 1, 3, 0))
 
     return jax.shard_map(forward, mesh=mesh, in_specs=(P('dp', 'sp', None), P(), P(), P(), P(), P(), P(), P(), P(), P()), out_specs=(P('dp', 'sp', None), P('dp', None, 'sp', None, None), P('dp', None, None, None)), check_vma=False)

time: 803 us -> 748 us (0.932)
  the two profiles are of different devices: /device:TPU:112 before, /device:TPU:117 now
where the time goes in v3:
time: 748 us; the launch traced here: 739 us
  matrix products  259 us (35%)
  Pallas kernels  175 us (23%)
  waiting for transfers between devices  172 us (23%)
  starting transfers between devices  71.8 us (10%)
  local copies, waits for them, and re-layouts  35.8 us (5%)
  other arithmetic  25.1 us (3%)
    all_to_all x4, waiting for transfers between devices, forward(): arrived.append(lax.all_to_all(packs[c], 'sp', 0, 0, tiled=True))  113 us
    dot_general x4, matrix products, forward(): jnp.dot(g, w_out[l], preferred_element_type=jnp.float32)  90 us
    dot_general x4, matrix products, forward(): jnp.dot(rows, w_in[l, :, d_inner:], preferred_element_type=jnp.float32)  89.9 us
    pallas_call x4, Pallas kernels, scan_call(): pl.pallas_call(body, grid=(n_prompts,), in_specs=in_specs, out_specs=[pl....  83.7 us
    dot_general x4, matrix products, forward(): jnp.dot(h, w_in[l, :, :d_inner], preferred_element_type=jnp.float32)  78.8 us
    pallas_call x4, Pallas kernels, conv_call(): pl.pallas_call(body, grid=(n_dest,), in_specs=[pl.BlockSpec((tokens, widt...  47.5 us
    pallas_call x4, Pallas kernels, gate_call(): pl.pallas_call(functools.partial(gate_kernel, n_src, blocks, seg_len, gro...  34.7 us
    all_to_all x4, starting transfers between devices, forward(): y = lax.all_to_all(y, 'sp', 0, 0, tiled=True)  31.1 us
  transfers between devices with their start and end apart: 18, of which 7 were waited for; matrix products, arithmetic and copies ran while one was open for 38% of the time, Pallas kernels for 20%

profile of v3, /device:TPU:117, one launch (start us, length us, event | category | flops | bytes accessed | tf_op | source)
XLA Modules:
  0.0 739.2 jit_solution(5351901495679587312)
XLA Ops:
  0.6 1.5 slice.113
  3.0 3.6 collective-permute-start
  6.6 8.4 %multiply_reduce_fusion.1 = (f32[8,64]{1,0:T(8,128)S(1)}, f32[8,64]{1,0:T(8,128)S(1)}, f32[8,64,2560]{2,1,0:T(8,128)}, f32[8,64,2560]{2,1,0:T(8,128)}) fusion(f32[16,64,2560]{2,1,0:T(8,128)} %param.10), kind=kLoop, calls=%fused_computation.56 | loop fusion | flops 5241856 | bytes 20975616 | tf_op jit(solution)/shard_map/reduce_sum | solution.py:337
  17.1 3.0 fusion.63
  22.2 22.7 %fusion.36.x_ref.bc_ref.dtr_ref.refs_0_.refs_1_.refs_2_.refs_3_.refs_4_.refs_5_.refs_6_.refs_7_ = bf16[536,5456]{1,0:T(8,128)(2,1)} fusion(bf16[2,2560,10576]{1,2,0:T(8,128)(2,1)} %param.12, bf16[24,2560]{1,0:T(8,128)(2,1)S(1)} %get-tuple-element.68, bf16[512,2560]{1,0:T(8,128)(2,1)S(1)} %fusion.63), kind=kOutput, calls=%fused_computation.36 | convolution fusion | flops 14981423104 | bytes 36527872 | tf_op jit(solution)/shard_map/dot_general | solution.py:346
  44.9 1.7 slice_bitcast_fusion.1.xh_ref.bch_ref
  46.5 11.9 %conv_pack.4 = bf16[8,3136,128]{2,1,0:T(8,128)(2,1)} custom-call(bf16[536,5456]{1,0:T(8,128)(2,1)} %fusion.36.x_ref.bc_ref.dtr_ref.refs_0_.refs_1_.refs_2_.refs_3_.refs_4_.refs_5_.refs_6_.refs_7_, bf16[536,5456]{1,0:T(8,128)(2,1)} %fusion.36.x_ref.bc_ref.dtr_ref.refs_0_.refs_1_.refs_2_.refs_3_.refs_4_.refs_5_.refs_6_.refs_7_, ...), custom_call_target="tpu_custom_call" | custom-call | flops 157286400 | bytes 10485760 | tf_op jit(solution)/shard_map/conv_pack/pallas_call | solution.py:100
  58.4 5.3 all-to-all-start
  63.7 2.2 tail.4
  66.0 4.5 fusion.61
  70.5 23.4 %fusion.39.refs_0_.refs_1_.refs_2_.refs_3_.refs_4_.refs_5_.refs_6_.refs_7_.x_ref.bc_ref.dtr_ref = bf16[536,5456]{1,0:T(8,128)(2,1)} fusion(bf16[2,2560,10576]{1,2,0:T(8,128)(2,1)} %param.12, bf16[24,2560]{1,0:T(8,128)(2,1)S(1)} %get-tuple-element.67, bf16[512,2560]{1,0:T(8,128)(2,1)} %fusion.61), kind=kOutput, calls=%fused_computation.37 | convolution fusion | flops 14981423104 | bytes 36527872 | tf_op jit(solution)/shard_map/dot_general | solution.py:346
  93.9 1.7 slice_bitcast_fusion.xh_ref.bch_ref
  95.6 11.9 %conv_pack.6 = bf16[8,3136,128]{2,1,0:T(8,128)(2,1)} custom-call(bf16[536,5456]{1,0:T(8,128)(2,1)} %fusion.39.refs_0_.refs_1_.refs_2_.refs_3_.refs_4_.refs_5_.refs_6_.refs_7_.x_ref.bc_ref.dtr_ref, bf16[536,5456]{1,0:T(8,128)(2,1)} %fusion.39.refs_0_.refs_1_.refs_2_.refs_3_.refs_4_.refs_5_.refs_6_.refs_7_.x_ref.bc_ref.dtr_ref, ...), custom_call_target="tpu_custom_call" | custom-call | flops 157286400 | bytes 10485760 | tf_op jit(solution)/shard_map/conv_pack/pallas_call | solution.py:100
  107.5 26.5 %all-to-all-done.x_ref.mine_ref.dt_ref = bf16[8,3136,128]{2,1,0:T(8,128)(2,1)} async-done(((bf16[8,3136,128]{2,1,0:T(8,128)(2,1)}), bf16[8,3136,128]{2,1,0:T(8,128)(2,1)}, u32[]{:S(2)}, u32[]{:S(2)}) %all-to-all-start) | async-done | bytes 6422560 | tf_op jit(solution)/shard_map/all_to_all | solution.py:361
  134.0 7.8 %all-to-all-start.3 = ((bf16[8,3136,128]{2,1,0:T(8,128)(2,1)}), bf16[8,3136,128]{2,1,0:T(8,128)(2,1)}, u32[]{:S(2)}, u32[]{:S(2)}) async-start(bf16[8,3136,128]{2,1,0:T(8,128)(2,1)} %conv_pack.6), calls=%async_computation.3 | async-start | bytes 12845056 | tf_op jit(solution)/shard_map/all_to_all | solution.py:361
  141.9 2.3 slice.145
  147.8 20.8 %scan.4 = (bf16[8,2560,128]{2,1,0:T(8,128)(2,1)}, f32[16,2,10,64,128]{4,3,2,1,0:T(8,128)}) custom-call(s32[1]{0:T(128)} %bitcast.1.par_ref, bf16[8,3136,128]{2,1,0:T(8,128)(2,1)} %all-to-all-done.x_ref.mine_ref.dt_ref, bf16[8,3136,128]{2,1,0:T(8,128)(2,1)} %all-to-all-done.x_ref.mine_ref.dt_ref, bf16[8,512,128]{2,1,0:T(8,128)(2,1)} %collective-permute-done.1.other_ref, ...), custom_call_target="tpu_custom_call" | custom-call | flops 655360000 | bytes 15728640 | tf_op jit(solution)/shard_map/scan/pallas_call | solution.py:231
  168.6 43.3 %all-to-all-done.3.x_ref.mine_ref.dt_ref = bf16[8,3136,128]{2,1,0:T(8,128)(2,1)} async-done(((bf16[8,3136,128]{2,1,0:T(8,128)(2,1)}), bf16[8,3136,128]{2,1,0:T(8,128)(2,1)}, u32[]{:S(2)}, u32[]{:S(2)}) %all-to-all-start.3) | async-done | bytes 6422560 | tf_op jit(solution)/shard_map/all_to_all | solution.py:361
  211.9 8.3 %all-to-all-start.1 = ((bf16[8,2560,128]{2,1,0:T(8,128)(2,1)}), bf16[8,2560,128]{2,1,0:T(8,128)(2,1)}, u32[]{:S(2)}, u32[]{:S(2)}) async-start(bf16[8,2560,128]{2,1,0:T(8,128)(2,1)} %get-tuple-element.32), calls=%async_computation.1 | async-start | bytes 10485760 | tf_op jit(solution)/shard_map/all_to_all | solution.py:370
  220.9 2.3 slice.150
  223.5 19.6 %fusion.48.z_ref = bf16[512,5120]{1,0:T(8,128)(2,1)} fusion(bf16[512,2560]{1,0:T(8,128)(2,1)S(1)} %fusion.63, bf16[2,2560,10576]{1,2,0:T(8,128)(2,1)} %param.12), kind=kOutput, calls=%fused_computation.40 | convolution fusion | flops 13424394240 | bytes 34078720 | tf_op jit(solution)/shard_map/dot_general | solution.py:356
  243.1 2.2 tail.5
  245.4 21.1 %scan.5 = (bf16[8,2560,128]{2,1,0:T(8,128)(2,1)}, f32[16,2,10,64,128]{4,3,2,1,0:T(8,128)}) custom-call(s32[1]{0:T(128)} %bitcast.1.par_ref, bf16[8,3136,128]{2,1,0:T(8,128)(2,1)} %all-to-all-done.3.x_ref.mine_ref.dt_ref, bf16[8,3136,128]{2,1,0:T(8,128)(2,1)} %all-to-all-done.3.x_ref.mine_ref.dt_ref, ...), custom_call_target="tpu_custom_call", output_to_operand_aliasing={{1}: (7, {})} | custom-call | flops 655360000 | bytes 15728640 | tf_op jit(solution)/shard_map/scan/pallas_call | solution.py:231
  266.4 11.3 %all-to-all-done.1.y_ref = bf16[8,2560,128]{2,1,0:T(8,128)(2,1)} async-done(((bf16[8,2560,128]{2,1,0:T(8,128)(2,1)}), bf16[8,2560,128]{2,1,0:T(8,128)(2,1)}, u32[]{:S(2)}, u32[]{:S(2)}) %all-to-all-start.1) | async-done | bytes 5242912 | tf_op jit(solution)/shard_map/all_to_all | solution.py:370
  277.7 8.5 %all-to-all-start.5 = ((bf16[8,2560,128]{2,1,0:T(8,128)(2,1)}), bf16[8,2560,128]{2,1,0:T(8,128)(2,1)}, u32[]{:S(2)}, u32[]{:S(2)}) async-start(bf16[8,2560,128]{2,1,0:T(8,128)(2,1)} %get-tuple-element.41), calls=%async_computation.5 | async-start | bytes 10485760 | tf_op jit(solution)/shard_map/all_to_all | solution.py:370
  286.2 8.6 %gate.4 = bf16[512,5120]{1,0:T(8,128)(2,1)} custom-call(bf16[8,2560,128]{2,1,0:T(8,128)(2,1)} %all-to-all-done.1.y_ref, bf16[512,5120]{1,0:T(8,128)(2,1)} %fusion.48.z_ref, f32[1,5120]{1,0:T(1,128)} %get-tuple-element.74.w_ref), custom_call_target="tpu_custom_call" | custom-call | flops 104857600 | bytes 15728640 | tf_op jit(solution)/shard_map/gate/pallas_call | solution.py:274
  294.9 22.7 %multiply_reduce_fusion.2 = (f32[512]{0:T(512)S(1)}, f32[512,2560]{1,0:T(8,128)}) fusion(bf16[512,5120]{1,0:T(8,128)(2,1)} %gate.4, bf16[2,5120,2560]{2,1,0:T(8,128)(2,1)} %param.19, f32[8,64,2560]{2,1,0:T(8,128)} %get-tuple-element.66), kind=kOutput, calls=%fused_computation.57 | convolution fusion | flops 13425704960 | bytes 41945088 | tf_op jit(solution)/shard_map/dot_general | solution.py:378
  317.6 3.0 multiply_convert_fusion.1
  320.7 1.5 copy-done.1
  322.2 21.9 %fusion.42.refs_0_.refs_1_.refs_2_.refs_3_.refs_4_.refs_5_.refs_6_.refs_7_.x_ref.bc_ref.dtr_ref = bf16[512,5456]{1,0:T(8,128)(2,1)} fusion(bf16[512,2560]{1,0:T(8,128)(2,1)S(1)} %multiply_convert_fusion.1, bf16[2,2560,10576]{1,2,0:T(8,128)(2,1)} %param.12), kind=kOutput, calls=%fused_computation.38 | convolution fusion | flops 14305370112 | bytes 36143104 | tf_op jit(solution)/shard_map/dot_general | solution.py:346
  344.0 2.3 tail.6
  346.4 3.5 collective-permute-start.2
  349.9 19.6 %fusion.51.z_ref = bf16[512,5120]{1,0:T(8,128)(2,1)} fusion(bf16[512,2560]{1,0:T(8,128)(2,1)S(1)} %copy-done, bf16[2,2560,10576]{1,2,0:T(8,128)(2,1)} %param.12), kind=kOutput, calls=%fused_computation.41 | convolution fusion | flops 13424394240 | bytes 34078720 | tf_op jit(solution)/shard_map/dot_general | solution.py:356
  369.5 8.7 %gate.5 = bf16[512,5120]{1,0:T(8,128)(2,1)} custom-call(bf16[8,2560,128]{2,1,0:T(8,128)(2,1)} %all-to-all-done.5.y_ref, bf16[512,5120]{1,0:T(8,128)(2,1)} %fusion.51.z_ref, f32[1,5120]{1,0:T(1,128)} %get-tuple-element.74.w_ref), custom_call_target="tpu_custom_call" | custom-call | flops 104857600 | bytes 15728640 | tf_op jit(solution)/shard_map/gate/pallas_call | solution.py:274
  378.9 11.8 %conv_pack.5 = bf16[8,3136,128]{2,1,0:T(8,128)(2,1)} custom-call(bf16[512,5456]{1,0:T(8,128)(2,1)} %fusion.42.refs_0_.refs_1_.refs_2_.refs_3_.refs_4_.refs_5_.refs_6_.refs_7_.x_ref.bc_ref.dtr_ref, bf16[512,5456]{1,0:T(8,128)(2,1)} %fusion.42.refs_0_.refs_1_.refs_2_.refs_3_.refs_4_.refs_5_.refs_6_.refs_7_.x_ref.bc_ref.dtr_ref, ...), custom_call_target="tpu_custom_call" | custom-call | flops 157286400 | bytes 10485760 | tf_op jit(solution)/shard_map/conv_pack/pallas_call | solution.py:100
  390.7 4.8 all-to-all-start.2
  395.6 22.6 %multiply_reduce_fusion = (f32[512]{0:T(512)S(1)}, f32[512,2560]{1,0:T(8,128)}) fusion(bf16[512,5120]{1,0:T(8,128)(2,1)} %gate.5, bf16[2,5120,2560]{2,1,0:T(8,128)(2,1)} %param.19, f32[8,64,2560]{2,1,0:T(8,128)} %get-tuple-element.65), kind=kOutput, calls=%fused_computation.54 | convolution fusion | flops 13425704960 | bytes 41945088 | tf_op jit(solution)/shard_map/dot_general | solution.py:378
  418.2 3.0 multiply_convert_fusion
  421.2 1.6 copy-done.3
  422.7 21.9 %fusion.45.refs_0_.refs_1_.refs_2_.refs_3_.refs_4_.refs_5_.refs_6_.refs_7_.x_ref.bc_ref.dtr_ref = bf16[512,5456]{1,0:T(8,128)(2,1)} fusion(bf16[512,2560]{1,0:T(8,128)(2,1)S(1)} %multiply_convert_fusion, bf16[2,2560,10576]{1,2,0:T(8,128)(2,1)} %param.12), kind=kOutput, calls=%fused_computation.39 | convolution fusion | flops 14305370112 | bytes 36143104 | tf_op jit(solution)/shard_map/dot_general | solution.py:346
  444.6 2.2 tail.7
  446.9 2.8 collective-permute-start.5
  449.7 18.2 %collective-permute-done.5.xh_ref.bch_ref = bf16[3,8,5376]{2,1,0:T(8,128)(2,1)S(1)} collective-permute-done((bf16[3,8,5376]{2,1,0:T(8,128)(2,1)}, bf16[3,8,5376]{2,1,0:T(8,128)(2,1)S(1)}, u32[]{:S(2)}, u32[]{:S(2)}) %collective-permute-start.5) | collective-permute-done | bytes 258080 | tf_op jit(solution)/shard_map/ppermute | solution.py:352
  468.5 11.9 %conv_pack.7 = bf16[8,3136,128]{2,1,0:T(8,128)(2,1)} custom-call(bf16[512,5456]{1,0:T(8,128)(2,1)} %fusion.45.refs_0_.refs_1_.refs_2_.refs_3_.refs_4_.refs_5_.refs_6_.refs_7_.x_ref.bc_ref.dtr_ref, bf16[512,5456]{1,0:T(8,128)(2,1)} %fusion.45.refs_0_.refs_1_.refs_2_.refs_3_.refs_4_.refs_5_.refs_6_.refs_7_.x_ref.bc_ref.dtr_ref, ...), custom_call_target="tpu_custom_call" | custom-call | flops 157286400 | bytes 10485760 | tf_op jit(solution)/shard_map/conv_pack/pallas_call | solution.py:100
  480.5 6.1 all-to-all-start.6
  486.6 1.3 slice.148
  490.3 1.8 collective-permute-start.6
  493.0 20.8 %scan.6 = (bf16[8,2560,128]{2,1,0:T(8,128)(2,1)}, f32[16,2,10,64,128]{4,3,2,1,0:T(8,128)}) custom-call(s32[1]{0:T(128)} %bitcast.1.par_ref, bf16[8,3136,128]{2,1,0:T(8,128)(2,1)} %all-to-all-done.2.x_ref.mine_ref.dt_ref, bf16[8,3136,128]{2,1,0:T(8,128)(2,1)} %all-to-all-done.2.x_ref.mine_ref.dt_ref, ...), custom_call_target="tpu_custom_call", output_to_operand_aliasing={{1}: (7, {})} | custom-call | flops 655360000 | bytes 15728640 | tf_op jit(solution)/shard_map/scan/pallas_call | solution.py:231
  513.9 43.1 %all-to-all-done.6.x_ref.mine_ref.dt_ref = bf16[8,3136,128]{2,1,0:T(8,128)(2,1)} async-done(((bf16[8,3136,128]{2,1,0:T(8,128)(2,1)}), bf16[8,3136,128]{2,1,0:T(8,128)(2,1)}, u32[]{:S(2)}, u32[]{:S(2)}) %all-to-all-start.6) | async-done | bytes 6422560 | tf_op jit(solution)/shard_map/all_to_all | solution.py:361
  556.9 8.3 %all-to-all-start.4 = ((bf16[8,2560,128]{2,1,0:T(8,128)(2,1)}), bf16[8,2560,128]{2,1,0:T(8,128)(2,1)}, u32[]{:S(2)}, u32[]{:S(2)}) async-start(bf16[8,2560,128]{2,1,0:T(8,128)(2,1)} %get-tuple-element.40), calls=%async_computation.4 | async-start | bytes 10485760 | tf_op jit(solution)/shard_map/all_to_all | solution.py:370
  565.3 19.8 %fusion.54.z_ref = bf16[512,5120]{1,0:T(8,128)(2,1)} fusion(bf16[512,2560]{1,0:T(8,128)(2,1)S(1)} %copy-done.2, bf16[2,2560,10576]{1,2,0:T(8,128)(2,1)} %param.12), kind=kOutput, calls=%fused_computation.42 | convolution fusion | flops 13424394240 | bytes 34078720 | tf_op jit(solution)/shard_map/dot_general | solution.py:356
  585.3 1.3 slice.141
  587.1 19.8 %fusion.57.z_ref = bf16[512,5120]{1,0:T(8,128)(2,1)} fusion(bf16[512,2560]{1,0:T(8,128)(2,1)S(1)} %copy-done.4, bf16[2,2560,10576]{1,2,0:T(8,128)(2,1)} %param.12), kind=kOutput, calls=%fused_computation.43 | convolution fusion | flops 13424394240 | bytes 34078720 | tf_op jit(solution)/shard_map/dot_general | solution.py:356
  607.9 21.0 %scan.7 = (bf16[8,2560,128]{2,1,0:T(8,128)(2,1)}, f32[16,2,10,64,128]{4,3,2,1,0:T(8,128)}) custom-call(s32[1]{0:T(128)} %bitcast.1.par_ref, bf16[8,3136,128]{2,1,0:T(8,128)(2,1)} %all-to-all-done.6.x_ref.mine_ref.dt_ref, bf16[8,3136,128]{2,1,0:T(8,128)(2,1)} %all-to-all-done.6.x_ref.mine_ref.dt_ref, ...), custom_call_target="tpu_custom_call", output_to_operand_aliasing={{1}: (7, {})} | custom-call | flops 655360000 | bytes 15728640 | tf_op jit(solution)/shard_map/scan/pallas_call | solution.py:231
  628.9 6.0 all-to-all-start.7
  634.9 1.5 collective-permute-start.8
  636.4 8.6 %gate.6 = bf16[512,5120]{1,0:T(8,128)(2,1)} custom-call(bf16[8,2560,128]{2,1,0:T(8,128)(2,1)} %all-to-all-done.4.y_ref, bf16[512,5120]{1,0:T(8,128)(2,1)} %fusion.54.z_ref, f32[1,5120]{1,0:T(1,128)} %get-tuple-element.73.w_ref), custom_call_target="tpu_custom_call" | custom-call | flops 104857600 | bytes 15728640 | tf_op jit(solution)/shard_map/gate/pallas_call | solution.py:274
  645.1 22.3 %fusion.68 = f32[512,2560]{1,0:T(8,128)} fusion(f32[512,2560]{1,0:T(8,128)} %get-tuple-element.82, bf16[512,5120]{1,0:T(8,128)(2,1)} %gate.6, bf16[2,5120,2560]{2,1,0:T(8,128)(2,1)} %param.19), kind=kOutput, calls=%fused_computation.59 | convolution fusion | flops 13423083520 | bytes 41943040 | tf_op jit(solution)/shard_map/dot_general | solution.py:378
  667.4 8.0 %dynamic_update_slice.6 = f32[1024,2560]{1,0:T(8,128)} pad(f32[512,2560]{1,0:T(8,128)} %fusion.68, f32[]{:T(128)} %constant.65.clone.1), padding=0_512x0_0 | pad | bytes 15728644 | tf_op jit(solution)/shard_map/dynamic_update_slice | solution.py:381
  675.4 28.8 %collective-permute-done.8 = bf16[3,32,5376]{2,1,0:T(8,128)(2,1)S(1)} collective-permute-done((bf16[3,32,5376]{2,1,0:T(8,128)(2,1)S(1)}, bf16[3,32,5376]{2,1,0:T(8,128)(2,1)S(1)}, u32[]{:S(2)}, u32[]{:S(2)}) %collective-permute-start.8) | collective-permute-done | bytes 1032224 | tf_op jit(solution)/shard_map/ppermute | solution.py:324
  704.4 1.6 collective-permute-start.9
  706.0 8.7 %gate.7 = bf16[512,5120]{1,0:T(8,128)(2,1)} custom-call(bf16[8,2560,128]{2,1,0:T(8,128)(2,1)} %all-to-all-done.7.y_ref, bf16[512,5120]{1,0:T(8,128)(2,1)} %fusion.57.z_ref, f32[1,5120]{1,0:T(1,128)} %get-tuple-element.73.w_ref), custom_call_target="tpu_custom_call" | custom-call | flops 104857600 | bytes 15728640 | tf_op jit(solution)/shard_map/gate/pallas_call | solution.py:274
  714.7 22.3 %add_dynamic-update-slice_fusion = f32[1024,2560]{1,0:T(8,128)} fusion(f32[1024,2560]{1,0:T(8,128)} %dynamic_update_slice.6, f32[512,2560]{1,0:T(8,128)} %get-tuple-element.84, bf16[512,5120]{1,0:T(8,128)(2,1)} %gate.7, bf16[2,5120,2560]{2,1,0:T(8,128)(2,1)} %param.19), kind=kOutput, calls=%fused_computation.52 | convolution fusion | flops 13423083520 | bytes 41943040 | tf_op jit(solution)/shard_map/dot_general | solution.py:378
  737.2 1.8 copy.36
  (104 shorter events, 16.5 us)
Async XLA Ops:
  3.0 12.0 %copy-start.18 = (f32[2,2560]{1,0:T(2,128)S(1)}, f32[2,2560]{1,0:T(2,128)}, u32[]{:S(2)}) copy-start(f32[2,2560]{1,0:T(2,128)} %param.11) | copy-start | bytes 61444
  3.0 12.7 %copy-start.14 = (f32[2,5376,4]{1,2,0:T(4,128)S(1)}, f32[2,5376,4]{1,2,0:T(4,128)}, u32[]{:S(2)}) copy-start(f32[2,5376,4]{1,2,0:T(4,128)} %param.13) | copy-start | bytes 516100
  3.0 13.4 %copy-start.16 = (f32[2,5376]{1,0:T(2,128)S(1)}, f32[2,5376]{1,0:T(2,128)}, u32[]{:S(2)}) copy-start(f32[2,5376]{1,0:T(2,128)} %param.14) | copy-start | bytes 129028
  3.0 18.4 %collective-permute-start = (f32[3,16,2560]{2,1,0:T(8,128)}, f32[3,16,2560]{2,1,0:T(8,128)S(1)}, u32[]{:S(2)}, u32[]{:S(2)}) collective-permute-start(f32[3,16,2560]{2,1,0:T(8,128)} %bitcast.128), channel_id=1, source_target_pairs={{0,1},{1,2},{2,3},{3,4},{4,5},{5,6},{6,7},{8,9},{9,10},{10,11},{11... | collective-permute-start | bytes 1474568 | tf_op jit(solution)/shard_map/ppermute | solution.py:319
  15.1 5.1 copy-start.20
  58.4 75.6 %all-to-all-start = ((bf16[8,3136,128]{2,1,0:T(8,128)(2,1)}), bf16[8,3136,128]{2,1,0:T(8,128)(2,1)}, u32[]{:S(2)}, u32[]{:S(2)}) async-start(bf16[8,3136,128]{2,1,0:T(8,128)(2,1)} %conv_pack.4), calls=%async_computation | async-start | bytes 12845056 | tf_op jit(solution)/shard_map/all_to_all | solution.py:361
  107.5 37.0 %copy-start.21 = (f32[2,80]{1,0:T(2,128)S(1)}, f32[2,80]{1,0:T(2,128)}, u32[]{:S(2)}) copy-start(f32[2,80]{1,0:T(2,128)} %param.17) | copy-start | bytes 1924
  107.5 38.4 %copy-start.22 = (f32[2,80]{1,0:T(2,128)S(1)}, f32[2,80]{1,0:T(2,128)}, u32[]{:S(2)}) copy-start(f32[2,80]{1,0:T(2,128)} %param.16) | copy-start | bytes 1924
  134.0 77.9 %all-to-all-start.3 = ((bf16[8,3136,128]{2,1,0:T(8,128)(2,1)}), bf16[8,3136,128]{2,1,0:T(8,128)(2,1)}, u32[]{:S(2)}, u32[]{:S(2)}) async-start(bf16[8,3136,128]{2,1,0:T(8,128)(2,1)} %conv_pack.6), calls=%async_computation.3 | async-start | bytes 12845056 | tf_op jit(solution)/shard_map/all_to_all | solution.py:361
  144.1 3.0 collective-permute-start.1
  211.9 8.3 %copy-start.17 = (f32[2,1,5120]{2,1,0:T(1,128)S(1)}, f32[2,1,5120]{2,1,0:T(1,128)}, u32[]{:S(2)}) copy-start(f32[2,1,5120]{2,1,0:T(1,128)} %param.18) | copy-start | bytes 122884
  211.9 65.8 %all-to-all-start.1 = ((bf16[8,2560,128]{2,1,0:T(8,128)(2,1)}), bf16[8,2560,128]{2,1,0:T(8,128)(2,1)}, u32[]{:S(2)}, u32[]{:S(2)}) async-start(bf16[8,2560,128]{2,1,0:T(8,128)(2,1)} %get-tuple-element.32), calls=%async_computation.1 | async-start | bytes 10485760 | tf_op jit(solution)/shard_map/all_to_all | solution.py:370
  223.1 22.2 %collective-permute-start.4 = (bf16[8,512,128]{2,1,0:T(8,128)(2,1)}, bf16[8,512,128]{2,1,0:T(8,128)(2,1)}, u32[]{:S(2)}, u32[]{:S(2)}) collective-permute-start(bf16[8,512,128]{2,1,0:T(8,128)(2,1)} %slice.150), channel_id=1, source_target_pairs={{0,1},{1,0},{2,3},{3,2},{4,5},{5,4},{6,7},{7,6},{8,9},{9,8},{10,11... | collective-permute-start | bytes 3145736 | tf_op jit(solution)/shard_map/ppermute | solution.py:368
  277.7 91.8 %all-to-all-start.5 = ((bf16[8,2560,128]{2,1,0:T(8,128)(2,1)}), bf16[8,2560,128]{2,1,0:T(8,128)(2,1)}, u32[]{:S(2)}, u32[]{:S(2)}) async-start(bf16[8,2560,128]{2,1,0:T(8,128)(2,1)} %get-tuple-element.41), calls=%async_computation.5 | async-start | bytes 10485760 | tf_op jit(solution)/shard_map/all_to_all | solution.py:370
  294.9 22.8 %copy-start.15 = (f32[2560]{0:T(1024)S(1)}, f32[2560]{0:T(1024)}, u32[]{:S(2)}) copy-start(f32[2560]{0:T(1024)} %get-tuple-element.63) | copy-start | bytes 30724
  320.6 1.5 copy-start.1
  344.0 5.9 copy-start
  346.4 31.8 %collective-permute-start.2 = (bf16[3,8,5376]{2,1,0:T(8,128)(2,1)}, bf16[3,8,5376]{2,1,0:T(8,128)(2,1)S(1)}, u32[]{:S(2)}, u32[]{:S(2)}) collective-permute-start(bf16[3,8,5376]{2,1,0:T(8,128)(2,1)} %tail.6), channel_id=1, source_target_pairs={{0,1},{1,2},{2,3},{3,4},{4,5},{5,6},{6,7},{8,9},{9,10},{10,11},{11... | collective-permute-start | bytes 774152 | tf_op jit(solution)/shard_map/ppermute | solution.py:352
  378.2 0.7 copy-start.12
  390.7 89.7 %all-to-all-start.2 = ((bf16[8,3136,128]{2,1,0:T(8,128)(2,1)}), bf16[8,3136,128]{2,1,0:T(8,128)(2,1)}, u32[]{:S(2)}, u32[]{:S(2)}) async-start(bf16[8,3136,128]{2,1,0:T(8,128)(2,1)} %conv_pack.5), calls=%async_computation.2 | async-start | bytes 12845056 | tf_op jit(solution)/shard_map/all_to_all | solution.py:361
  421.2 1.6 copy-start.3
  446.9 21.0 %collective-permute-start.5 = (bf16[3,8,5376]{2,1,0:T(8,128)(2,1)}, bf16[3,8,5376]{2,1,0:T(8,128)(2,1)S(1)}, u32[]{:S(2)}, u32[]{:S(2)}) collective-permute-start(bf16[3,8,5376]{2,1,0:T(8,128)(2,1)} %tail.7), channel_id=1, source_target_pairs={{0,1},{1,2},{2,3},{3,4},{4,5},{5,6},{6,7},{8,9},{9,10},{10,11},{11... | collective-permute-start | bytes 774152 | tf_op jit(solution)/shard_map/ppermute | solution.py:352
  467.8 0.7 copy-start.13
  480.4 8.1 %copy-start.23 = (f32[10]{0:T(128)S(1)}, f32[10]{0:T(128)}, u32[]{:S(2)}) copy-start(f32[10]{0:T(128)} %get-tuple-element.87) | copy-start | bytes 124
  480.4 8.1 %copy-start.19 = (f32[10]{0:T(128)S(1)}, f32[10]{0:T(128)}, u32[]{:S(2)}) copy-start(f32[10]{0:T(128)} %get-tuple-element.90) | copy-start | bytes 124
  480.4 8.8 %copy-start.5 = (bf16[3,8,5376]{2,1,0:T(8,128)(2,1)S(1)}, bf16[3,8,5376]{2,1,0:T(8,128)(2,1)}, u32[]{:S(2)}) copy-start(bf16[3,8,5376]{2,1,0:T(8,128)(2,1)} %tail.4) | copy-start | bytes 774148
  480.5 8.8 %copy-start.6 = (bf16[3,8,5376]{2,1,0:T(8,128)(2,1)S(1)}, bf16[3,8,5376]{2,1,0:T(8,128)(2,1)}, u32[]{:S(2)}) copy-start(bf16[3,8,5376]{2,1,0:T(8,128)(2,1)} %tail.5) | copy-start | bytes 774148
  480.5 8.8 %copy-start.7 = (bf16[3,8,5376]{2,1,0:T(8,128)(2,1)S(1)}, bf16[3,8,5376]{2,1,0:T(8,128)(2,1)}, u32[]{:S(2)}) copy-start(bf16[3,8,5376]{2,1,0:T(8,128)(2,1)} %tail.6) | copy-start | bytes 774148
  480.5 8.8 %copy-start.8 = (bf16[3,8,5376]{2,1,0:T(8,128)(2,1)S(1)}, bf16[3,8,5376]{2,1,0:T(8,128)(2,1)}, u32[]{:S(2)}) copy-start(bf16[3,8,5376]{2,1,0:T(8,128)(2,1)} %tail.7) | copy-start | bytes 774148
  480.5 76.4 %all-to-all-start.6 = ((bf16[8,3136,128]{2,1,0:T(8,128)(2,1)}), bf16[8,3136,128]{2,1,0:T(8,128)(2,1)}, u32[]{:S(2)}, u32[]{:S(2)}) async-start(bf16[8,3136,128]{2,1,0:T(8,128)(2,1)} %conv_pack.7), calls=%async_computation.6 | async-start | bytes 12845056 | tf_op jit(solution)/shard_map/all_to_all | solution.py:361
  487.9 4.1 collective-permute-start.3
  490.3 94.8 %collective-permute-start.6 = (bf16[3,32,5376]{2,1,0:T(8,128)(2,1)}, bf16[3,32,5376]{2,1,0:T(8,128)(2,1)}, u32[]{:S(2)}, u32[]{:S(2)}) collective-permute-start(bf16[3,32,5376]{2,1,0:T(8,128)(2,1)} %pad_maximum_fusion), channel_id=1, source_target_pairs={{7,1},{15,9}} | collective-permute-start | bytes 3096584 | tf_op jit(solution)/shard_map/ppermute | solution.py:324
  492.1 1.0 copy-start.10
  556.9 8.3 %copy-start.2 = (bf16[512,2560]{1,0:T(8,128)(2,1)S(1)}, bf16[512,2560]{1,0:T(8,128)(2,1)}, u32[]{:S(2)}) copy-start(bf16[512,2560]{1,0:T(8,128)(2,1)} %copy-done.1) | copy-start | bytes 7864324
  556.9 72.0 %all-to-all-start.4 = ((bf16[8,2560,128]{2,1,0:T(8,128)(2,1)}), bf16[8,2560,128]{2,1,0:T(8,128)(2,1)}, u32[]{:S(2)}, u32[]{:S(2)}) async-start(bf16[8,2560,128]{2,1,0:T(8,128)(2,1)} %get-tuple-element.40), calls=%async_computation.4 | async-start | bytes 10485760 | tf_op jit(solution)/shard_map/all_to_all | solution.py:370
  565.2 19.8 %copy-start.9 = (bf16[3,8,5376]{2,1,0:T(8,128)(2,1)S(1)}, bf16[3,8,5376]{2,1,0:T(8,128)(2,1)}, u32[]{:S(2)}) copy-start(bf16[3,8,5376]{2,1,0:T(8,128)(2,1)} %tail.7) | copy-start | bytes 774148
  565.2 21.8 %copy-start.4 = (bf16[512,2560]{1,0:T(8,128)(2,1)S(1)}, bf16[512,2560]{1,0:T(8,128)(2,1)}, u32[]{:S(2)}) copy-start(bf16[512,2560]{1,0:T(8,128)(2,1)} %copy-done.3) | copy-start | bytes 7864324
  586.7 20.2 %collective-permute-start.7 = (bf16[8,512,128]{2,1,0:T(8,128)(2,1)S(1)}, bf16[8,512,128]{2,1,0:T(8,128)(2,1)S(1)}, u32[]{:S(2)}, u32[]{:S(2)}) collective-permute-start(bf16[8,512,128]{2,1,0:T(8,128)(2,1)S(1)} %slice.141), channel_id=1, source_target_pairs={{0,1},{1,0},{2,3},{3,2},{4,5},{5,4},{6,7},{7,6},{8,9},{9,8},{10,11... | collective-permute-start | bytes 3145736 | tf_op jit(solution)/shard_map/ppermute | solution.py:368
  606.9 1.1 copy-start.11
  628.9 75.4 %all-to-all-start.7 = ((bf16[8,2560,128]{2,1,0:T(8,128)(2,1)}), bf16[8,2560,128]{2,1,0:T(8,128)(2,1)}, u32[]{:S(2)}, u32[]{:S(2)}) async-start(bf16[8,2560,128]{2,1,0:T(8,128)(2,1)} %get-tuple-element.53), calls=%async_computation.7 | async-start | bytes 10485760 | tf_op jit(solution)/shard_map/all_to_all | solution.py:370
  634.9 69.3 %collective-permute-start.8 = (bf16[3,32,5376]{2,1,0:T(8,128)(2,1)S(1)}, bf16[3,32,5376]{2,1,0:T(8,128)(2,1)S(1)}, u32[]{:S(2)}, u32[]{:S(2)}) collective-permute-start(bf16[3,32,5376]{2,1,0:T(8,128)(2,1)S(1)} %broadcast_select_fusion.2), channel_id=1, source_target_pairs={{7,5},{1,3},{15,13},{9,11}} | collective-permute-start | bytes 3096584 | tf_op jit(solution)/shard_map/ppermute | solution.py:324
  704.4 32.7 %collective-permute-start.9 = (bf16[3,32,5376]{2,1,0:T(8,128)(2,1)S(1)}, bf16[3,32,5376]{2,1,0:T(8,128)(2,1)S(1)}, u32[]{:S(2)}, u32[]{:S(2)}) collective-permute-start(bf16[3,32,5376]{2,1,0:T(8,128)(2,1)S(1)} %broadcast_select_fusion.1), channel_id=1, source_target_pairs={{1,0},{3,2},{5,4},{7,6},{9,8},{11,10},{13,12},{15,14}} | collective-permute-start | bytes 3096584 | tf_op jit(solution)/shard_map/ppermute | solution.py:324
